TPU v7x, 8 devices: a whole 2x2x1 slice. The times are simulated.
8 devices in a mesh: fsdp: 8 (over z, y, x, core).
Axes of the slice: x: 2, y: 2, z: 1, core: 2. Of those that a mesh axis runs over, the one named last changes fastest.
Arguments:
- x_resid: bfloat16 [32, 1024, 1024], P('fsdp')
- g_mlp: float32 [1024], P('fsdp')
- w_gate: bfloat16 [1024, 2816], P('fsdp')
- w_up: bfloat16 [1024, 2816], P('fsdp')
- w_down: bfloat16 [2816, 1024], P('fsdp')
- g_attn: float32 [1024], P('fsdp')
- w_dq: bfloat16 [1024, 384], P('fsdp')
- g_q: float32 [384], P('fsdp')
- w_uq: bfloat16 [384, 1536], P('fsdp')
- w_dkv: bfloat16 [1024, 320], P('fsdp')
- g_kv: float32 [256], P('fsdp')
- w_uk: bfloat16 [256, 1024], P('fsdp')
- w_uv: bfloat16 [256, 1024], P('fsdp')
- w_out: bfloat16 [1024, 1024], P('fsdp')
- g_moe: float32 [1024], P('fsdp')
- w_router: float32 [64, 1024], replicated
- we_gate: bfloat16 [64, 1024, 256], P('fsdp')
- we_up: bfloat16 [64, 1024, 256], P('fsdp')
- we_down: bfloat16 [64, 256, 1024], P('fsdp')
- ws_gate: bfloat16 [1024, 256], replicated
- ws_up: bfloat16 [1024, 256], replicated
- ws_down: bfloat16 [256, 1024], replicated
- expert_ids: int32 [32, 1024, 8], P('fsdp')
Outputs:
- output: bfloat16 [32, 1024, 1024], P('fsdp')
All inputs are finite; a program needn't handle non-finite values.
Results may differ from a plain program's by a relative error of at most 0.0192166.
Values are sent between devices in bfloat16 or wider.
A program may use at most 1 GiB of HBM per device.

v0:
```python
import jax
import jax.numpy as jnp
from jax import lax
from jax.sharding import PartitionSpec as P

AXIS = "fsdp"
ROPE_BASE = 10000.0
EPS = 1e-6
ROUTE_SCALE = 2.5


def rms_norm(vals, gain):
    vals = vals.astype(jnp.float32)
    scaled = vals * lax.rsqrt(jnp.mean(vals * vals, axis=-1, keepdims=True) + EPS)
    return (scaled * gain).astype(jnp.bfloat16)


def swiglu(rows, w_gate, w_up, w_down):
    gate = jnp.dot(rows, w_gate, preferred_element_type=jnp.float32)
    upper = jnp.dot(rows, w_up, preferred_element_type=jnp.float32)
    hidden = (jax.nn.silu(gate) * upper).astype(jnp.bfloat16)
    return jnp.dot(hidden, w_down, preferred_element_type=jnp.float32).astype(jnp.bfloat16)


def rotate(vals, cos_t, sin_t):
    half = vals.shape[-1] // 2
    first = vals[..., :half].astype(jnp.float32)
    second = vals[..., half:].astype(jnp.float32)
    return jnp.concatenate([first * cos_t - second * sin_t, second * cos_t + first * sin_t], axis=-1).astype(jnp.bfloat16)


def attention(normed, w_dq, g_q, w_uq, w_dkv, g_kv, w_uk, w_uv, w_out, seq_len):
    tokens = normed.shape[0]
    num_seqs = tokens // seq_len
    kv_rank = w_uk.shape[0]
    rope_dim = w_dkv.shape[1] - kv_rank
    heads = (w_uq.shape[1] - w_uk.shape[1]) // rope_dim
    nope_dim = w_uk.shape[1] // heads
    v_dim = w_uv.shape[1] // heads
    positions = jnp.arange(seq_len)
    inv_freq = 1.0 / (ROPE_BASE ** (jnp.arange(0, rope_dim, 2).astype(jnp.float32) / rope_dim))
    angles = positions.astype(jnp.float32)[:, None] * inv_freq[None, :]
    cos_t = jnp.cos(angles)
    sin_t = jnp.sin(angles)
    q_lat = jnp.dot(normed, w_dq, preferred_element_type=jnp.float32).astype(jnp.bfloat16)
    q_all = jnp.dot(rms_norm(q_lat, g_q), w_uq, preferred_element_type=jnp.float32).astype(jnp.bfloat16)
    q_all = q_all.reshape(num_seqs, seq_len, heads, nope_dim + rope_dim)
    q_nope = q_all[..., :nope_dim]
    q_rot = rotate(q_all[..., nope_dim:], cos_t[:, None, :], sin_t[:, None, :])
    kv_all = jnp.dot(normed, w_dkv, preferred_element_type=jnp.float32).astype(jnp.bfloat16)
    latent = rms_norm(kv_all[:, :kv_rank], g_kv)
    k_rot = rotate(kv_all[:, kv_rank:].reshape(num_seqs, seq_len, rope_dim), cos_t, sin_t)
    k_nope = jnp.dot(latent, w_uk, preferred_element_type=jnp.float32).astype(jnp.bfloat16).reshape(num_seqs, seq_len, heads, nope_dim)
    values = jnp.dot(latent, w_uv, preferred_element_type=jnp.float32).astype(jnp.bfloat16).reshape(num_seqs, seq_len, heads, v_dim)
    scores = jnp.einsum("bqhd,bkhd->bhqk", q_nope, k_nope, preferred_element_type=jnp.float32)
    scores = scores + jnp.einsum("crie,cle->cirl", q_rot, k_rot, preferred_element_type=jnp.float32)
    causal = positions[:, None] >= positions[None, :]
    scores = jnp.where(causal, scores * (nope_dim + rope_dim) ** -0.5, -jnp.inf)
    attn_probs = jax.nn.softmax(scores, axis=-1).astype(jnp.bfloat16)
    attended = jnp.einsum("bhqk,bkhd->bqhd", attn_probs, values, preferred_element_type=jnp.float32).astype(jnp.bfloat16)
    return jnp.dot(attended.reshape(tokens, heads * v_dim), w_out, preferred_element_type=jnp.float32).astype(jnp.bfloat16)


def route_gates(u_norm, w_router, choice_ids):
    logits = jnp.einsum("td,ed->te", u_norm.astype(jnp.float32), w_router, precision=lax.Precision.HIGHEST)
    picked = jnp.take_along_axis(jax.nn.sigmoid(logits), choice_ids, axis=1)
    return ROUTE_SCALE * picked / jnp.sum(picked, axis=1, keepdims=True)


def route_plan(choice_ids, num_experts, capacity):
    tokens, num_top = choice_ids.shape
    slots = tokens * num_top
    flat_ids = choice_ids.reshape(slots)
    order = jnp.argsort(flat_ids, stable=True)
    counts = jnp.bincount(flat_ids, length=num_experts)
    starts = jnp.cumsum(counts) - counts
    ranks = jnp.arange(capacity)
    picks = order[jnp.minimum(starts[:, None] + ranks[None, :], slots - 1)]
    valid = ranks[None, :] < counts[:, None]
    sorted_ids = flat_ids[order]
    sorted_pos = sorted_ids * capacity + jnp.arange(slots) - starts[sorted_ids]
    slot_pos = jnp.zeros((slots,), jnp.int32).at[order].set(sorted_pos.astype(jnp.int32))
    return picks // num_top, valid, slot_pos.reshape(tokens, num_top)


def assemble(shard):
    return lax.all_gather(shard, AXIS, axis=0, tiled=True)


def routed_experts(u_norm, gates, choice_ids, we_gate, we_up, we_down, num_experts, groups):
    tokens, num_top = choice_ids.shape
    width = u_norm.shape[1]
    local_experts = we_gate.shape[0]
    capacity = 2 * tokens * num_top // num_experts
    src_rows, valid, slot_pos = route_plan(choice_ids, num_experts, capacity)
    send = jnp.where(valid[:, :, None], u_norm[src_rows], jnp.zeros((), jnp.bfloat16))
    send = send.reshape(groups, local_experts, capacity, width)
    received = lax.all_to_all(send, AXIS, 0, 0, tiled=True)
    gate = jnp.einsum("secd,edi->seci", received, we_gate, preferred_element_type=jnp.float32)
    upper = jnp.einsum("secd,edi->seci", received, we_up, preferred_element_type=jnp.float32)
    hidden = (jax.nn.silu(gate) * upper).astype(jnp.bfloat16)
    expert_out = jnp.einsum("seci,eid->secd", hidden, we_down, preferred_element_type=jnp.float32).astype(jnp.bfloat16)
    back = lax.all_to_all(expert_out, AXIS, 0, 0, tiled=True).reshape(num_experts * capacity, width)
    rows = back[slot_pos]
    return jnp.sum(gates[:, :, None] * rows, axis=1)


def solution(mesh):
    groups = mesh.shape[AXIS]
    rows_spec = P(AXIS, None)
    vec_spec = P(AXIS)
    full_spec = P(None, None)
    cube_spec = P(AXIS, None, None)
    in_specs = (cube_spec, vec_spec, rows_spec, rows_spec, rows_spec, vec_spec, rows_spec, vec_spec, rows_spec, rows_spec, vec_spec, rows_spec, rows_spec, rows_spec, vec_spec, full_spec, cube_spec, cube_spec, cube_spec, full_spec, full_spec, full_spec, cube_spec)

    def local(x_resid, g_mlp, w_gate, w_up, w_down, g_attn, w_dq, g_q, w_uq, w_dkv, g_kv, w_uk, w_uv, w_out, g_moe, w_router, we_gate, we_up, we_down, ws_gate, ws_up, ws_down, expert_ids):
        num_seqs, seq_len, width = x_resid.shape
        tokens = num_seqs * seq_len
        flat_x = x_resid.reshape(tokens, width)
        mlp_out = swiglu(rms_norm(flat_x, assemble(g_mlp)), assemble(w_gate), assemble(w_up), assemble(w_down))
        h_one = (flat_x.astype(jnp.float32) + mlp_out.astype(jnp.float32)).astype(jnp.bfloat16)
        attn_out = attention(rms_norm(h_one, assemble(g_attn)), assemble(w_dq), assemble(g_q), assemble(w_uq), assemble(w_dkv), assemble(g_kv), assemble(w_uk), assemble(w_uv), assemble(w_out), seq_len)
        h_two = (h_one.astype(jnp.float32) + attn_out.astype(jnp.float32)).astype(jnp.bfloat16)
        u_norm = rms_norm(h_two, assemble(g_moe))
        choice_ids = expert_ids.reshape(tokens, expert_ids.shape[2])
        gates = route_gates(u_norm, w_router, choice_ids)
        routed = routed_experts(u_norm, gates, choice_ids, we_gate, we_up, we_down, w_router.shape[0], groups)
        shared = swiglu(u_norm, ws_gate, ws_up, ws_down)
        z_out = (h_two.astype(jnp.float32) + shared.astype(jnp.float32) + routed).astype(jnp.bfloat16)
        return z_out.reshape(num_seqs, seq_len, width)

    return jax.shard_map(local, mesh=mesh, in_specs=in_specs, out_specs=cube_spec, check_vma=False)
```

profile of v0, /device:TPU:0, one launch (start us, length us, event | category | flops | bytes accessed | tf_op | source)
XLA Modules:
  0.0 5505.1 jit_solution(2293963133742623301)
XLA Ops:
  10.8 1.5 copy.105
  12.4 1.3 iota_compare_fusion
  13.7 1.9 copy.104
  15.6 2.7 reshape.611
  18.3 226.3 %scatter_custom_fusion = s32[64]{0:T(128)S(1)} fusion(s32[32768]{0:T(1024)S(1)} %reshape.611, s32[32768]{0:T(1024)S(1)} %broadcast.558, s32[]{:T(128)} %constant.45.clone.1), kind=kCustom, calls=%fused_computation.216 | custom fusion | flops 32768 | bytes 260 | tf_op jit(solution)/shard_map/scatter-add | solution.py:75
  246.1 5.1 fusion.24
  251.3 13.5 all-gather
  264.8 10.7 all-gather.1
  275.5 13.3 all_gather.50
  288.9 13.7 all_gather.47
  302.6 12.4 all_gather.53
  315.0 12.4 all_gather.49
  327.4 11.2 all-gather.2
  338.8 11.2 sort.17
  350.0 362.9 %gather_fusion = s32[65536]{0:T(1024)S(1)} fusion(s32[32768]{0:T(1024)S(1)} %get-tuple-element.6, s32[65536]{0:T(1024)S(1)} %broadcast_clamp_fusion.1), kind=kCustom, calls=%fused_computation | custom fusion | bytes 786432 | tf_op jit(solution)/shard_map/gather | solution.py:78
  714.7 7.9 fusion.26
  723.0 22.2 all-reduce.2
  745.2 1.2 multiply_cosine_fusion
  746.4 32.0 fusion.104
  778.4 35.8 multiply_convert_fusion.clone.3.clone.4
  814.2 30.5 fusion.15
  844.7 3.5 convolution_convert_fusion.2
  848.7 5.5 fusion.43
  854.3 11.6 convolution_convert_fusion
  865.9 16.8 copy.90
  882.6 21.2 reshape.488
  903.8 4.4 fusion.93
  908.2 8.3 slice.107
  916.5 1.2 reshape.490
  917.7 1.2 fusion.94
  919.0 7.5 convert_bitcast_fusion.2
  926.4 8.9 copy.126
  935.3 5.8 convert_bitcast_fusion.3
  941.2 8.9 copy.125
  950.1 1.8 fusion.54
  952.4 43.3 fusion.57
  995.6 113.5 %fusion.99 = (f32[4,8,1024]{2,1,0:T(8,128)S(1)}, f32[4,8,1024,1024]{2,3,1,0:T(8,128)}) fusion(f32[4,1024,1024,8]{2,1,3,0:T(8,128)} %fusion.57, pred[1024,1024]{0,1:T(8,128)(4,1)S(1)} %copy-done.18, bf16[4,1024,8,128]{1,0,3,2:T(4,128)(2,1)} %slice.107, bf16[4,1024,8,128]{3,2,1,0:T(8,128)(2,1)} %bitcast.221), kind=kOutput, calls=%fused_computation.228 | convolution fusion | flops 8757707776 | bytes 286392320 | tf_op jit(solution)/shard_map/sub | solution.py:59
  1109.1 47.8 convert_bitcast_fusion.1
  1156.9 12.3 copy.99
  1169.2 15.8 fusion.19
  1185.0 3.4 copy-done.6
  1188.4 4.4 fusion.21
  1192.8 321.8 %gather_fusion.1 = bf16[65536,1024]{1,0:T(8,128)(2,1)} fusion(bf16[4096,1024]{1,0:T(8,128)(2,1)} %fusion.21, s32[65536]{0:T(1024)S(1)} %copy-done.17), kind=kCustom, calls=%fused_computation.1 | custom fusion | bytes 268697600 | tf_op jit(solution)/shard_map/gather | solution.py:96
  1514.6 87.1 %broadcast_select_fusion = bf16[8,8,1024,1024]{3,2,1,0:T(8,128)(2,1)} fusion(bf16[8,8,1024,1024]{3,2,1,0:T(8,128)(2,1)} %bitcast.14, pred[8,8,1024]{2,1,0:T(8,128)(4,1)S(1)} %copy-done.22), kind=kLoop, calls=%fused_computation.16 | loop fusion | flops 67108864 | bytes 268500992 | tf_op jit(solution)/shard_map/jit(_where)/select_n | solution.py:96
  1601.7 1474.2 %all_to_all.10 = bf16[8,8,1024,1024]{3,2,1,0:T(8,128)(2,1)} all-to-all(bf16[8,8,1024,1024]{3,2,1,0:T(8,128)(2,1)} %broadcast_select_fusion), channel_id=1, replica_groups=mesh['fsdp'=8] {'fsdp'}, dimensions={0} | all-to-all | bytes 268435456 | tf_op jit(solution)/shard_map/all_to_all | solution.py:98
  3075.9 70.1 %fusion.4 = f32[8,8,1024,256]{3,2,1,0:T(8,128)} fusion(bf16[8,8,1024,1024]{3,2,1,0:T(8,128)(2,1)} %all_to_all.10, bf16[8,1024,256]{2,1,0:T(8,128)(2,1)} %param.40), kind=kOutput, calls=%fused_computation.17 | convolution fusion | flops 34359738368 | bytes 205520896 | tf_op jit(solution)/shard_map/secd,edi->seci/dot_general | solution.py:100
  3145.9 136.3 %convert_bitcast_fusion = bf16[8,8,1024,1024]{3,2,0,1:T(8,128)(2,1)} fusion(f32[8,8,1024,256]{3,2,1,0:T(8,128)} %fusion.4, bf16[8,8,1024,1024]{3,2,1,0:T(8,128)(2,1)} %all_to_all.10, bf16[8,256,1024]{2,1,0:T(8,128)(2,1)} %param.41, bf16[8,1024,256]{2,1,0:T(8,128)(2,1)} %param.39), kind=kOutput, calls=%fused_computation.13 | convolution fusion | flops 68887248896 | bytes 343932928 | tf_op jit(solution)/shard_map/seci,eid->secd/dot_general | solution.py:102
  3282.2 87.5 %copy.109 = bf16[8,8,1024,1024]{3,2,1,0:T(8,128)(2,1)} copy(bf16[8,8,1024,1024]{3,2,0,1:T(8,128)(2,1)} %convert_bitcast_fusion) | data formatting | bytes 268435456 | tf_op jit(solution)/shard_map/convert_element_type | solution.py:102
  3369.7 12.1 all-to-all-start.1
  3382.8 180.5 %gather_fusion.2 = s32[32768]{0:T(1024)S(1)} fusion(s32[32768]{0:T(1024)S(1)} %copy-done.4, s32[32768]{0:T(1024)S(1)} %get-tuple-element.76), kind=kCustom, calls=%fused_computation.2 | custom fusion | bytes 393216 | tf_op jit(solution)/shard_map/gather | solution.py:80
  3566.2 4.8 compare_select_fusion.3
  3571.0 27.0 compare_reduce_fusion.56
  3598.1 36.9 select_subtract_fusion
  3634.9 120.1 %scatter_custom_fusion.1 = s32[32768]{0:T(1024)S(1)} fusion(s32[32768]{0:T(1024)S(1)} %get-tuple-element.77, s32[32768]{0:T(1024)S(1)} %select_subtract_fusion, s32[]{:T(128)} %constant.45.clone.1), kind=kCustom, calls=%fused_computation.204 | custom fusion | bytes 131076 | tf_op jit(solution)/shard_map/scatter | solution.py:82
  3760.8 10.3 fusion.49
  3771.1 260.6 %gather_fusion.4 = f32[32768]{0:T(1024)S(1)} fusion(f32[4096,64]{0,1:T(8,128)S(1)} %fusion.49, s32[32768]{0:T(1024)S(1)} %reshape.603), kind=kCustom, calls=%fused_computation.4 | custom fusion | bytes 524288 | tf_op jit(solution)/shard_map/jit(take_along_axis)/gather | solution.py:66
  4031.7 2.5 gather.28
  4035.3 2.2 copy.102
  4038.2 1.9 copy.103
  4040.1 7.7 fusion.105
  4047.8 777.6 %all-to-all-done.1 = bf16[8,8,1024,1024]{3,2,1,0:T(8,128)(2,1)} async-done(((bf16[8,8,1024,1024]{3,2,1,0:T(8,128)(2,1)}), bf16[8,8,1024,1024]{3,2,1,0:T(8,128)(2,1)}, u32[]{:S(2)}, u32[]{:S(2)}) %all-to-all-start.1) | async-done | bytes 134217760 | tf_op jit(solution)/shard_map/all_to_all | solution.py:103
  4825.4 599.4 %gather_fusion.3 = bf16[32768,1024]{1,0:T(8,128)(2,1)} fusion(bf16[65536,1024]{1,0:T(8,128)(2,1)} %bitcast.24, s32[32768]{0:T(1024)S(1)} %copy-done.5), kind=kCustom, calls=%fused_computation.3 | custom fusion | bytes 134348800 | tf_op jit(solution)/shard_map/gather | solution.py:104
  5424.8 54.8 fusion.1
  5479.6 18.5 fusion.23
  (146 shorter events, 20.5 us)
Async XLA Ops:
  6.5 5473.1 %copy-start = (bf16[256,1024]{1,0:T(8,128)(2,1)S(1)}, bf16[256,1024]{1,0:T(8,128)(2,1)}, u32[]{:S(2)}) copy-start(bf16[256,1024]{1,0:T(8,128)(2,1)} %param.44) | copy-start | bytes 1572868
  6.5 739.9 %all-gather.9.cloned.1.call-start = ((), (), s32[]{:S(2)}) async-start(), calls=%async_computation.2 | async-start | bytes 6488064 | tf_op jit(solution)/shard_map/all_gather | solution.py:87
  7.3 771.1 %all-gather.11.cloned.1.call-start = ((), (), s32[]{:S(2)}) async-start(), calls=%async_computation.3 | async-start | bytes 6488064 | tf_op jit(solution)/shard_map/all_gather | solution.py:87
  8.0 806.2 %all-gather.13.cloned.1.call-start = ((), (), s32[]{:S(2)}) async-start(), calls=%async_computation.4 | async-start | bytes 6488064 | tf_op jit(solution)/shard_map/all_gather | solution.py:87
  8.7 845.5 %all-gather.15.cloned.1.call-start = ((), (), s32[]{:S(2)}) async-start(), calls=%async_computation.5 | async-start | bytes 1327104 | tf_op jit(solution)/shard_map/all_gather | solution.py:87
  9.3 1159.9 %all-gather.17.cloned.1.call-start = ((), (), s32[]{:S(2)}) async-start(), calls=%async_computation.6 | async-start | bytes 2359296 | tf_op jit(solution)/shard_map/all_gather | solution.py:87
  12.3 238.9 %copy-start.29 = (f32[128]{0:T(128)S(1)}, f32[128]{0:T(128)}, u32[]{:S(2)}) copy-start(f32[128]{0:T(128)} %param.24) | copy-start | bytes 1540
  12.4 252.5 %copy-start.30 = (f32[128]{0:T(128)S(1)}, f32[128]{0:T(128)}, u32[]{:S(2)}) copy-start(f32[128]{0:T(128)} %param.28) | copy-start | bytes 1540
  12.4 263.2 %copy-start.23 = (bf16[128,384]{1,0:T(8,128)(2,1)S(1)}, bf16[128,384]{1,0:T(8,128)(2,1)}, u32[]{:S(2)}) copy-start(bf16[128,384]{1,0:T(8,128)(2,1)} %param.29) | copy-start | bytes 294916
  13.7 275.1 %copy-start.24 = (bf16[128,320]{0,1:T(8,128)(2,1)S(1)}, bf16[128,320]{0,1:T(8,128)(2,1)}, u32[]{:S(2)}) copy-start(bf16[128,320]{0,1:T(8,128)(2,1)} %param.32) | copy-start | bytes 245764
  13.7 288.9 %copy-start.25 = (bf16[32,1024]{1,0:T(8,128)(2,1)S(1)}, bf16[32,1024]{1,0:T(8,128)(2,1)}, u32[]{:S(2)}) copy-start(bf16[32,1024]{1,0:T(8,128)(2,1)} %param.34) | copy-start | bytes 196612
  13.7 301.3 %copy-start.26 = (bf16[32,1024]{1,0:T(8,128)(2,1)S(1)}, bf16[32,1024]{1,0:T(8,128)(2,1)}, u32[]{:S(2)}) copy-start(bf16[32,1024]{1,0:T(8,128)(2,1)} %param.35) | copy-start | bytes 196612
  15.6 311.7 %copy-start.31 = (f32[128]{0:T(128)S(1)}, f32[128]{0:T(128)}, u32[]{:S(2)}) copy-start(f32[128]{0:T(128)} %param.37) | copy-start | bytes 1540
  245.0 467.8 %copy-start.13 = (s32[64]{0:T(128)}, s32[64]{0:T(128)S(1)}, u32[]{:S(2)}) copy-start(s32[64]{0:T(128)S(1)} %sub.30) | copy-start | bytes 772
  246.1 466.8 %copy-start.3 = (s32[32768]{0:T(1024)}, s32[32768]{0:T(1024)S(1)}, u32[]{:S(2)}) copy-start(s32[32768]{0:T(1024)S(1)} %reshape_reshape.3) | copy-start | bytes 393220
  350.0 362.9 %copy-start.1 = (s32[32768]{0:T(1024)}, s32[32768]{0:T(1024)S(1)}, u32[]{:S(2)}) copy-start(s32[32768]{0:T(1024)S(1)} %get-tuple-element.6) | copy-start | bytes 393220
  714.7 7.9 copy-start.37
  714.7 8.1 copy-start.38
  814.2 30.5 copy-start.20
  814.2 30.5 copy-start.28
  844.7 4.0 copy-start.39
  844.7 4.0 copy-start.19
  848.2 6.0 copy-start.11
  848.7 5.6 copy-start.35
  908.2 8.3 slice-start
  908.2 10.7 copy-start.36
  926.4 8.9 copy-start.12
  926.4 8.9 copy-start.21
  941.2 8.9 copy-start.7
  941.2 8.9 copy-start.15
  941.2 8.9 copy-start.16
  952.4 43.3 copy-start.18
  1169.2 19.2 copy-start.27
  1185.0 3.4 copy-start.6
  1188.4 4.4 copy-start.17
  1192.8 321.8 %copy-start.22 = (pred[8,8,1024]{2,1,0:T(8,128)(4,1)S(1)}, pred[8,8,1024]{2,1,0:T(8,128)(4,1)}, u32[]{:S(2)}) copy-start(pred[8,8,1024]{2,1,0:T(8,128)(4,1)} %iota_compare_fusion.1) | copy-start | bytes 196612
  3369.7 12.2 copy-start.2
  3369.7 1455.7 %all-to-all-start.1 = ((bf16[8,8,1024,1024]{3,2,1,0:T(8,128)(2,1)}), bf16[8,8,1024,1024]{3,2,1,0:T(8,128)(2,1)}, u32[]{:S(2)}, u32[]{:S(2)}) async-start(bf16[8,8,1024,1024]{3,2,1,0:T(8,128)(2,1)} %copy.109), calls=%async_computation.1 | async-start | bytes 268435456 | tf_op jit(solution)/shard_map/all_to_all | solution.py:103
  3381.8 0.9 copy-start.4
  3382.8 180.5 %copy-start.14 = (s32[64]{0:T(128)S(1)}, s32[64]{0:T(128)}, u32[]{:S(2)}) copy-start(s32[64]{0:T(128)} %copy-done.13) | copy-start | bytes 772
  3563.3 195.1 %copy-start.9 = (s32[4,1024,8]{1,2,0:T(8,128)S(1)}, s32[4,1024,8]{1,2,0:T(8,128)}, u32[]{:S(2)}) copy-start(s32[4,1024,8]{1,2,0:T(8,128)} %param.45) | copy-start | bytes 393220
  3598.0 162.7 %copy-start.34 = (f32[64,1024]{1,0:T(8,128)S(1)}, f32[64,1024]{1,0:T(8,128)}, u32[]{:S(2)}) copy-start(f32[64,1024]{1,0:T(8,128)} %param.38) | copy-start | bytes 786436
  3771.1 266.4 %copy-start.10 = (s32[4,1024,8]{1,2,0:T(8,128)S(1)}, s32[4,1024,8]{1,2,0:T(8,128)}, u32[]{:S(2)}) copy-start(s32[4,1024,8]{1,2,0:T(8,128)} %param.45) | copy-start | bytes 393220
  4031.7 8.5 copy-start.32
  4040.1 785.3 %copy-start.5 = (s32[32768]{0:T(1024)S(1)}, s32[32768]{0:T(1024)}, u32[]{:S(2)}) copy-start(s32[32768]{0:T(1024)} %broadcast_clamp_fusion.2) | copy-start | bytes 393220
  4825.4 599.4 %copy-start.8 = (f32[4096,8]{1,0:T(8,128)S(1)}, f32[4096,8]{1,0:T(8,128)}, u32[]{:S(2)}) copy-start(f32[4096,8]{1,0:T(8,128)} %copy.103) | copy-start | bytes 393220
  5424.8 54.8 copy-start.33
Sparse Core Ops, SparseCore 0:
  9.1 40.1 all-gather.8
  51.2 37.3 all-gather.10
  90.4 37.3 all-gather.12
  129.4 18.0 all-gather.14
  149.2 21.9 all-gather.16
where the time goes:
time: 5520 us; the launch traced here: 5510 us
  local copies, waits for them, and re-layouts  2040 us (37%)
  blocking collectives  1580 us (29%)
  waiting for transfers between devices  781 us (14%)
  matrix products  595 us (11%)
  other arithmetic  475 us (9%)
    all_to_all x1, blocking collectives, routed_experts(): received = lax.all_to_all(send, AXIS, 0, 0, tiled=True)  1470 us
    all_to_all x1, waiting for transfers between devices, routed_experts(): lax.all_to_all(expert_out, AXIS, 0, 0, tiled=True)  778 us
    gather x1, local copies, waits for them, and re-layouts, routed_experts(): rows = back[slot_pos]  599 us
    gather x2, local copies, waits for them, and re-layouts, route_plan(): picks = order[jnp.minimum(starts[:, None] + ranks[None, :], slots - 1)]  363 us
    gather x1, local copies, waits for them, and re-layouts, routed_experts(): u_norm[src_rows]  322 us
    gather x7, local copies, waits for them, and re-layouts, route_gates(): picked = jnp.take_along_axis(jax.nn.sigmoid(logits), choice_ids, axis=1)  269 us
    scatter-add x1, other arithmetic, route_plan(): counts = jnp.bincount(flat_ids, length=num_experts)  226 us
    gather x1, local copies, waits for them, and re-layouts, route_plan(): sorted_ids = flat_ids[order]  181 us
  transfers between devices with their start and end apart: 6, of which 1 were waited for; matrix products, arithmetic and copies ran while one was open for 31% of the time, Pallas kernels for 0%

commit v1 on v0

v1 whole, which is shorter than its diff:
```python
import functools

import jax
import jax.numpy as jnp
from jax import lax
from jax.experimental import pallas as pl
from jax.experimental.pallas import tpu as pltpu
from jax.sharding import PartitionSpec as P


AXIS = "fsdp"
ROPE_BASE = 10000.0
EPS = 1e-6
ROUTE_SCALE = 2.5
TILE = 256
PITCH = TILE + 8
LANES = 128
CHUNKS = (2, 2, 2, 2)
VMEM_LIMIT = 60 * 1024 * 1024


def rms_norm(vals, gain):
    vals = vals.astype(jnp.float32)
    scaled = vals * lax.rsqrt(jnp.mean(vals * vals, axis=-1, keepdims=True) + EPS)
    return (scaled * gain).astype(jnp.bfloat16)


def mm(lhs, rhs):
    return jnp.dot(lhs, rhs, preferred_element_type=jnp.float32)


def swiglu(rows, w_gate, w_up, w_down):
    hidden = (jax.nn.silu(mm(rows, w_gate)) * mm(rows, w_up)).astype(jnp.bfloat16)
    return mm(hidden, w_down).astype(jnp.bfloat16)


def to_blocks(shard):
    rows, cols = shard.shape
    return shard.reshape(rows, cols // LANES, LANES).transpose(1, 0, 2).reshape(-1, LANES)


def from_blocks(gathered, start, rows, cols):
    groups = gathered.shape[0]
    blocks = cols // LANES
    part = gathered[:, start : start + rows * blocks].reshape(groups, blocks, rows, LANES)
    return part.transpose(0, 2, 1, 3).reshape(groups * rows, cols)


def attn_kernel(scale, block, qn_ref, qr_ref, kn_ref, kr_ref, v_ref, o_ref):
    seq = qn_ref.shape[0]
    keys = jnp.concatenate([kn_ref[...], kr_ref[...]], axis=1)
    vals = v_ref[...]
    for start in range(0, seq, block):
        stop = start + block
        query = jnp.concatenate([qn_ref[start:stop, :], qr_ref[start:stop, :]], axis=1)
        scores = lax.dot_general(query, keys[:stop], (((1,), (1,)), ((), ())), preferred_element_type=jnp.float32)
        row = lax.broadcasted_iota(jnp.int32, scores.shape, 0) + start
        col = lax.broadcasted_iota(jnp.int32, scores.shape, 1)
        scores = jnp.where(row >= col, scores * scale, -jnp.inf)
        expo = jnp.exp(scores - jnp.max(scores, axis=1, keepdims=True))
        probs = (expo * (1.0 / jnp.sum(expo, axis=1, keepdims=True))).astype(jnp.bfloat16)
        o_ref[start:stop, :] = mm(probs, vals[:stop]).astype(jnp.bfloat16)


def attention_core(q_nope, q_rot, k_nope, k_rot, values, seq_len, scale):
    tokens, width = q_nope.shape
    seqs, heads = tokens // seq_len, width // LANES
    spec = lambda fn: pl.BlockSpec((seq_len, LANES), fn)
    return pl.pallas_call(
        functools.partial(attn_kernel, scale, 256),
        grid=(seqs, heads),
        in_specs=[
            spec(lambda s, h: (s, h)),
            spec(lambda s, h: (s, h // 2)),
            spec(lambda s, h: (s, h)),
            spec(lambda s, h: (s, h % 2)),
            spec(lambda s, h: (s, h)),
        ],
        out_specs=spec(lambda s, h: (s, h)),
        out_shape=jax.ShapeDtypeStruct((tokens, width), jnp.bfloat16),
        cost_estimate=pl.CostEstimate(flops=4 * tokens * seq_len * width, bytes_accessed=10 * tokens * width, transcendentals=0),
        name="attention_core",
    )(q_nope, q_rot, k_nope, k_rot, values)


def swap_halves(cols, half):
    rows, width = cols.shape
    pairs = cols.reshape(rows, width // (2 * half), 2, half)
    return pairs[:, :, ::-1, :].reshape(rows, width)


def attention(normed, w_dq, g_q, w_uq, w_dkv, g_kv, w_uk, w_uv, w_out, seq_len, rope_dim):
    tokens = normed.shape[0]
    num_seqs = tokens // seq_len
    kv_rank, heads_nope = w_uk.shape
    half = rope_dim // 2
    heads = (w_uq.shape[1] - heads_nope) // rope_dim
    nope_dim = heads_nope // heads
    positions = jnp.arange(seq_len)
    inv_freq = 1.0 / (ROPE_BASE ** (jnp.arange(0, rope_dim, 2).astype(jnp.float32) / rope_dim))
    angles = positions.astype(jnp.float32)[:, None] * inv_freq[None, :]
    cos_t, sin_t = jnp.cos(angles), jnp.sin(angles)
    cos_w = jnp.concatenate([cos_t, cos_t], axis=1)
    sin_w = jnp.concatenate([-sin_t, sin_t], axis=1)

    q_lat = rms_norm(mm(normed, w_dq).astype(jnp.bfloat16), g_q)
    q_nope = mm(q_lat, w_uq[:, :heads_nope]).astype(jnp.bfloat16)
    w_pe = w_uq[:, heads_nope:]
    q_pe = mm(q_lat, w_pe).astype(jnp.bfloat16)
    q_sw = mm(q_lat, swap_halves(w_pe, half)).astype(jnp.bfloat16)

    def turn(vals, swapped):
        reps = vals.shape[1] // rope_dim
        cos_r, sin_r = jnp.tile(cos_w, (num_seqs, reps)), jnp.tile(sin_w, (num_seqs, reps))
        return (vals.astype(jnp.float32) * cos_r + swapped.astype(jnp.float32) * sin_r).astype(jnp.bfloat16)

    q_rot = turn(q_pe, q_sw)
    kv_all = mm(normed, w_dkv).astype(jnp.bfloat16)
    latent = rms_norm(kv_all[:, :kv_rank], g_kv)
    k_pe = kv_all[:, kv_rank : kv_rank + rope_dim]
    k_rot = turn(k_pe, kv_all[:, kv_rank + rope_dim :])
    blank = jnp.zeros_like(k_rot)
    k_rot = jnp.concatenate([k_rot, blank, blank, k_rot], axis=1)
    k_nope = mm(latent, w_uk).astype(jnp.bfloat16)
    values = mm(latent, w_uv).astype(jnp.bfloat16)
    attended = attention_core(q_nope, q_rot, k_nope, k_rot, values, seq_len, (nope_dim + rope_dim) ** -0.5)
    return mm(attended, w_out).astype(jnp.bfloat16)


def moe_kernel(first, last, experts, meta_ref, tab_ref, rank_ref, gate_ref, u_hbm, *refs):
    if first:
        h_hbm, s_hbm, w_hbm, *refs = refs
    else:
        a_hbm, w_hbm, *refs = refs
    o_hbm, u_vm, acc, wbuf, xbuf, obuf, st_a, st_b, wsem, sem_a, sem_b, asem = refs
    tokens, width = u_hbm.shape
    pieces = width // LANES
    inter = w_hbm.shape[2]
    tile_lo, tile_hi, rank_lo = meta_ref[0], meta_ref[1], meta_ref[2]
    blocks = tokens // TILE

    def w_copy(expert):
        slot = lax.rem(expert, 2)
        return pltpu.make_async_copy(w_hbm.at[expert], wbuf.at[slot], wsem.at[slot])

    w_copy(0).start()
    if not first:
        acc_in = pltpu.make_async_copy(a_hbm, acc.at[pl.ds(0, tokens * pieces), :], asem)
        acc_in.start()

    def spread(dst, base, block):
        for j in range(pieces):
            dst[pl.ds(base * pieces + j, TILE, stride=pieces), :] = block[:, j * LANES : (j + 1) * LANES]

    def load_rows(src, stage, sem, step):
        return pltpu.make_async_copy(src.at[pl.ds(step * TILE, TILE), :], stage.at[lax.rem(step, 2)], sem.at[lax.rem(step, 2)])

    load_rows(u_hbm, st_a, sem_a, 0).start()

    @pl.loop(0, blocks)
    def _(step):
        @pl.when(step + 1 < blocks)
        def _():
            load_rows(u_hbm, st_a, sem_a, step + 1).start()

        load_rows(u_hbm, st_a, sem_a, step).wait()
        spread(u_vm, step * TILE, st_a[lax.rem(step, 2)].astype(jnp.float32))

    u_vm[pl.ds(tokens * pieces, 8), :] = jnp.zeros((8, LANES), jnp.float32)
    if first:
        load_rows(h_hbm, st_a, sem_a, 0).start()
        load_rows(s_hbm, st_b, sem_b, 0).start()

        @pl.loop(0, blocks)
        def _(step):
            @pl.when(step + 1 < blocks)
            def _():
                load_rows(h_hbm, st_a, sem_a, step + 1).start()
                load_rows(s_hbm, st_b, sem_b, step + 1).start()

            load_rows(h_hbm, st_a, sem_a, step).wait()
            load_rows(s_hbm, st_b, sem_b, step).wait()
            slot = lax.rem(step, 2)
            spread(acc, step * TILE, st_a[slot].astype(jnp.float32) + st_b[slot].astype(jnp.float32))
    else:
        acc_in.wait()
    acc[pl.ds(tokens * pieces, 8), :] = jnp.zeros((8, LANES), jnp.float32)

    def row_of(slot):
        return pl.ds(pl.multiple_of((slot >> 3) << 3, 8), 8)

    def tile_step(tile, current):
        expert = rank_ref[tile] - rank_lo

        @pl.loop(current + 1, expert + 1)
        def _(e):
            w_copy(e).wait()

            @pl.when(e + 1 < experts)
            def _():
                w_copy(e + 1).start()

        base = tile * TILE

        @pl.loop(0, TILE // 16)
        def _(group):
            for r in range(16):
                slot = tab_ref[base + group * 16 + r]
                xbuf[pl.ds(group * 16 + r, pieces, stride=PITCH), :] = u_vm[row_of(slot), :]

        rows = jnp.concatenate([xbuf[j * PITCH : j * PITCH + TILE, :].astype(jnp.bfloat16) for j in range(pieces)], axis=1)
        weights = wbuf.at[lax.rem(expert, 2)]
        gate = mm(rows, weights[0:width, :])
        upper = mm(rows, weights[width : 2 * width, :])
        hidden = (jax.nn.silu(gate) * upper).astype(jnp.bfloat16)
        for b in range(width // inter):
            out = mm(hidden, weights[2 * width + b * inter : 2 * width + (b + 1) * inter, :])
            out = out.astype(jnp.bfloat16).astype(jnp.float32)
            for j in range(inter // LANES):
                piece = b * (inter // LANES) + j
                obuf[piece * PITCH : piece * PITCH + TILE, :] = out[:, j * LANES : (j + 1) * LANES]

        @pl.loop(0, TILE // 8)
        def _(group):
            slots = [tab_ref[base + group * 8 + r] for r in range(8)]
            gates = [gate_ref[jnp.minimum(s, tokens * pieces - 1)] for s in slots]
            sums = [
                acc[row_of(s), :] + g * obuf[pl.ds(group * 8 + r, pieces, stride=PITCH), :]
                for r, (s, g) in enumerate(zip(slots, gates))
            ]
            for s, total in zip(slots, sums):
                acc[row_of(s), :] = total

        return expert

    final = lax.fori_loop(tile_lo, tile_hi, tile_step, jnp.int32(-1))

    @pl.loop(final + 1, experts)
    def _(e):
        w_copy(e).wait()

        @pl.when(e + 1 < experts)
        def _():
            w_copy(e + 1).start()

    if last:

        def store_rows(step):
            return pltpu.make_async_copy(st_a.at[lax.rem(step, 2)], o_hbm.at[pl.ds(step * TILE, TILE), :], sem_a.at[lax.rem(step, 2)])

        @pl.loop(0, blocks)
        def _(step):
            @pl.when(step >= 2)
            def _():
                store_rows(step - 2).wait()

            parts = [acc[pl.ds(step * TILE * pieces + j, TILE, stride=pieces), :].astype(jnp.bfloat16) for j in range(pieces)]
            st_a[lax.rem(step, 2)] = jnp.concatenate(parts, axis=1)
            store_rows(step).start()

        store_rows(blocks - 2).wait()
        store_rows(blocks - 1).wait()
    else:
        acc_out = pltpu.make_async_copy(acc.at[pl.ds(0, tokens * pieces), :], o_hbm, asem)
        acc_out.start()
        acc_out.wait()


def moe_call(first, last, meta, table, ranks, gates, u_norm, extra, weights):
    tokens, width = u_norm.shape
    pieces = width // LANES
    experts, wrows, inter = weights.shape
    smem = pl.BlockSpec(memory_space=pltpu.SMEM)
    hbm = pl.BlockSpec(memory_space=pl.ANY)
    scratch = [
        pltpu.VMEM((tokens * pieces + 8, LANES), jnp.float32),
        pltpu.VMEM((tokens * pieces + 8, LANES), jnp.float32),
        pltpu.VMEM((2, wrows, inter), jnp.bfloat16),
        pltpu.VMEM((pieces * PITCH, LANES), jnp.float32),
        pltpu.VMEM((pieces * PITCH, LANES), jnp.float32),
        pltpu.VMEM((2, TILE, width), jnp.bfloat16),
        pltpu.VMEM((2, TILE, width), jnp.bfloat16),
        pltpu.SemaphoreType.DMA((2,)),
        pltpu.SemaphoreType.DMA((2,)),
        pltpu.SemaphoreType.DMA((2,)),
        pltpu.SemaphoreType.DMA,
    ]
    out_shape = jax.ShapeDtypeStruct((tokens, width), jnp.bfloat16) if last else jax.ShapeDtypeStruct((tokens * pieces, LANES), jnp.float32)
    rows = experts * tokens // 8
    return pl.pallas_call(
        functools.partial(moe_kernel, first, last, experts),
        in_specs=[smem] * 4 + [hbm] * (2 + len(extra)),
        out_specs=hbm,
        out_shape=out_shape,
        scratch_shapes=scratch,
        compiler_params=pltpu.CompilerParams(vmem_limit_bytes=VMEM_LIMIT),
        cost_estimate=pl.CostEstimate(flops=2 * rows * wrows * inter, bytes_accessed=2 * experts * wrows * inter, transcendentals=0),
        name="routed_experts",
    )(meta, table, ranks, gates, u_norm, *extra, weights)


def route_plan(choice_ids, num_experts, groups):
    tokens, num_top = choice_ids.shape
    local = num_experts // groups
    device, index = choice_ids // local, choice_ids % local
    rank = jnp.zeros_like(choice_ids)
    low = 0
    for size in CHUNKS:
        rank = jnp.where((index >= low) & (index < low + size), low * groups + device * size + index - low, rank)
        low += size
    hits = rank[:, :, None] == jnp.arange(num_experts)[None, None, :]
    counts = jnp.sum(hits.astype(jnp.int32), axis=(0, 1))
    slots = jnp.arange(tokens)[:, None] * num_top + jnp.arange(num_top)[None, :]
    keys = (rank * 65536 + slots).reshape(-1)
    spare = jnp.arange(TILE)[None, :] < ((-counts) % TILE)[:, None]
    dummy = tokens * num_top
    fill = jnp.where(spare, jnp.arange(num_experts)[:, None] * 65536 + dummy, num_experts * 65536 + dummy)
    ordered = jnp.sort(jnp.concatenate([keys, fill.reshape(-1)]), stable=False)
    tiles = (counts + TILE - 1) // TILE
    ends = jnp.cumsum(tiles)
    metas = []
    low = 0
    for size in CHUNKS:
        begin = ends[low * groups - 1] if low else jnp.int32(0)
        low += size
        metas.append(jnp.stack([begin, ends[low * groups - 1], jnp.int32((low - size) * groups), jnp.int32(0)]).astype(jnp.int32))
    return ordered & 65535, ordered[::TILE] // 65536, metas


def solution(mesh):
    groups = mesh.shape[AXIS]
    rows_spec = P(AXIS, None)
    vec_spec = P(AXIS)
    full_spec = P(None, None)
    cube_spec = P(AXIS, None, None)
    in_specs = (cube_spec, vec_spec, rows_spec, rows_spec, rows_spec, vec_spec, rows_spec, vec_spec, rows_spec, rows_spec, vec_spec, rows_spec, rows_spec, rows_spec, vec_spec, full_spec, cube_spec, cube_spec, cube_spec, full_spec, full_spec, full_spec, cube_spec)

    def gather(shard):
        return lax.all_gather(shard, AXIS, axis=0, tiled=True)

    def local(x_resid, g_mlp, w_gate, w_up, w_down, g_attn, w_dq, g_q, w_uq, w_dkv, g_kv, w_uk, w_uv, w_out, g_moe, w_router, we_gate, we_up, we_down, ws_gate, ws_up, ws_down, expert_ids):
        num_seqs, seq_len, width = x_resid.shape
        tokens = num_seqs * seq_len
        num_experts = w_router.shape[0]
        inter = we_gate.shape[2]
        flat_x = x_resid.reshape(tokens, width)
        choice_ids = expert_ids.reshape(tokens, expert_ids.shape[2])

        gains = [g_mlp, g_attn, g_q, g_kv, g_moe]
        sizes = [g.shape[0] for g in gains]
        packed = lax.all_gather(jnp.concatenate(gains), AXIS, axis=0, tiled=False)
        offs = [sum(sizes[:i]) for i in range(len(sizes))]
        g_mlp, g_attn, g_q, g_kv, g_moe = [packed[:, o : o + s].reshape(-1) for o, s in zip(offs, sizes)]

        inner = w_gate.shape[1]
        gate_up = gather(jnp.concatenate([w_gate, w_up], axis=1))
        down = gather(w_down)
        kv_rank = w_uk.shape[0] * groups
        rope_dim = w_dkv.shape[1] - kv_rank
        heads = (w_uq.shape[1] - w_uk.shape[1]) // rope_dim
        nope_dim = w_uk.shape[1] // heads
        per_head = w_uq.reshape(w_uq.shape[0], heads, nope_dim + rope_dim)
        uq_local = jnp.concatenate([per_head[:, :, :nope_dim].reshape(-1, heads * nope_dim), per_head[:, :, nope_dim:].reshape(-1, heads * rope_dim)], axis=1)
        dkv_local = jnp.concatenate([w_dkv, swap_halves(w_dkv[:, kv_rank:], rope_dim // 2)], axis=1)
        shards = [w_dq, dkv_local, uq_local, w_uk, w_uv, w_out]
        blocks = [to_blocks(s) for s in shards]
        attn_w = gather(jnp.concatenate(blocks, axis=0)[None])
        starts = [sum(b.shape[0] for b in blocks[:i]) for i in range(len(blocks))]
        w_dq, w_dkv, w_uq, w_uk, w_uv, w_out = [from_blocks(attn_w, st, s.shape[0], s.shape[1]) for st, s in zip(starts, shards)]

        down_blocks = we_down.reshape(we_down.shape[0], inter, width // inter, inter).transpose(0, 2, 1, 3).reshape(we_down.shape[0], width, inter)
        pack = jnp.concatenate([we_gate, we_up, down_blocks], axis=1)
        expert_w = []
        low = 0
        for size in CHUNKS:
            expert_w.append(gather(pack[low : low + size]))
            low += size

        table, ranks, metas = route_plan(choice_ids, num_experts, groups)

        normed = rms_norm(flat_x, g_mlp)
        hidden = (jax.nn.silu(mm(normed, gate_up[:, :inner])) * mm(normed, gate_up[:, inner:])).astype(jnp.bfloat16)
        mlp_out = mm(hidden, down).astype(jnp.bfloat16)
        h_one = (flat_x.astype(jnp.float32) + mlp_out.astype(jnp.float32)).astype(jnp.bfloat16)
        attn_out = attention(rms_norm(h_one, g_attn), w_dq, g_q, w_uq, w_dkv, g_kv, w_uk, w_uv, w_out, seq_len, rope_dim)
        h_two = (h_one.astype(jnp.float32) + attn_out.astype(jnp.float32)).astype(jnp.bfloat16)
        u_norm = rms_norm(h_two, g_moe)
        logits = jnp.einsum("td,ed->te", u_norm.astype(jnp.float32), w_router, precision=lax.Precision.HIGHEST)
        scores = jax.nn.sigmoid(logits)
        hits = choice_ids[:, :, None] == jnp.arange(num_experts)[None, None, :]
        picked = jnp.sum(jnp.where(hits, scores[:, None, :], 0.0), axis=2)
        gates = (ROUTE_SCALE * picked / jnp.sum(picked, axis=1, keepdims=True)).reshape(-1)
        shared = swiglu(u_norm, ws_gate, ws_up, ws_down)

        total = None
        for i, weights in enumerate(expert_w):
            extra = (h_two, shared) if i == 0 else (total,)
            total = moe_call(i == 0, i == len(expert_w) - 1, metas[i], table, ranks, gates, u_norm, extra, weights)
        return total.reshape(num_seqs, seq_len, width)

    return jax.shard_map(local, mesh=mesh, in_specs=in_specs, out_specs=cube_spec, check_vma=False)
```

time: 5520 us -> 929 us (0.17)
  local copies, waits for them, and re-layouts: 2040 us -> 102 us
  blocking collectives: 1580 us -> 26.7 us
  waiting for transfers between devices: 781 us -> 2.27 us
  Pallas kernels: 0 us -> 532 us
  matrix products: 595 us -> 182 us
  other arithmetic: 475 us -> 62.7 us
    gather x16 -> x0, local copies, waits for them, and re-layouts: 1740 us -> none  [the longest x1 599 us: routed_experts(): rows = back[slot_pos]]
    all_to_all x1 -> x0, blocking collectives: 1470 us -> none  [routed_experts(): received = lax.all_to_all(send, AXIS, 0, 0, tiled=True)]
    all_to_all x1 -> x0, waiting for transfers between devices: 778 us -> none  [routed_experts(): lax.all_to_all(expert_out, AXIS, 0, 0, tiled=True)]
    pallas_call x0 -> x5, Pallas kernels: none -> 532 us  [the longest x4 455 us: moe_call(): pl.pallas_call(functools.partial(moe_kernel, first, last, experts), in_sp...]
    dot_general x16 -> x14, matrix products: 482 us -> 182 us  [the longest x13 175 us: mm(): return jnp.dot(lhs, rhs, preferred_element_type=jnp.float32)]
    scatter-add x1 -> x0, other arithmetic: 226 us -> none  [route_plan(): counts = jnp.bincount(flat_ids, length=num_experts)]
    scatter x1 -> x0, local copies, waits for them, and re-layouts: 120 us -> none  [route_plan(): jnp.zeros((slots,), jnp.int32).at[order].set(sorted_pos.astype(jnp.int32))]
    convert_element_type x3 -> x0, local copies, waits for them, and re-layouts: 117 us -> none  [the longest x1 87.5 us: routed_experts(): jnp.einsum('seci,eid->secd', hidden, we_down, preferred_element_type=jnp....]
  transfers between devices with their start and end apart: 6 -> 7, of which waited for: 1 -> 0; matrix products, arithmetic and copies ran while one was open for 31% -> 36% of each run, Pallas kernels for 0% -> 46%
where the time goes in v1:
time: 929 us; the launch traced here: 922 us
  Pallas kernels  532 us (57%)
  matrix products  182 us (20%)
  local copies, waits for them, and re-layouts  102 us (11%)
  other arithmetic  62.7 us (7%)
  blocking collectives  26.7 us (3%)
  between operations  14.6 us (2%)
    pallas_call x4, Pallas kernels, moe_call(): pl.pallas_call(functools.partial(moe_kernel, first, last, experts), in_sp...  455 us
    dot_general x13, matrix products, mm(): return jnp.dot(lhs, rhs, preferred_element_type=jnp.float32)  175 us
    pallas_call x1, Pallas kernels, attention_core(): pl.pallas_call(functools.partial(attn_kernel, scale, 256), grid=(seqs, he...  76.9 us
    unnamed x86, local copies, waits for them, and re-layouts  33.4 us
    unnamed x1, blocking collectives  26.7 us
  transfers between devices with their start and end apart: 7, of which 0 were waited for; matrix products, arithmetic and copies ran while one was open for 36% of the time, Pallas kernels for 46%

profile of v1, /device:TPU:0, one launch (start us, length us, event | category | flops | bytes accessed | tf_op | source)
XLA Modules:
  0.0 922.3 jit_solution(14425373819529847710)
XLA Ops:
  6.5 1.2 reshape.371
  8.1 1.0 copy.106
  12.8 1.1 copy.112
  15.2 2.6 pad_maximum_fusion.2
  18.6 2.9 copy.174
  22.1 1.7 copy-done.4
  23.8 16.2 %pad_maximum_fusion = bf16[8,3072,256]{2,1,0:T(8,128)(2,1)S(1)} fusion(bf16[8,1024,256]{2,1,0:T(8,128)(2,1)S(1)} %bitcast.176, bf16[8,1024,256]{2,1,0:T(8,128)(2,1)S(1)} %copy-done.3, bf16[8,1024,256]{2,1,0:T(8,128)(2,1)S(1)} %copy-done.4), kind=kLoop, calls=%fused_computation.20 | loop fusion | flops 37748736 | bytes 25165824 | tf_op jit(solution)/shard_map/concatenate | solution.py:372
  40.0 4.7 fusion.57
  48.5 5.1 fusion.7
  53.8 2.9 iota_add_fusion
  56.8 2.6 add.278
  59.4 1.0 reshape.364
  61.7 26.7 %all-reduce = f32[3712]{0:T(1024)S(1)} all-reduce(f32[3712]{0:T(1024)S(1)} %dynamic-update-slice), channel_id=2, replica_groups=mesh['fsdp'=8] {'fsdp'}, use_global_device_ids=true, to_apply=%add | all-reduce | flops 3712 | bytes 29696
  89.2 1.0 copy.122
  90.2 2.1 tile.16
  92.3 11.5 %copy.140 = f32[64,8,4,1024]{3,1,2,0:T(8,128)} copy(f32[64,8,4,1024]{3,2,1,0:T(4,128)S(1)} %bitcast.172) | data formatting | bytes 16777216
  103.8 9.3 %copy.116 = f32[4096,512]{1,0:T(8,128)} copy(f32[4096,512]{0,1:T(8,128)} %bitcast.173) | data formatting | bytes 16777216 | tf_op jit(solution)/shard_map/tile | solution.py:114
  113.2 1.0 copy.123
  114.2 2.1 tile.18
  116.3 11.5 %copy.141 = f32[64,8,4,1024]{3,1,2,0:T(8,128)} copy(f32[64,8,4,1024]{3,2,1,0:T(4,128)S(1)} %bitcast.174) | data formatting | bytes 16777216
  127.8 9.3 %copy.118 = f32[4096,512]{1,0:T(8,128)} copy(f32[4096,512]{0,1:T(8,128)} %bitcast.175) | data formatting | bytes 16777216 | tf_op jit(solution)/shard_map/tile | solution.py:114
  137.7 9.2 sort.8
  148.6 1.3 pad_add_fusion.4.meta_ref
  149.9 1.8 pad_add_fusion.1.meta_ref
  151.7 1.9 pad_add_fusion.2.meta_ref
  153.5 1.8 pad_add_fusion.3.meta_ref
  156.6 8.2 fusion.9
  165.6 2.6 slice.149
  168.2 2.1 slice.159
  170.3 2.5 fusion.59
  172.8 2.6 copy.114
  175.4 1.6 copy.115
  177.3 1.0 copy-done.9
  179.1 1.9 copy.117
  181.1 1.8 rev.7
  182.9 1.3 copy.119
  184.1 1.3 fusion.58
  185.4 1.0 copy.124
  186.5 1.0 copy.121
  187.5 2.8 copy.125
  190.2 32.1 %fusion.17 = f32[4096,2816]{1,0:T(8,128)} fusion(bf16[4096,1024]{1,0:T(8,128)(2,1)} %fusion.9, bf16[1024,5632]{1,0:T(8,128)(2,1)} %all-gather.10.cloned.1.call-done), kind=kOutput, calls=%fused_computation.40 | convolution fusion | flops 23622320128 | bytes 60293120 | tf_op jit(solution)/shard_map/dot_general | solution.py:29
  222.3 36.4 %multiply_convert_fusion.clone.3.clone.4 = bf16[4096,2816]{1,0:T(8,128)(2,1)} fusion(f32[4096,2816]{1,0:T(8,128)} %fusion.17, bf16[4096,1024]{1,0:T(8,128)(2,1)} %fusion.9, bf16[1024,5632]{1,0:T(8,128)(2,1)} %all-gather.10.cloned.1.call-done), kind=kOutput, calls=%fused_computation.clone.clone.clone.clone.clone.clone.clone.1 | convolution fusion | flops 23691526144 | bytes 83361792 | tf_op jit(solution)/shard_map/dot_general | solution.py:29
  258.7 30.1 %fusion.3 = (f32[4096]{0:T(1024)S(1)}, bf16[4096,1024]{1,0:T(8,128)(2,1)S(1)}) fusion(bf16[2816,1024]{1,0:T(8,128)(2,1)} %all-gather.12.cloned.1.call-done, bf16[4,1024,1024]{2,1,0:T(8,128)(2,1)} %param.23, bf16[4096,2816]{1,0:T(8,128)(2,1)} %multiply_convert_fusion.clone.3.clone.4), kind=kOutput, calls=%fused_computation.9 | convolution fusion | flops 23655870464 | bytes 45629440 | tf_op jit(solution)/shard_map/dot_general | solution.py:29
  288.9 5.1 convolution_convert_fusion.6
  294.7 3.9 fusion.12
  299.3 4.6 convolution_convert_fusion.1.v_ref
  303.9 4.7 convolution_convert_fusion.2.kn_ref
  308.6 2.5 convolution_convert_fusion.5
  311.2 7.4 convolution_convert_fusion.3.qn_ref
  318.6 2.0 pad_maximum_fusion.1.kr_ref
  320.6 9.5 %add_convert_fusion.qr_ref = bf16[4096,512]{1,0:T(8,128)(2,1)} fusion(f32[4096,512]{1,0:T(8,128)} %copy.118, f32[4096,512]{1,0:T(8,128)S(1)} %bitcast.171, bf16[4096,512]{1,0:T(8,128)(2,1)S(1)} %convolution_convert_fusion.5, bf16[384,512]{0,1:T(8,128)(2,1)} %bitcast.195, bf16[4096,384]{0,1:T(8,128)(2,1)} %copy-done.5, f32[384]{0:T(512)S(1)} %copy-done.20, ...), kind=kOutput, calls=%fused_computation.24 | convolution fusion | flops 1631584256 | bytes 28722688 | tf_op jit(solution)/shard_map/dot_general | solution.py:29
  330.2 76.9 %attention_core.1 = bf16[4096,1024]{1,0:T(8,128)(2,1)} custom-call(bf16[4096,1024]{1,0:T(8,128)(2,1)} %convolution_convert_fusion.3.qn_ref, bf16[4096,512]{1,0:T(8,128)(2,1)} %add_convert_fusion.qr_ref, bf16[4096,1024]{1,0:T(8,128)(2,1)} %convolution_convert_fusion.2.kn_ref, bf16[4096,256]{1,0:T(8,128)(2,1)} %pad_maximum_fusion.1.kr_ref, ...), custom_call_target="tpu_custom_call" | custom-call | flops 17179869184 | bytes 41943040 | tf_op jit(solution)/shard_map/attention_core/pallas_call | solution.py:69
  407.1 17.1 %fusion = (f32[4096]{0:T(1024)S(1)}, bf16[4096,1024]{1,0:T(8,128)(2,1)S(1)}) fusion(bf16[4096,1024]{1,0:T(8,128)(2,1)} %attention_core.1, bf16[128,8,8,128]{3,2,1,0:T(8,128)(2,1)S(1)} %bitcast.189, bf16[4096,1024]{1,0:T(8,128)(2,1)} %copy-done.31), kind=kOutput, calls=%fused_computation.6 | convolution fusion | flops 8623484928 | bytes 27279360 | tf_op jit(solution)/shard_map/dot_general | solution.py:29
  424.3 2.4 fusion.2.u_hbm
  426.7 0.9 copy-done.2
  427.7 7.7 fusion.22
  435.4 1.6 select_reduce_fusion
  437.6 1.6 div.131.gate_ref
  439.2 7.7 fusion.63
  447.0 13.4 %convolution_convert_fusion.refs_1_ = bf16[4096,1024]{1,0:T(8,128)(2,1)} fusion(bf16[256,1024]{1,0:T(8,128)(2,1)S(1)} %copy-done, bf16[4096,1024]{1,0:T(8,128)(2,1)} %copy-done.1, bf16[1024,256]{1,0:T(8,128)(2,1)S(1)} %copy-done.29, f32[4096,256]{1,0:T(8,128)} %fusion.63), kind=kOutput, calls=%fused_computation.30 | convolution fusion | flops 4305453056 | bytes 22020096 | tf_op jit(solution)/shard_map/dot_general | solution.py:29
  460.4 121.5 %routed_experts.4.refs_0_ = f32[32768,128]{1,0:T(8,128)} custom-call(s32[4]{0:T(128)} %pad_add_fusion.4.meta_ref, s32[49152]{0:T(1024)} %broadcast_and_fusion.tab_ref, s32[192]{0:T(256)} %and_select_fusion.rank_ref, f32[32768]{0:T(1024)} %div.131.gate_ref, bf16[4096,1024]{1,0:T(8,128)(2,1)} %copy-done.1, bf16[4096,1024]{1,0:T(8,128)(2,1)} %copy-done.2, ...), custom_call_target="tpu_custom_call" | custom-call | flops 12884901888 | bytes 25165824 | tf_op jit(solution)/shard_map/routed_experts/pallas_call | solution.py:290
  581.9 111.3 %routed_experts.5.refs_0_ = f32[32768,128]{1,0:T(8,128)} custom-call(s32[4]{0:T(128)} %pad_add_fusion.1.meta_ref, s32[49152]{0:T(1024)} %broadcast_and_fusion.tab_ref, s32[192]{0:T(256)} %and_select_fusion.rank_ref, f32[32768]{0:T(1024)} %div.131.gate_ref, bf16[4096,1024]{1,0:T(8,128)(2,1)} %copy-done.1, f32[32768,128]{1,0:T(8,128)} %routed_experts.4.refs_0_, ...), custom_call_target="tpu_custom_call" | custom-call | flops 12884901888 | bytes 25165824 | tf_op jit(solution)/shard_map/routed_experts/pallas_call | solution.py:290
  693.2 116.6 %routed_experts.6.refs_0_ = f32[32768,128]{1,0:T(8,128)} custom-call(s32[4]{0:T(128)} %pad_add_fusion.2.meta_ref, s32[49152]{0:T(1024)} %broadcast_and_fusion.tab_ref, s32[192]{0:T(256)} %and_select_fusion.rank_ref, f32[32768]{0:T(1024)} %div.131.gate_ref, bf16[4096,1024]{1,0:T(8,128)(2,1)} %copy-done.1, f32[32768,128]{1,0:T(8,128)} %routed_experts.5.refs_0_, ...), custom_call_target="tpu_custom_call" | custom-call | flops 12884901888 | bytes 25165824 | tf_op jit(solution)/shard_map/routed_experts/pallas_call | solution.py:290
  809.9 105.3 %routed_experts.7 = bf16[4096,1024]{1,0:T(8,128)(2,1)} custom-call(s32[4]{0:T(128)} %pad_add_fusion.3.meta_ref, s32[49152]{0:T(1024)} %broadcast_and_fusion.tab_ref, s32[192]{0:T(256)} %and_select_fusion.rank_ref, f32[32768]{0:T(1024)} %div.131.gate_ref, bf16[4096,1024]{1,0:T(8,128)(2,1)} %copy-done.1, f32[32768,128]{1,0:T(8,128)} %routed_experts.6.refs_0_, ...), custom_call_target="tpu_custom_call" | custom-call | flops 12884901888 | bytes 25165824 | tf_op jit(solution)/shard_map/routed_experts/pallas_call | solution.py:290
  (154 shorter events, 19.8 us)
Async XLA Ops:
  6.5 440.4 %copy-start = (bf16[256,1024]{1,0:T(8,128)(2,1)S(1)}, bf16[256,1024]{1,0:T(8,128)(2,1)}, u32[]{:S(2)}) copy-start(bf16[256,1024]{1,0:T(8,128)(2,1)} %param.44) | copy-start | bytes 1572868
  6.5 159.0 %all-gather.22.cloned.1.call-start = ((), (), s32[]{:S(2)}) async-start(), calls=%async_computation.6 | async-start | bytes 6635520 | tf_op jit(solution)/shard_map/all_gather | solution.py:339
  14.2 0.9 copy-start.15
  15.1 175.1 %all-gather.10.cloned.1.call-start = ((), (), s32[]{:S(2)}) async-start(), calls=%async_computation | async-start | bytes 12976128 | tf_op jit(solution)/shard_map/all_gather | solution.py:339
  17.7 241.0 %all-gather.12.cloned.1.call-start = ((), (), s32[]{:S(2)}) async-start(), calls=%async_computation.1 | async-start | bytes 6488064 | tf_op jit(solution)/shard_map/all_gather | solution.py:339
  18.5 441.9 %all-gather.14.cloned.1.call-start = ((), (), s32[]{:S(2)}) async-start(), calls=%async_computation.2 | async-start | bytes 28311552 | tf_op jit(solution)/shard_map/all_gather | solution.py:339
  18.5 3.6 copy-start.3
  18.5 5.2 copy-start.4
  44.7 2.0 copy-start.13
  44.7 537.2 %all-gather.16.cloned.1.call-start = ((), (), s32[]{:S(2)}) async-start(), calls=%async_computation.3 | async-start | bytes 28311552 | tf_op jit(solution)/shard_map/all_gather | solution.py:339
  45.3 647.9 %all-gather.18.cloned.1.call-start = ((), (), s32[]{:S(2)}) async-start(), calls=%async_computation.4 | async-start | bytes 28311552 | tf_op jit(solution)/shard_map/all_gather | solution.py:339
  45.9 764.0 %all-gather.20.cloned.1.call-start = ((), (), s32[]{:S(2)}) async-start(), calls=%async_computation.5 | async-start | bytes 28311552 | tf_op jit(solution)/shard_map/all_gather | solution.py:339
  48.5 12.9 %copy-start.22 = (f32[128]{0:T(128)S(1)}, f32[128]{0:T(128)}, u32[]{:S(2)}) copy-start(f32[128]{0:T(128)} %param.24) | copy-start | bytes 1540
  48.5 12.8 %copy-start.23 = (f32[128]{0:T(128)S(1)}, f32[128]{0:T(128)}, u32[]{:S(2)}) copy-start(f32[128]{0:T(128)} %param.28) | copy-start | bytes 1540
  48.5 12.8 %copy-start.24 = (f32[48]{0:T(128)S(1)}, f32[48]{0:T(128)}, u32[]{:S(2)}) copy-start(f32[48]{0:T(128)} %param.30) | copy-start | bytes 580
  48.5 12.8 %copy-start.25 = (f32[32]{0:T(128)S(1)}, f32[32]{0:T(128)}, u32[]{:S(2)}) copy-start(f32[32]{0:T(128)} %param.33) | copy-start | bytes 388
  48.5 12.8 %copy-start.26 = (f32[128]{0:T(128)S(1)}, f32[128]{0:T(128)}, u32[]{:S(2)}) copy-start(f32[128]{0:T(128)} %param.37) | copy-start | bytes 1540
  177.3 1.0 copy-start.9
  258.7 30.2 %copy-start.17 = (bf16[8,128,3,128]{1,0,3,2:T(8,128)(2,1)S(1)}, bf16[8,128,3,128]{1,0,3,2:T(8,128)(2,1)}, u32[]{:S(2)}) copy-start(bf16[8,128,3,128]{1,0,3,2:T(8,128)(2,1)} %copy.119) | copy-start | bytes 2359300
  258.7 30.2 %copy-start.21 = (f32[1024]{0:T(1024)S(1)}, f32[1024]{0:T(1024)}, u32[]{:S(2)}) copy-start(f32[1024]{0:T(1024)} %get-tuple-element.20) | copy-start | bytes 12292
  288.9 5.8 copy-start.31
  288.9 5.1 copy-start.11
  288.9 5.1 copy-start.12
  288.9 5.7 copy-start.16
  294.7 4.6 copy-start.6
  294.7 4.6 copy-start.18
  298.6 12.6 %copy-start.5 = (bf16[4096,384]{0,1:T(8,128)(2,1)}, bf16[4096,384]{0,1:T(8,128)(2,1)S(1)}, u32[]{:S(2)}) copy-start(bf16[4096,384]{0,1:T(8,128)(2,1)S(1)} %get-tuple-element.28) | copy-start | bytes 9437188
  299.2 4.7 copy-start.7
  303.9 4.7 copy-start.10
  303.9 4.7 copy-start.20
  308.6 12.0 %slice-start = ((s8[8388608]{0:T(1024)(128)(4,1)}), s8[4194304]{0:T(1024)(128)(4,1)S(1)}, s32[]{:S(2)}) async-start(s8[8388608]{0:T(1024)(128)(4,1)} %bitcast.170), calls=%async_computation.7 | async-start | bytes 8388608
  311.2 7.4 copy-start.27
  311.2 9.5 %slice-start.1 = ((s8[8388608]{0:T(1024)(128)(4,1)}), s8[4194304]{0:T(1024)(128)(4,1)S(1)}, s32[]{:S(2)}) async-start(s8[8388608]{0:T(1024)(128)(4,1)} %bitcast.170), calls=%async_computation.8 | async-start | bytes 8388608
  330.2 76.9 %copy-start.8 = (bf16[8,128,8,128]{3,2,1,0:T(8,128)(2,1)S(1)}, bf16[8,128,8,128]{3,2,1,0:T(8,128)(2,1)}, u32[]{:S(2)}) copy-start(bf16[8,128,8,128]{3,2,1,0:T(8,128)(2,1)} %copy.125) | copy-start | bytes 6291460
  407.1 17.2 %copy-start.19 = (f32[1024]{0:T(1024)S(1)}, f32[1024]{0:T(1024)}, u32[]{:S(2)}) copy-start(f32[1024]{0:T(1024)} %get-tuple-element.19) | copy-start | bytes 12292
  424.2 3.4 copy-start.2
  424.3 3.4 copy-start.30
  427.6 9.3 %copy-start.1 = (bf16[4096,1024]{1,0:T(8,128)(2,1)}, bf16[4096,1024]{1,0:T(8,128)(2,1)S(1)}, u32[]{:S(2)}) copy-start(bf16[4096,1024]{1,0:T(8,128)(2,1)S(1)} %fusion.2.u_hbm) | copy-start | bytes 25165828
  427.6 7.7 copy-start.14
  427.6 11.6 %copy-start.28 = (bf16[1024,256]{1,0:T(8,128)(2,1)S(1)}, bf16[1024,256]{1,0:T(8,128)(2,1)}, u32[]{:S(2)}) copy-start(bf16[1024,256]{1,0:T(8,128)(2,1)} %param.42) | copy-start | bytes 1572868
  439.2 7.8 copy-start.29
Sparse Core Ops, SparseCore 0:
  15.2 40.9 all-gather.21
  58.1 62.8 all-gather.9
  122.8 37.8 all-gather.11
  162.4 119.6 all-gather.13
  283.7 119.6 all-gather.15
  405.0 119.6 all-gather.17
  526.5 119.6 all-gather.19

commit v2 on v1

--- a/solution.py
+++ b/solution.py
@@ -13,7 +13,9 @@
 EPS = 1e-6
 ROUTE_SCALE = 2.5
 TILE = 256
-PITCH = TILE + 8
+PITCH = TILE + 4
+GROUP = 4
+ORDER = (("D", 0), ("S", 5), ("D", 1), ("S", 5), ("D", 2), ("S", 5), ("D", 3), ("S", 5), ("G", 0), ("S", 6), ("U", 0), ("S", 5), ("G", 1), ("S", 5), ("U", 1), ("S", 5), ("G", 2), ("S", 6), ("U", 2), ("S", 5), ("G", 3), ("S", 6), ("U", 3), ("S", 6), ("H", 0))
 LANES = 128
 CHUNKS = (2, 2, 2, 2)
 VMEM_LIMIT = 60 * 1024 * 1024
@@ -46,13 +48,14 @@
     return part.transpose(0, 2, 1, 3).reshape(groups * rows, cols)
 
 
-def attn_kernel(scale, block, qn_ref, qr_ref, kn_ref, kr_ref, v_ref, o_ref):
+def attn_kernel(scale, block, qn_ref, qp_ref, qs_ref, kn_ref, kr_ref, v_ref, cos_ref, sin_ref, o_ref):
     seq = qn_ref.shape[0]
     keys = jnp.concatenate([kn_ref[...], kr_ref[...]], axis=1)
     vals = v_ref[...]
     for start in range(0, seq, block):
         stop = start + block
-        query = jnp.concatenate([qn_ref[start:stop, :], qr_ref[start:stop, :]], axis=1)
+        turned = qp_ref[start:stop, :].astype(jnp.float32) * cos_ref[start:stop, :] + qs_ref[start:stop, :].astype(jnp.float32) * sin_ref[start:stop, :]
+        query = jnp.concatenate([qn_ref[start:stop, :], turned.astype(jnp.bfloat16)], axis=1)
         scores = lax.dot_general(query, keys[:stop], (((1,), (1,)), ((), ())), preferred_element_type=jnp.float32)
         row = lax.broadcasted_iota(jnp.int32, scores.shape, 0) + start
         col = lax.broadcasted_iota(jnp.int32, scores.shape, 1)
@@ -62,7 +65,7 @@
         o_ref[start:stop, :] = mm(probs, vals[:stop]).astype(jnp.bfloat16)
 
 
-def attention_core(q_nope, q_rot, k_nope, k_rot, values, seq_len, scale):
+def attention_core(q_nope, q_pe, k_nope, k_rot, values, cos_w, sin_w, seq_len, scale):
     tokens, width = q_nope.shape
     seqs, heads = tokens // seq_len, width // LANES
     spec = lambda fn: pl.BlockSpec((seq_len, LANES), fn)
@@ -72,15 +75,18 @@
         in_specs=[
             spec(lambda s, h: (s, h)),
             spec(lambda s, h: (s, h // 2)),
+            spec(lambda s, h: (s, heads // 2 + h // 2)),
             spec(lambda s, h: (s, h)),
             spec(lambda s, h: (s, h % 2)),
             spec(lambda s, h: (s, h)),
+            spec(lambda s, h: (0, 0)),
+            spec(lambda s, h: (0, 0)),
         ],
         out_specs=spec(lambda s, h: (s, h)),
         out_shape=jax.ShapeDtypeStruct((tokens, width), jnp.bfloat16),
         cost_estimate=pl.CostEstimate(flops=4 * tokens * seq_len * width, bytes_accessed=10 * tokens * width, transcendentals=0),
         name="attention_core",
-    )(q_nope, q_rot, k_nope, k_rot, values)
+    )(q_nope, q_pe, q_pe, k_nope, k_rot, values, cos_w, sin_w)
 
 
 def swap_halves(cols, half):
@@ -100,50 +106,48 @@
     inv_freq = 1.0 / (ROPE_BASE ** (jnp.arange(0, rope_dim, 2).astype(jnp.float32) / rope_dim))
     angles = positions.astype(jnp.float32)[:, None] * inv_freq[None, :]
     cos_t, sin_t = jnp.cos(angles), jnp.sin(angles)
-    cos_w = jnp.concatenate([cos_t, cos_t], axis=1)
-    sin_w = jnp.concatenate([-sin_t, sin_t], axis=1)
-
+    cos_w = jnp.concatenate([cos_t] * 4, axis=1)
+    sin_w = jnp.concatenate([-sin_t, sin_t] * 2, axis=1)
     q_lat = rms_norm(mm(normed, w_dq).astype(jnp.bfloat16), g_q)
     q_nope = mm(q_lat, w_uq[:, :heads_nope]).astype(jnp.bfloat16)
     w_pe = w_uq[:, heads_nope:]
-    q_pe = mm(q_lat, w_pe).astype(jnp.bfloat16)
-    q_sw = mm(q_lat, swap_halves(w_pe, half)).astype(jnp.bfloat16)
-
-    def turn(vals, swapped):
-        reps = vals.shape[1] // rope_dim
-        cos_r, sin_r = jnp.tile(cos_w, (num_seqs, reps)), jnp.tile(sin_w, (num_seqs, reps))
-        return (vals.astype(jnp.float32) * cos_r + swapped.astype(jnp.float32) * sin_r).astype(jnp.bfloat16)
-
-    q_rot = turn(q_pe, q_sw)
+    q_pe = mm(q_lat, jnp.concatenate([w_pe, swap_halves(w_pe, half)], axis=1)).astype(jnp.bfloat16)
+
     kv_all = mm(normed, w_dkv).astype(jnp.bfloat16)
     latent = rms_norm(kv_all[:, :kv_rank], g_kv)
-    k_pe = kv_all[:, kv_rank : kv_rank + rope_dim]
-    k_rot = turn(k_pe, kv_all[:, kv_rank + rope_dim :])
+    k_pe = kv_all[:, kv_rank:].reshape(num_seqs, seq_len, 2 * rope_dim).astype(jnp.float32)
+    k_rot = k_pe[..., :rope_dim] * cos_w[None, :, :rope_dim] + k_pe[..., rope_dim:] * sin_w[None, :, :rope_dim]
+    k_rot = k_rot.astype(jnp.bfloat16).reshape(tokens, rope_dim)
     blank = jnp.zeros_like(k_rot)
     k_rot = jnp.concatenate([k_rot, blank, blank, k_rot], axis=1)
     k_nope = mm(latent, w_uk).astype(jnp.bfloat16)
     values = mm(latent, w_uv).astype(jnp.bfloat16)
-    attended = attention_core(q_nope, q_rot, k_nope, k_rot, values, seq_len, (nope_dim + rope_dim) ** -0.5)
+    attended = attention_core(q_nope, q_pe, k_nope, k_rot, values, cos_w, sin_w, seq_len, (nope_dim + rope_dim) ** -0.5)
     return mm(attended, w_out).astype(jnp.bfloat16)
 
 
-def moe_kernel(first, last, experts, meta_ref, tab_ref, rank_ref, gate_ref, u_hbm, *refs):
+def moe_kernel(first, last, meta_ref, rank_ref, gate_ref, tab_hbm, u_hbm, *refs):
     if first:
         h_hbm, s_hbm, w_hbm, *refs = refs
     else:
         a_hbm, w_hbm, *refs = refs
-    o_hbm, u_vm, acc, wbuf, xbuf, obuf, st_a, st_b, wsem, sem_a, sem_b, asem = refs
+    o_hbm, u_vm, acc, wbuf, *refs = refs
+    x_bufs, o_bufs, h_bufs, t_next, t_prev, s_prev = (refs[i : i + 2] for i in range(0, 12, 2))
+    st_a, st_b, wsem, sem_a, sem_b, asem, lsem = refs[12:]
     tokens, width = u_hbm.shape
     pieces = width // LANES
     inter = w_hbm.shape[2]
-    tile_lo, tile_hi, rank_lo = meta_ref[0], meta_ref[1], meta_ref[2]
+    tile_lo, tile_hi, experts = meta_ref[0], meta_ref[1], meta_ref[2]
     blocks = tokens // TILE
 
-    def w_copy(expert):
-        slot = lax.rem(expert, 2)
-        return pltpu.make_async_copy(w_hbm.at[expert], wbuf.at[slot], wsem.at[slot])
-
-    w_copy(0).start()
+    def w_copy(order):
+        slot = lax.rem(order, 3)
+        return pltpu.make_async_copy(w_hbm.at[meta_ref[3 + order]], wbuf.at[slot], wsem.at[slot])
+
+    @pl.when(experts > 0)
+    def _():
+        w_copy(0).start()
+
     if not first:
         acc_in = pltpu.make_async_copy(a_hbm, acc.at[pl.ds(0, tokens * pieces), :], asem)
         acc_in.start()
@@ -186,62 +190,103 @@
         acc_in.wait()
     acc[pl.ds(tokens * pieces, 8), :] = jnp.zeros((8, LANES), jnp.float32)
 
-    def row_of(slot):
-        return pl.ds(pl.multiple_of((slot >> 3) << 3, 8), 8)
-
-    def tile_step(tile, current):
-        expert = rank_ref[tile] - rank_lo
-
-        @pl.loop(current + 1, expert + 1)
-        def _(e):
-            w_copy(e).wait()
-
-            @pl.when(e + 1 < experts)
+    idle = tab_hbm.shape[0] - 1
+    count = tile_hi - tile_lo
+
+    def tile_at(step):
+        return jnp.where((step >= 0) & (step < count), tile_lo + step, idle)
+
+    def list_copies(step, parity):
+        ahead, behind = tab_hbm.at[tile_at(step + 1)], tab_hbm.at[tile_at(step - 2)]
+        return (
+            pltpu.make_async_copy(ahead.at[0], t_next[parity], lsem.at[parity, 0]),
+            pltpu.make_async_copy(behind.at[0], t_prev[parity], lsem.at[parity, 1]),
+            pltpu.make_async_copy(behind.at[1], s_prev[parity], lsem.at[parity, 2]),
+        )
+
+    def row_at(offset):
+        return pl.ds(pl.multiple_of(offset, pieces), pieces)
+
+    def order_at(step):
+        return jnp.where((step >= 0) & (step < count), rank_ref[tile_at(step)], 0)
+
+    depth = 2 * LANES
+    half = TILE // 2
+
+    def column(buf, j):
+        parts = [buf[pl.ds(j * PITCH + odd, half, stride=2), :] for odd in (0, 1)]
+        return jnp.concatenate(parts, axis=0)
+
+    def half_step(step, parity):
+        x_now, x_next = x_bufs[parity], x_bufs[1 - parity]
+        h_now, h_prev = h_bufs[parity], h_bufs[1 - parity]
+        o_now, o_prev = o_bufs[parity], o_bufs[1 - parity]
+        ahead, behind, slots = t_next[parity], t_prev[parity], s_prev[parity]
+        for copy in list_copies(step + 1, 1 - parity):
+            copy.start()
+        mine, before = order_at(step), order_at(step - 1)
+
+        @pl.when((step < count) & ((step == 0) | (mine != before)))
+        def _():
+            w_copy(mine).wait()
+
+            @pl.when(mine + 1 < experts)
             def _():
-                w_copy(e + 1).start()
-
-        base = tile * TILE
-
-        @pl.loop(0, TILE // 16)
-        def _(group):
-            for r in range(16):
-                slot = tab_ref[base + group * 16 + r]
-                xbuf[pl.ds(group * 16 + r, pieces, stride=PITCH), :] = u_vm[row_of(slot), :]
-
-        rows = jnp.concatenate([xbuf[j * PITCH : j * PITCH + TILE, :].astype(jnp.bfloat16) for j in range(pieces)], axis=1)
-        weights = wbuf.at[lax.rem(expert, 2)]
-        gate = mm(rows, weights[0:width, :])
-        upper = mm(rows, weights[width : 2 * width, :])
-        hidden = (jax.nn.silu(gate) * upper).astype(jnp.bfloat16)
-        for b in range(width // inter):
-            out = mm(hidden, weights[2 * width + b * inter : 2 * width + (b + 1) * inter, :])
-            out = out.astype(jnp.bfloat16).astype(jnp.float32)
-            for j in range(inter // LANES):
-                piece = b * (inter // LANES) + j
-                obuf[piece * PITCH : piece * PITCH + TILE, :] = out[:, j * LANES : (j + 1) * LANES]
-
-        @pl.loop(0, TILE // 8)
-        def _(group):
-            slots = [tab_ref[base + group * 8 + r] for r in range(8)]
-            gates = [gate_ref[jnp.minimum(s, tokens * pieces - 1)] for s in slots]
-            sums = [
-                acc[row_of(s), :] + g * obuf[pl.ds(group * 8 + r, pieces, stride=PITCH), :]
-                for r, (s, g) in enumerate(zip(slots, gates))
-            ]
-            for s, total in zip(slots, sums):
-                acc[row_of(s), :] = total
-
-        return expert
-
-    final = lax.fori_loop(tile_lo, tile_hi, tile_step, jnp.int32(-1))
-
-    @pl.loop(final + 1, experts)
-    def _(e):
-        w_copy(e).wait()
-
-        @pl.when(e + 1 < experts)
-        def _():
-            w_copy(e + 1).start()
+                w_copy(mine + 1).start()
+
+        for copy in list_copies(step, parity):
+            copy.wait()
+
+        def side_work(low, high):
+            for start in range(low, high, GROUP):
+                for r in range(start, start + GROUP):
+                    x_next[pl.ds(r, pieces, stride=PITCH), :] = u_vm[row_at(ahead[r]), :]
+                spots = [behind[r] for r in range(start, start + GROUP)]
+                sums = [acc[row_at(t), :] + gate_ref[slots[start + r]] * o_prev[pl.ds(start + r, pieces, stride=PITCH), :] for r, t in enumerate(spots)]
+                for r, total in enumerate(sums):
+                    acc[row_at(behind[start + r]), :] = total
+
+        w_now, w_prev = wbuf.at[lax.rem(mine, 3)], wbuf.at[lax.rem(before, 3)]
+        sums, parts = {}, {}
+        done = 0
+        for kind, k in ORDER:
+            if kind in "GU":
+                if k not in parts:
+                    parts[k] = jnp.concatenate([column(x_now, 2 * k).astype(jnp.bfloat16), column(x_now, 2 * k + 1).astype(jnp.bfloat16)], axis=1)
+                low = (0 if kind == "G" else width) + k * depth
+                term = mm(parts[k], w_now[low : low + depth, :])
+                sums[kind] = term if k == 0 else sums[kind] + term
+            elif kind == "D":
+                low = 2 * width + k * inter
+                out = mm(h_prev[...], w_prev[low : low + inter, :]).astype(jnp.bfloat16).astype(jnp.float32)
+                for j in range(inter // LANES):
+                    for odd in (0, 1):
+                        at = pl.ds((k * (inter // LANES) + j) * PITCH + odd, half, stride=2)
+                        o_now[at, :] = out[odd * half : (odd + 1) * half, j * LANES : (j + 1) * LANES]
+            elif kind == "S":
+                side_work(done, done + k * GROUP)
+                done += k * GROUP
+            else:
+                h_now[...] = (jax.nn.silu(sums["G"]) * sums["U"]).astype(jnp.bfloat16)
+        side_work(done, TILE)
+
+    first_list = pltpu.make_async_copy(tab_hbm.at[tile_at(0), 0], t_next[1], lsem.at[1, 0])
+    first_list.start()
+    for copy in list_copies(0, 0):
+        copy.start()
+    first_list.wait()
+    for r in range(TILE):
+        x_bufs[0][pl.ds(r, pieces, stride=PITCH), :] = u_vm[row_at(t_next[1][r]), :]
+
+    pairs = (count + 3) // 2
+
+    @pl.loop(0, pairs)
+    def _(i):
+        half_step(2 * i, 0)
+        half_step(2 * i + 1, 1)
+
+    for copy in list_copies(2 * pairs, 0):
+        copy.wait()
 
     if last:
 
@@ -275,28 +320,30 @@
     scratch = [
         pltpu.VMEM((tokens * pieces + 8, LANES), jnp.float32),
         pltpu.VMEM((tokens * pieces + 8, LANES), jnp.float32),
-        pltpu.VMEM((2, wrows, inter), jnp.bfloat16),
-        pltpu.VMEM((pieces * PITCH, LANES), jnp.float32),
-        pltpu.VMEM((pieces * PITCH, LANES), jnp.float32),
+        pltpu.VMEM((3, wrows, inter), jnp.bfloat16),
+        *[pltpu.VMEM((pieces * PITCH, LANES), jnp.float32)] * 4,
+        *[pltpu.VMEM((TILE, inter), jnp.bfloat16)] * 2,
+        *[pltpu.SMEM((TILE,), jnp.int32)] * 6,
         pltpu.VMEM((2, TILE, width), jnp.bfloat16),
         pltpu.VMEM((2, TILE, width), jnp.bfloat16),
-        pltpu.SemaphoreType.DMA((2,)),
+        pltpu.SemaphoreType.DMA((3,)),
         pltpu.SemaphoreType.DMA((2,)),
         pltpu.SemaphoreType.DMA((2,)),
         pltpu.SemaphoreType.DMA,
+        pltpu.SemaphoreType.DMA((2, 3)),
     ]
     out_shape = jax.ShapeDtypeStruct((tokens, width), jnp.bfloat16) if last else jax.ShapeDtypeStruct((tokens * pieces, LANES), jnp.float32)
     rows = experts * tokens // 8
     return pl.pallas_call(
-        functools.partial(moe_kernel, first, last, experts),
-        in_specs=[smem] * 4 + [hbm] * (2 + len(extra)),
+        functools.partial(moe_kernel, first, last),
+        in_specs=[smem] * 3 + [hbm] * (3 + len(extra)),
         out_specs=hbm,
         out_shape=out_shape,
         scratch_shapes=scratch,
         compiler_params=pltpu.CompilerParams(vmem_limit_bytes=VMEM_LIMIT),
         cost_estimate=pl.CostEstimate(flops=2 * rows * wrows * inter, bytes_accessed=2 * experts * wrows * inter, transcendentals=0),
         name="routed_experts",
-    )(meta, table, ranks, gates, u_norm, *extra, weights)
+    )(meta, ranks, gates, table, u_norm, *extra, weights)
 
 
 def route_plan(choice_ids, num_experts, groups):
@@ -317,14 +364,24 @@
     fill = jnp.where(spare, jnp.arange(num_experts)[:, None] * 65536 + dummy, num_experts * 65536 + dummy)
     ordered = jnp.sort(jnp.concatenate([keys, fill.reshape(-1)]), stable=False)
     tiles = (counts + TILE - 1) // TILE
-    ends = jnp.cumsum(tiles)
-    metas = []
-    low = 0
-    for size in CHUNKS:
-        begin = ends[low * groups - 1] if low else jnp.int32(0)
-        low += size
-        metas.append(jnp.stack([begin, ends[low * groups - 1], jnp.int32((low - size) * groups), jnp.int32(0)]).astype(jnp.int32))
-    return ordered & 65535, ordered[::TILE] // 65536, metas
+    spans = [(sum(CHUNKS[:i]) * groups, sum(CHUNKS[: i + 1]) * groups) for i in range(len(CHUNKS))]
+    experts = jnp.arange(num_experts)
+    chunk = sum((experts >= low).astype(jnp.int32) for low, _ in spans) - 1
+    used = counts > 0
+    ahead = (chunk[:, None] == chunk[None, :]) & (experts[None, :] < experts[:, None])
+    order = jnp.sum(jnp.where(ahead & used[None, :], 1, 0), axis=1)
+    start = jnp.array([low for low, _ in spans])
+    stop = jnp.array([high for _, high in spans])
+    member = (experts[None, :] >= start[:, None]) & (experts[None, :] < stop[:, None]) & used[None, :]
+    names = jnp.sum(jnp.where(member[:, None, :] & (order[None, None, :] == experts[None, :, None]), experts[None, None, :] - start[:, None, None], 0), axis=2)
+    first = jnp.sum(jnp.where(experts[None, :] < start[:, None], tiles[None, :], 0), axis=1)
+    final = jnp.sum(jnp.where(experts[None, :] < stop[:, None], tiles[None, :], 0), axis=1)
+    metas = jnp.concatenate([jnp.stack([first, final, jnp.sum(member.astype(jnp.int32), axis=1)], axis=1), names], axis=1).astype(jnp.int32)
+    ranks = ordered[::TILE] // 65536
+    orders = jnp.sum(jnp.where(ranks[:, None] == experts[None, :], order[None, :], 0), axis=1)
+    low = ordered & 65535
+    table = jnp.stack([(low & ~7).reshape(-1, TILE), low.reshape(-1, TILE)], axis=1)
+    return table, orders, metas
 
 
 def solution(mesh):
@@ -390,6 +447,7 @@
         hits = choice_ids[:, :, None] == jnp.arange(num_experts)[None, None, :]
         picked = jnp.sum(jnp.where(hits, scores[:, None, :], 0.0), axis=2)
         gates = (ROUTE_SCALE * picked / jnp.sum(picked, axis=1, keepdims=True)).reshape(-1)
+        gates = jnp.concatenate([gates, jnp.zeros((8,), jnp.float32)])
         shared = swiglu(u_norm, ws_gate, ws_up, ws_down)
 
         total = None

time: 929 us -> 734 us (0.79)
  the two profiles are of different devices: /device:TPU:0 before, /device:TPU:5 now
where the time goes in v2:
time: 734 us; the launch traced here: 725 us
  Pallas kernels  357 us (49%)
  matrix products  180 us (25%)
  other arithmetic  61.8 us (8%)
  local copies, waits for them, and re-layouts  55.3 us (8%)
  waiting for transfers between devices  32.5 us (4%)
  blocking collectives  23.4 us (3%)
  between operations  14.5 us (2%)
    pallas_call x4, Pallas kernels, moe_call(): pl.pallas_call(functools.partial(moe_kernel, first, last), in_specs=[smem...  279 us
    dot_general x12, matrix products, mm(): return jnp.dot(lhs, rhs, preferred_element_type=jnp.float32)  173 us
    pallas_call x1, Pallas kernels, attention_core(): pl.pallas_call(functools.partial(attn_kernel, scale, 256), grid=(seqs, he...  77.9 us
    all_gather x7, waiting for transfers between devices, gather(): return lax.all_gather(shard, AXIS, axis=0, tiled=True)  30 us
    unnamed x1, blocking collectives  23.4 us
    concatenate x1, other arithmetic, local(): pack = jnp.concatenate([we_gate, we_up, down_blocks], axis=1)  16.4 us
  transfers between devices with their start and end apart: 7, of which 1 were waited for; matrix products, arithmetic and copies ran while one was open for 39% of the time, Pallas kernels for 39%

profile of v2, /device:TPU:5, one launch (start us, length us, event | category | flops | bytes accessed | tf_op | source)
XLA Modules:
  0.0 724.9 jit_solution(4394166213593830482)
XLA Ops:
  6.5 1.2 reshape.454
  8.1 1.0 copy.105
  9.3 0.7 slice.103
  10.0 0.9 pad_maximum_fusion.8
  11.0 0.9 copy.130
  11.9 0.9 copy.131
  12.8 1.1 copy.111
  14.2 0.9 copy-done.15
  15.2 2.5 pad_maximum_fusion.2
  18.5 3.0 copy.166
  21.5 0.9 copy-done.3
  22.4 1.6 copy-done.4
  24.0 16.4 %pad_maximum_fusion = bf16[8,3072,256]{2,1,0:T(8,128)(2,1)S(1)} fusion(bf16[8,1024,256]{2,1,0:T(8,128)(2,1)S(1)} %bitcast.153, bf16[8,1024,256]{2,1,0:T(8,128)(2,1)S(1)} %copy-done.3, bf16[8,1024,256]{2,1,0:T(8,128)(2,1)S(1)} %copy-done.4), kind=kLoop, calls=%fused_computation.20 | loop fusion | flops 37748736 | bytes 25165824 | tf_op jit(solution)/shard_map/concatenate | solution.py:429
  40.4 4.7 fusion.68
  47.3 0.9 convert_reduce_fusion
  48.9 5.2 fusion.7
  55.0 3.1 iota_add_fusion
  58.1 2.6 add.313
  60.7 1.0 reshape.447
  62.0 9.2 %sort.8 = s32[49152]{0:T(1024)S(1)} sort(s32[49152]{0:T(1024)S(1)} %pad_add_fusion.1), dimensions={0}, to_apply=%region_6.7 | sort | flops 786432 | bytes 393216 | tf_op jit(solution)/shard_map/jit(sort)/sort | solution.py:365
  72.3 23.4 %all-reduce.1 = f32[3712]{0:T(1024)S(1)} all-reduce(f32[3712]{0:T(1024)S(1)} %dynamic-update-slice), channel_id=2, replica_groups=mesh['fsdp'=8] {'fsdp'}, use_global_device_ids=true, to_apply=%add.1 | all-reduce | flops 3712 | bytes 29696
  98.4 1.1 pad_add_fusion.tab_hbm
  99.5 1.9 multiply_cosine_fusion
  101.4 1.3 pad_maximum_fusion.3
  102.7 1.9 pad_maximum_fusion.5
  105.8 7.9 %fusion.9 = bf16[4096,1024]{1,0:T(8,128)(2,1)} fusion(bf16[4,1024,1024]{2,1,0:T(8,128)(2,1)} %param.25, f32[1024]{0:T(1024)S(1)} %get-tuple-element.23, f32[4096]{0:T(1024)S(1)} %bitcast.200), kind=kLoop, calls=%fused_computation.18 | loop fusion | flops 16777216 | bytes 16797696 | tf_op jit(solution)/shard_map/convert_element_type | solution.py:27
  113.7 2.4 slice.136
  116.0 1.7 slice.147
  117.8 2.4 fusion.70
  120.2 2.4 copy.113
  122.6 1.6 copy.114
  124.6 1.0 copy-done.10
  125.6 0.8 slice.138
  126.4 1.9 copy.115
  128.4 1.8 rev.7
  130.2 1.9 copy.116
  132.1 1.3 copy.117
  133.4 1.3 fusion.69
  134.7 1.0 copy.119
  135.7 1.0 copy.118
  136.7 2.8 copy.120
  139.5 34.2 %fusion.17 = f32[4096,2816]{1,0:T(8,128)} fusion(bf16[4096,1024]{1,0:T(8,128)(2,1)} %fusion.9, bf16[1024,5632]{1,0:T(8,128)(2,1)} %all-gather.10.cloned.1.call-done), kind=kOutput, calls=%fused_computation.38 | convolution fusion | flops 23622320128 | bytes 60293120 | tf_op jit(solution)/shard_map/dot_general | solution.py:31
  173.6 36.4 %multiply_convert_fusion.clone.3.clone.4 = bf16[4096,2816]{1,0:T(8,128)(2,1)} fusion(f32[4096,2816]{1,0:T(8,128)} %fusion.17, bf16[4096,1024]{1,0:T(8,128)(2,1)} %fusion.9, bf16[1024,5632]{1,0:T(8,128)(2,1)} %all-gather.10.cloned.1.call-done), kind=kOutput, calls=%fused_computation.clone.clone.clone.clone.clone.clone.clone.1 | convolution fusion | flops 23691526144 | bytes 83361792 | tf_op jit(solution)/shard_map/dot_general | solution.py:31
  210.1 33.2 %fusion.3 = (f32[4096]{0:T(1024)S(1)}, bf16[4096,1024]{1,0:T(8,128)(2,1)S(1)}) fusion(bf16[2816,1024]{1,0:T(8,128)(2,1)} %all-gather.12.cloned.1.call-done, bf16[4,1024,1024]{2,1,0:T(8,128)(2,1)} %param.25, bf16[4096,2816]{1,0:T(8,128)(2,1)} %multiply_convert_fusion.clone.3.clone.4), kind=kOutput, calls=%fused_computation.9 | convolution fusion | flops 23655870464 | bytes 45629440 | tf_op jit(solution)/shard_map/dot_general | solution.py:31
  243.4 5.0 convolution_convert_fusion.5
  248.6 4.0 fusion.12
  254.0 4.6 convolution_convert_fusion.1.v_ref
  258.6 4.8 convolution_convert_fusion.2.kn_ref
  263.4 7.0 convolution_convert_fusion.4.qn_ref
  270.4 2.0 pad_maximum_fusion.1.kr_ref
  272.5 7.0 convolution_convert_fusion.3.qp_ref.qs_ref
  279.4 77.9 %attention_core.1 = bf16[4096,1024]{1,0:T(8,128)(2,1)} custom-call(bf16[4096,1024]{1,0:T(8,128)(2,1)} %convolution_convert_fusion.4.qn_ref, bf16[4096,1024]{1,0:T(8,128)(2,1)} %convolution_convert_fusion.3.qp_ref.qs_ref, bf16[4096,1024]{1,0:T(8,128)(2,1)} %convolution_convert_fusion.3.qp_ref.qs_ref, bf16[4096,1024]{1,0:T(8,128)(2,1)} %convolution_convert_fusion.2.kn_ref, ...), custom_call_target="tpu_custom_call" | custom-call | flops 17179869184 | bytes 41943040 | tf_op jit(solution)/shard_map/attention_core/pallas_call | solution.py:72
  357.3 15.1 %fusion = (f32[4096]{0:T(1024)S(1)}, bf16[4096,1024]{1,0:T(8,128)(2,1)S(1)}) fusion(bf16[4096,1024]{1,0:T(8,128)(2,1)} %attention_core.1, bf16[128,8,8,128]{3,2,1,0:T(8,128)(2,1)S(1)} %bitcast.168, bf16[4096,1024]{1,0:T(8,128)(2,1)} %copy-done.33), kind=kOutput, calls=%fused_computation.6 | convolution fusion | flops 8623484928 | bytes 27279360 | tf_op jit(solution)/shard_map/dot_general | solution.py:31
  372.5 2.6 fusion.2.u_hbm
  375.8 7.7 %fusion.22 = f32[4096,64]{0,1:T(8,128)S(1)} fusion(bf16[4096,1024]{1,0:T(8,128)(2,1)S(1)} %fusion.2.u_hbm, f32[64,1024]{1,0:T(8,128)S(1)} %copy-done.32), kind=kOutput, calls=%fused_computation.49 | convolution fusion | flops 3222011904 | bytes 9699328 | tf_op jit(solution)/shard_map/td,ed->te/dot_general | solution.py:445
  383.5 1.6 select_reduce_fusion
  385.8 1.0 div.147
  387.5 7.8 %fusion.73 = f32[4096,256]{1,0:T(8,128)} fusion(bf16[4096,1024]{1,0:T(8,128)(2,1)} %copy-done.1, bf16[1024,256]{1,0:T(8,128)(2,1)S(1)} %copy-done.30), kind=kOutput, calls=%fused_computation.181 | convolution fusion | flops 2147483648 | bytes 13107200 | tf_op jit(solution)/shard_map/dot_general | solution.py:31
  395.3 13.6 %convolution_convert_fusion.refs_1_ = bf16[4096,1024]{1,0:T(8,128)(2,1)} fusion(bf16[256,1024]{1,0:T(8,128)(2,1)S(1)} %copy-done, bf16[4096,1024]{1,0:T(8,128)(2,1)} %copy-done.1, bf16[1024,256]{1,0:T(8,128)(2,1)S(1)} %copy-done.31, f32[4096,256]{1,0:T(8,128)} %fusion.73), kind=kOutput, calls=%fused_computation.29 | convolution fusion | flops 4305453056 | bytes 22020096 | tf_op jit(solution)/shard_map/dot_general | solution.py:31
  408.9 73.7 %routed_experts.4.refs_0_ = f32[32768,128]{1,0:T(8,128)} custom-call(s32[67]{0:T(128)} %get-tuple-element.27.meta_ref, s32[192]{0:T(256)} %select_reduce_fusion.3.rank_ref, f32[32776]{0:T(1024)} %concatenate.62.gate_ref, s32[192,2,256]{2,1,0:T(2,128)} %pad_add_fusion.tab_hbm, bf16[4096,1024]{1,0:T(8,128)(2,1)} %copy-done.1, bf16[4096,1024]{1,0:T(8,128)(2,1)} %copy-done.2, ...), custom_call_target="tpu_custom_call" | custom-call | flops 12884901888 | bytes 25165824 | tf_op jit(solution)/shard_map/routed_experts/pallas_call | solution.py:337
  482.6 65.1 %routed_experts.5.refs_0_ = f32[32768,128]{1,0:T(8,128)} custom-call(s32[67]{0:T(128)} %get-tuple-element.28.meta_ref, s32[192]{0:T(256)} %select_reduce_fusion.3.rank_ref, f32[32776]{0:T(1024)} %concatenate.62.gate_ref, s32[192,2,256]{2,1,0:T(2,128)} %pad_add_fusion.tab_hbm, bf16[4096,1024]{1,0:T(8,128)(2,1)} %copy-done.1, ...), custom_call_target="tpu_custom_call" | custom-call | flops 12884901888 | bytes 25165824 | tf_op jit(solution)/shard_map/routed_experts/pallas_call | solution.py:337
  547.8 66.2 %routed_experts.6.refs_0_ = f32[32768,128]{1,0:T(8,128)} custom-call(s32[67]{0:T(128)} %get-tuple-element.29.meta_ref, s32[192]{0:T(256)} %select_reduce_fusion.3.rank_ref, f32[32776]{0:T(1024)} %concatenate.62.gate_ref, s32[192,2,256]{2,1,0:T(2,128)} %pad_add_fusion.tab_hbm, bf16[4096,1024]{1,0:T(8,128)(2,1)} %copy-done.1, ...), custom_call_target="tpu_custom_call" | custom-call | flops 12884901888 | bytes 25165824 | tf_op jit(solution)/shard_map/routed_experts/pallas_call | solution.py:337
  613.9 29.9 %all-gather.20.cloned.1.call-done.refs_1_ = bf16[16,3072,256]{2,1,0:T(8,128)(2,1)} async-done(((bf16[2,3072,256]{2,1,0:T(8,128)(2,1)}), bf16[16,3072,256]{2,1,0:T(8,128)(2,1)}) %all-gather.20.cloned.1.call-update) | async-done | bytes 25165840 | tf_op jit(solution)/shard_map/all_gather | solution.py:396
  643.9 73.9 %routed_experts.7 = bf16[4096,1024]{1,0:T(8,128)(2,1)} custom-call(s32[67]{0:T(128)} %get-tuple-element.30.meta_ref, s32[192]{0:T(256)} %select_reduce_fusion.3.rank_ref, f32[32776]{0:T(1024)} %concatenate.62.gate_ref, s32[192,2,256]{2,1,0:T(2,128)} %pad_add_fusion.tab_hbm, bf16[4096,1024]{1,0:T(8,128)(2,1)} %copy-done.1, ...), custom_call_target="tpu_custom_call" | custom-call | flops 12884901888 | bytes 25165824 | tf_op jit(solution)/shard_map/routed_experts/pallas_call | solution.py:337
  (154 shorter events, 14.5 us)
Async XLA Ops:
  6.5 388.7 %copy-start = (bf16[256,1024]{1,0:T(8,128)(2,1)S(1)}, bf16[256,1024]{1,0:T(8,128)(2,1)}, u32[]{:S(2)}) copy-start(bf16[256,1024]{1,0:T(8,128)(2,1)} %param.46) | copy-start | bytes 1572868
  6.5 107.1 %all-gather.22.cloned.1.call-start = ((), (), s32[]{:S(2)}) async-start(), calls=%async_computation.6 | async-start | bytes 6635520 | tf_op jit(solution)/shard_map/all_gather | solution.py:396
  14.2 0.9 copy-start.15
  15.1 124.3 %all-gather.10.cloned.1.call-start = ((), (), s32[]{:S(2)}) async-start(), calls=%async_computation | async-start | bytes 12976128 | tf_op jit(solution)/shard_map/all_gather | solution.py:396
  17.7 192.4 %all-gather.12.cloned.1.call-start = ((), (), s32[]{:S(2)}) async-start(), calls=%async_computation.1 | async-start | bytes 6488064 | tf_op jit(solution)/shard_map/all_gather | solution.py:396
  18.4 390.4 %all-gather.14.cloned.1.call-start = ((), (), s32[]{:S(2)}) async-start(), calls=%async_computation.2 | async-start | bytes 28311552 | tf_op jit(solution)/shard_map/all_gather | solution.py:396
  18.5 3.9 copy-start.3
  18.5 5.5 copy-start.4
  45.1 2.0 copy-start.13
  45.1 437.5 %all-gather.16.cloned.1.call-start = ((), (), s32[]{:S(2)}) async-start(), calls=%async_computation.3 | async-start | bytes 28311552 | tf_op jit(solution)/shard_map/all_gather | solution.py:396
  45.7 502.1 %all-gather.18.cloned.1.call-start = ((), (), s32[]{:S(2)}) async-start(), calls=%async_computation.4 | async-start | bytes 28311552 | tf_op jit(solution)/shard_map/all_gather | solution.py:396
  45.7 8.6 %copy-start.28 = (s32[4]{0:T(128)S(1)}, s32[4]{0:T(128)}, u32[]{:S(2)}) copy-start(s32[4]{0:T(128)} %constant.150.clone) | copy-start | bytes 52
  46.3 597.6 %all-gather.20.cloned.1.call-start = ((), (), s32[]{:S(2)}) async-start(), calls=%async_computation.5 | async-start | bytes 28311552 | tf_op jit(solution)/shard_map/all_gather | solution.py:396
  48.9 22.8 %copy-start.23 = (f32[128]{0:T(128)S(1)}, f32[128]{0:T(128)}, u32[]{:S(2)}) copy-start(f32[128]{0:T(128)} %param.26) | copy-start | bytes 1540
  48.9 22.8 %copy-start.24 = (f32[128]{0:T(128)S(1)}, f32[128]{0:T(128)}, u32[]{:S(2)}) copy-start(f32[128]{0:T(128)} %param.30) | copy-start | bytes 1540
  48.9 22.8 %copy-start.25 = (f32[48]{0:T(128)S(1)}, f32[48]{0:T(128)}, u32[]{:S(2)}) copy-start(f32[48]{0:T(128)} %param.32) | copy-start | bytes 580
  48.9 22.8 %copy-start.26 = (f32[32]{0:T(128)S(1)}, f32[32]{0:T(128)}, u32[]{:S(2)}) copy-start(f32[32]{0:T(128)} %param.35) | copy-start | bytes 388
  48.9 22.8 %copy-start.27 = (f32[128]{0:T(128)S(1)}, f32[128]{0:T(128)}, u32[]{:S(2)}) copy-start(f32[128]{0:T(128)} %param.39) | copy-start | bytes 1540
  124.6 1.1 copy-start.10
  210.1 33.3 %copy-start.17 = (bf16[8,128,3,128]{1,0,3,2:T(8,128)(2,1)S(1)}, bf16[8,128,3,128]{1,0,3,2:T(8,128)(2,1)}, u32[]{:S(2)}) copy-start(bf16[8,128,3,128]{1,0,3,2:T(8,128)(2,1)} %copy.117) | copy-start | bytes 2359300
  210.1 33.3 %copy-start.21 = (f32[1024]{0:T(1024)S(1)}, f32[1024]{0:T(1024)}, u32[]{:S(2)}) copy-start(f32[1024]{0:T(1024)} %get-tuple-element.22) | copy-start | bytes 12292
  243.3 5.3 copy-start.33
  243.4 5.2 copy-start.16
  248.6 4.7 copy-start.5
  248.6 4.7 copy-start.6
  252.6 1.3 copy-start.7
  252.6 1.3 copy-start.19
  254.0 4.6 copy-start.8
  258.6 4.8 copy-start.11
  258.6 4.8 copy-start.22
  263.4 7.0 copy-start.29
  263.4 9.0 %copy-start.12 = (bf16[384,512]{1,0:T(8,128)(2,1)S(1)}, bf16[384,512]{1,0:T(8,128)(2,1)}, u32[]{:S(2)}) copy-start(bf16[384,512]{1,0:T(8,128)(2,1)} %slice.138) | copy-start | bytes 1179652
  263.4 9.0 %copy-start.18 = (bf16[384,512]{1,0:T(8,128)(2,1)S(1)}, bf16[384,512]{1,0:T(8,128)(2,1)}, u32[]{:S(2)}) copy-start(bf16[384,512]{1,0:T(8,128)(2,1)} %copy.116) | copy-start | bytes 1179652
  279.4 77.9 %copy-start.9 = (bf16[8,128,8,128]{3,2,1,0:T(8,128)(2,1)S(1)}, bf16[8,128,8,128]{3,2,1,0:T(8,128)(2,1)}, u32[]{:S(2)}) copy-start(bf16[8,128,8,128]{3,2,1,0:T(8,128)(2,1)} %copy.120) | copy-start | bytes 6291460
  357.3 15.1 %copy-start.20 = (f32[1024]{0:T(1024)S(1)}, f32[1024]{0:T(1024)}, u32[]{:S(2)}) copy-start(f32[1024]{0:T(1024)} %get-tuple-element.21) | copy-start | bytes 12292
  372.4 3.4 copy-start.2
  372.4 3.4 copy-start.32
  375.8 9.3 %copy-start.1 = (bf16[4096,1024]{1,0:T(8,128)(2,1)}, bf16[4096,1024]{1,0:T(8,128)(2,1)S(1)}, u32[]{:S(2)}) copy-start(bf16[4096,1024]{1,0:T(8,128)(2,1)S(1)} %fusion.2.u_hbm) | copy-start | bytes 25165828
  375.8 7.7 %copy-start.14 = (s32[4,1024,8]{1,2,0:T(8,128)S(1)}, s32[4,1024,8]{1,2,0:T(8,128)}, u32[]{:S(2)}) copy-start(s32[4,1024,8]{1,2,0:T(8,128)} %param.47) | copy-start | bytes 393220
  375.8 11.7 %copy-start.30 = (bf16[1024,256]{1,0:T(8,128)(2,1)S(1)}, bf16[1024,256]{1,0:T(8,128)(2,1)}, u32[]{:S(2)}) copy-start(bf16[1024,256]{1,0:T(8,128)(2,1)} %param.44) | copy-start | bytes 1572868
  387.5 7.8 %copy-start.31 = (bf16[1024,256]{1,0:T(8,128)(2,1)S(1)}, bf16[1024,256]{1,0:T(8,128)(2,1)}, u32[]{:S(2)}) copy-start(bf16[1024,256]{1,0:T(8,128)(2,1)} %param.45) | copy-start | bytes 1572868
Sparse Core Ops, SparseCore 0:
  15.2 39.3 all-gather.21
  56.4 62.9 all-gather.9
  121.3 37.8 all-gather.11
  160.9 118.7 all-gather.13
  281.3 119.7 all-gather.15
  402.8 119.5 all-gather.17
  524.2 119.6 all-gather.19

commit v3 on v2

--- a/solution.py
+++ b/solution.py
@@ -15,9 +15,11 @@
 TILE = 256
 PITCH = TILE + 4
 GROUP = 4
+RING = 4
 ORDER = (("D", 0), ("S", 5), ("D", 1), ("S", 5), ("D", 2), ("S", 5), ("D", 3), ("S", 5), ("G", 0), ("S", 6), ("U", 0), ("S", 5), ("G", 1), ("S", 5), ("U", 1), ("S", 5), ("G", 2), ("S", 6), ("U", 2), ("S", 5), ("G", 3), ("S", 6), ("U", 3), ("S", 6), ("H", 0))
 LANES = 128
-CHUNKS = (2, 2, 2, 2)
+PLAN = (("S", 3), ("P", 2), ("S", 2), ("S", 1))
+CHUNKS = tuple(size for _, size in PLAN)
 VMEM_LIMIT = 60 * 1024 * 1024
 
 
@@ -126,27 +128,42 @@
     return mm(attended, w_out).astype(jnp.bfloat16)
 
 
-def moe_kernel(first, last, meta_ref, rank_ref, gate_ref, tab_hbm, u_hbm, *refs):
+def moe_kernel(first, last, arrays, meta_ref, rank_ref, gate_ref, tab_hbm, u_hbm, *refs):
     if first:
-        h_hbm, s_hbm, w_hbm, *refs = refs
+        h_hbm, s_hbm, *refs = refs
     else:
-        a_hbm, w_hbm, *refs = refs
+        a_hbm, *refs = refs
+    w_hbms, refs = refs[:arrays], refs[arrays:]
     o_hbm, u_vm, acc, wbuf, *refs = refs
-    x_bufs, o_bufs, h_bufs, t_next, t_prev, s_prev = (refs[i : i + 2] for i in range(0, 12, 2))
-    st_a, st_b, wsem, sem_a, sem_b, asem, lsem = refs[12:]
+    x_bufs, o_bufs, h_bufs = refs[0:2], refs[2:4], refs[4:6]
+    t_next, t_prev, s_prev = refs[6 : 6 + RING], refs[6 + RING : 6 + 2 * RING], refs[6 + 2 * RING : 6 + 3 * RING]
+    st_a, st_b, wsem, sem_a, sem_b, asem, lsem = refs[6 + 3 * RING :]
     tokens, width = u_hbm.shape
     pieces = width // LANES
-    inter = w_hbm.shape[2]
+    inter = w_hbms[0].shape[2]
     tile_lo, tile_hi, experts = meta_ref[0], meta_ref[1], meta_ref[2]
     blocks = tokens // TILE
 
-    def w_copy(order):
+    def w_start(order):
         slot = lax.rem(order, 3)
-        return pltpu.make_async_copy(w_hbm.at[meta_ref[3 + order]], wbuf.at[slot], wsem.at[slot])
+        name = meta_ref[3 + order]
+        low = 0
+        for w_hbm in w_hbms:
+            size = w_hbm.shape[0]
+
+            @pl.when((name >= low) & (name < low + size))
+            def _(w_hbm=w_hbm, low=low):
+                pltpu.make_async_copy(w_hbm.at[name - low], wbuf.at[slot], wsem.at[slot]).start()
+
+            low += size
+
+    def w_wait(order):
+        slot = lax.rem(order, 3)
+        pltpu.make_async_copy(w_hbms[0].at[0], wbuf.at[slot], wsem.at[slot]).wait()
 
     @pl.when(experts > 0)
     def _():
-        w_copy(0).start()
+        w_start(0)
 
     if not first:
         acc_in = pltpu.make_async_copy(a_hbm, acc.at[pl.ds(0, tokens * pieces), :], asem)
@@ -196,12 +213,12 @@
     def tile_at(step):
         return jnp.where((step >= 0) & (step < count), tile_lo + step, idle)
 
-    def list_copies(step, parity):
+    def list_copies(step, turn):
         ahead, behind = tab_hbm.at[tile_at(step + 1)], tab_hbm.at[tile_at(step - 2)]
         return (
-            pltpu.make_async_copy(ahead.at[0], t_next[parity], lsem.at[parity, 0]),
-            pltpu.make_async_copy(behind.at[0], t_prev[parity], lsem.at[parity, 1]),
-            pltpu.make_async_copy(behind.at[1], s_prev[parity], lsem.at[parity, 2]),
+            pltpu.make_async_copy(ahead.at[0], t_next[turn], lsem.at[turn, 0]),
+            pltpu.make_async_copy(behind.at[0], t_prev[turn], lsem.at[turn, 1]),
+            pltpu.make_async_copy(behind.at[1], s_prev[turn], lsem.at[turn, 2]),
         )
 
     def row_at(offset):
@@ -217,24 +234,25 @@
         parts = [buf[pl.ds(j * PITCH + odd, half, stride=2), :] for odd in (0, 1)]
         return jnp.concatenate(parts, axis=0)
 
-    def half_step(step, parity):
+    def tile_step(step, turn):
+        parity = turn % 2
         x_now, x_next = x_bufs[parity], x_bufs[1 - parity]
         h_now, h_prev = h_bufs[parity], h_bufs[1 - parity]
         o_now, o_prev = o_bufs[parity], o_bufs[1 - parity]
-        ahead, behind, slots = t_next[parity], t_prev[parity], s_prev[parity]
-        for copy in list_copies(step + 1, 1 - parity):
+        ahead, behind, slots = t_next[turn], t_prev[turn], s_prev[turn]
+        for copy in list_copies(step + RING - 1, (turn + RING - 1) % RING):
             copy.start()
         mine, before = order_at(step), order_at(step - 1)
 
         @pl.when((step < count) & ((step == 0) | (mine != before)))
         def _():
-            w_copy(mine).wait()
+            w_wait(mine)
 
             @pl.when(mine + 1 < experts)
             def _():
-                w_copy(mine + 1).start()
-
-        for copy in list_copies(step, parity):
+                w_start(mine + 1)
+
+        for copy in list_copies(step, turn):
             copy.wait()
 
         def side_work(low, high):
@@ -270,23 +288,25 @@
                 h_now[...] = (jax.nn.silu(sums["G"]) * sums["U"]).astype(jnp.bfloat16)
         side_work(done, TILE)
 
-    first_list = pltpu.make_async_copy(tab_hbm.at[tile_at(0), 0], t_next[1], lsem.at[1, 0])
+    first_list = pltpu.make_async_copy(tab_hbm.at[tile_at(0), 0], t_next[RING - 1], lsem.at[RING - 1, 0])
     first_list.start()
-    for copy in list_copies(0, 0):
-        copy.start()
+    for ahead in range(RING - 1):
+        for copy in list_copies(ahead, ahead):
+            copy.start()
     first_list.wait()
     for r in range(TILE):
-        x_bufs[0][pl.ds(r, pieces, stride=PITCH), :] = u_vm[row_at(t_next[1][r]), :]
-
-    pairs = (count + 3) // 2
-
-    @pl.loop(0, pairs)
+        x_bufs[0][pl.ds(r, pieces, stride=PITCH), :] = u_vm[row_at(t_next[RING - 1][r]), :]
+
+    rounds = (count + RING + 1) // RING
+
+    @pl.loop(0, rounds)
     def _(i):
-        half_step(2 * i, 0)
-        half_step(2 * i + 1, 1)
-
-    for copy in list_copies(2 * pairs, 0):
-        copy.wait()
+        for turn in range(RING):
+            tile_step(RING * i + turn, turn)
+
+    for ahead in range(RING - 1):
+        for copy in list_copies(RING * rounds + ahead, ahead):
+            copy.wait()
 
     if last:
 
@@ -314,7 +334,8 @@
 def moe_call(first, last, meta, table, ranks, gates, u_norm, extra, weights):
     tokens, width = u_norm.shape
     pieces = width // LANES
-    experts, wrows, inter = weights.shape
+    experts = sum(w.shape[0] for w in weights)
+    wrows, inter = weights[0].shape[1:]
     smem = pl.BlockSpec(memory_space=pltpu.SMEM)
     hbm = pl.BlockSpec(memory_space=pl.ANY)
     scratch = [
@@ -323,37 +344,38 @@
         pltpu.VMEM((3, wrows, inter), jnp.bfloat16),
         *[pltpu.VMEM((pieces * PITCH, LANES), jnp.float32)] * 4,
         *[pltpu.VMEM((TILE, inter), jnp.bfloat16)] * 2,
-        *[pltpu.SMEM((TILE,), jnp.int32)] * 6,
+        *[pltpu.SMEM((TILE,), jnp.int32)] * (3 * RING),
         pltpu.VMEM((2, TILE, width), jnp.bfloat16),
         pltpu.VMEM((2, TILE, width), jnp.bfloat16),
         pltpu.SemaphoreType.DMA((3,)),
         pltpu.SemaphoreType.DMA((2,)),
         pltpu.SemaphoreType.DMA((2,)),
         pltpu.SemaphoreType.DMA,
-        pltpu.SemaphoreType.DMA((2, 3)),
+        pltpu.SemaphoreType.DMA((RING, 3)),
     ]
     out_shape = jax.ShapeDtypeStruct((tokens, width), jnp.bfloat16) if last else jax.ShapeDtypeStruct((tokens * pieces, LANES), jnp.float32)
     rows = experts * tokens // 8
     return pl.pallas_call(
-        functools.partial(moe_kernel, first, last),
-        in_specs=[smem] * 3 + [hbm] * (3 + len(extra)),
+        functools.partial(moe_kernel, first, last, len(weights)),
+        in_specs=[smem] * 3 + [hbm] * (2 + len(extra) + len(weights)),
         out_specs=hbm,
         out_shape=out_shape,
         scratch_shapes=scratch,
         compiler_params=pltpu.CompilerParams(vmem_limit_bytes=VMEM_LIMIT),
         cost_estimate=pl.CostEstimate(flops=2 * rows * wrows * inter, bytes_accessed=2 * experts * wrows * inter, transcendentals=0),
         name="routed_experts",
-    )(meta, ranks, gates, table, u_norm, *extra, weights)
-
-
-def route_plan(choice_ids, num_experts, groups):
+    )(meta, ranks, gates, table, u_norm, *extra, *weights)
+
+
+def route_plan(choice_ids, num_experts, groups, here):
     tokens, num_top = choice_ids.shape
     local = num_experts // groups
     device, index = choice_ids // local, choice_ids % local
     rank = jnp.zeros_like(choice_ids)
     low = 0
-    for size in CHUNKS:
-        rank = jnp.where((index >= low) & (index < low + size), low * groups + device * size + index - low, rank)
+    for way, size in PLAN:
+        place = device ^ here if way == "P" else device
+        rank = jnp.where((index >= low) & (index < low + size), low * groups + place * size + index - low, rank)
         low += size
     hits = rank[:, :, None] == jnp.arange(num_experts)[None, None, :]
     counts = jnp.sum(hits.astype(jnp.int32), axis=(0, 1))
@@ -384,6 +406,24 @@
     return table, orders, metas
 
 
+def after(vals, token):
+    return lax.optimization_barrier((vals, token))[0]
+
+
+def spread_pair(own, early, late):
+    count = lax.axis_size(AXIS)
+
+    def send(bit, vals):
+        return lax.ppermute(vals, AXIS, [(i, i ^ bit) for i in range(count)])
+
+    own = after(own, early)
+    along_x, along_y = after((send(2, own), send(4, own)), late)
+    far = send(4, along_x[:1]), send(2, along_y[1:])
+    own_core = [own, along_x, along_y, *far]
+    other = [send(1, vals) for vals in own_core]
+    return (own, other[0], along_x, other[1], along_y, other[2], *far, *other[3:])
+
+
 def solution(mesh):
     groups = mesh.shape[AXIS]
     rows_spec = P(AXIS, None)
@@ -411,7 +451,6 @@
 
         inner = w_gate.shape[1]
         gate_up = gather(jnp.concatenate([w_gate, w_up], axis=1))
-        down = gather(w_down)
         kv_rank = w_uk.shape[0] * groups
         rope_dim = w_dkv.shape[1] - kv_rank
         heads = (w_uq.shape[1] - w_uk.shape[1]) // rope_dim
@@ -419,26 +458,27 @@
         per_head = w_uq.reshape(w_uq.shape[0], heads, nope_dim + rope_dim)
         uq_local = jnp.concatenate([per_head[:, :, :nope_dim].reshape(-1, heads * nope_dim), per_head[:, :, nope_dim:].reshape(-1, heads * rope_dim)], axis=1)
         dkv_local = jnp.concatenate([w_dkv, swap_halves(w_dkv[:, kv_rank:], rope_dim // 2)], axis=1)
-        shards = [w_dq, dkv_local, uq_local, w_uk, w_uv, w_out]
+        shards = [w_down, w_dq, dkv_local, uq_local, w_uk, w_uv, w_out]
         blocks = [to_blocks(s) for s in shards]
         attn_w = gather(jnp.concatenate(blocks, axis=0)[None])
         starts = [sum(b.shape[0] for b in blocks[:i]) for i in range(len(blocks))]
-        w_dq, w_dkv, w_uq, w_uk, w_uv, w_out = [from_blocks(attn_w, st, s.shape[0], s.shape[1]) for st, s in zip(starts, shards)]
+        down, w_dq, w_dkv, w_uq, w_uk, w_uv, w_out = [from_blocks(attn_w, st, s.shape[0], s.shape[1]) for st, s in zip(starts, shards)]
 
         down_blocks = we_down.reshape(we_down.shape[0], inter, width // inter, inter).transpose(0, 2, 1, 3).reshape(we_down.shape[0], width, inter)
         pack = jnp.concatenate([we_gate, we_up, down_blocks], axis=1)
-        expert_w = []
-        low = 0
-        for size in CHUNKS:
-            expert_w.append(gather(pack[low : low + size]))
-            low += size
-
-        table, ranks, metas = route_plan(choice_ids, num_experts, groups)
+        table, ranks, metas = route_plan(choice_ids, num_experts, groups, lax.axis_index(AXIS))
 
         normed = rms_norm(flat_x, g_mlp)
         hidden = (jax.nn.silu(mm(normed, gate_up[:, :inner])) * mm(normed, gate_up[:, inner:])).astype(jnp.bfloat16)
         mlp_out = mm(hidden, down).astype(jnp.bfloat16)
         h_one = (flat_x.astype(jnp.float32) + mlp_out.astype(jnp.float32)).astype(jnp.bfloat16)
+        expert_w = []
+        low = 0
+        for way, size in PLAN:
+            part = pack[low : low + size]
+            expert_w.append(spread_pair(part, gate_up, h_one) if way == "P" else (gather(part),))
+            low += size
+
         attn_out = attention(rms_norm(h_one, g_attn), w_dq, g_q, w_uq, w_dkv, g_kv, w_uk, w_uv, w_out, seq_len, rope_dim)
         h_two = (h_one.astype(jnp.float32) + attn_out.astype(jnp.float32)).astype(jnp.bfloat16)
         u_norm = rms_norm(h_two, g_moe)

time: 734 us -> 796 us (1.084)
  the two profiles are of different devices: /device:TPU:5 before, /device:TPU:0 now
where the time goes in v3:
time: 796 us; the launch traced here: 782 us
  Pallas kernels  362 us (45%)
  matrix products  182 us (23%)
  local copies, waits for them, and re-layouts  79.6 us (10%)
  other arithmetic  63.5 us (8%)
  waiting for transfers between devices  49.8 us (6%)
  blocking collectives  25 us (3%)
  between operations  14.7 us (2%)
    pallas_call x4, Pallas kernels, moe_call(): pl.pallas_call(functools.partial(moe_kernel, first, last, len(weights)),...  284 us
    dot_general x12, matrix products, mm(): return jnp.dot(lhs, rhs, preferred_element_type=jnp.float32)  174 us
    pallas_call x1, Pallas kernels, attention_core(): pl.pallas_call(functools.partial(attn_kernel, scale, 256), grid=(seqs, he...  77.9 us
    ppermute x9, waiting for transfers between devices, send(): return lax.ppermute(vals, AXIS, [(i, i ^ bit) for i in range(count)])  49.7 us
    unnamed x1, blocking collectives  25 us
    unnamed x112, local copies, waits for them, and re-layouts  17.4 us
    concatenate x1, other arithmetic, local(): pack = jnp.concatenate([we_gate, we_up, down_blocks], axis=1)  16.2 us
  transfers between devices with their start and end apart: 14, of which 2 were waited for; matrix products, arithmetic and copies ran while one was open for 39% of the time, Pallas kernels for 40%

profile of v3, /device:TPU:0, one launch (start us, length us, event | category | flops | bytes accessed | tf_op | source)
XLA Modules:
  0.0 782.3 jit_solution(3143349350115197308)
XLA Ops:
  6.6 2.6 pad_maximum_fusion.3
  9.3 1.1 reshape.471
  10.4 1.3 copy.135
  13.3 1.1 copy-done.7
  14.5 3.4 copy.181
  17.9 1.2 copy-done.5
  19.1 2.7 copy-done.6
  21.8 16.2 %pad_maximum_fusion = bf16[8,3072,256]{2,1,0:T(8,128)(2,1)S(1)} fusion(bf16[8,1024,256]{2,1,0:T(8,128)(2,1)S(1)} %bitcast.167, bf16[8,1024,256]{2,1,0:T(8,128)(2,1)S(1)} %copy-done.5, bf16[8,1024,256]{2,1,0:T(8,128)(2,1)S(1)} %copy-done.6), kind=kLoop, calls=%fused_computation.20 | loop fusion | flops 37748736 | bytes 25165824 | tf_op jit(solution)/shard_map/concatenate | solution.py:468
  38.0 6.1 copy-done.2
  44.1 2.5 slice.162
  46.7 5.8 fusion.68
  52.7 2.6 pad_maximum_fusion.2
  57.5 25.0 %all-reduce.1 = f32[3712]{0:T(1024)S(1)} all-reduce(f32[3712]{0:T(1024)S(1)} %dynamic-update-slice), channel_id=2, replica_groups=mesh['fsdp'=8] {'fsdp'}, use_global_device_ids=true, to_apply=%add.1 | all-reduce | flops 3712 | bytes 29696
  83.3 1.9 multiply_cosine_fusion
  85.3 1.3 pad_maximum_fusion.4
  86.6 1.9 pad_maximum_fusion.6
  88.6 2.9 iota_add_fusion
  91.5 2.8 add.313
  95.7 9.2 %sort.8 = s32[49152]{0:T(1024)S(1)} sort(s32[49152]{0:T(1024)S(1)} %pad_add_fusion.1), dimensions={0}, to_apply=%region_6.7 | sort | flops 786432 | bytes 393216 | tf_op jit(solution)/shard_map/jit(sort)/sort | solution.py:387
  107.4 5.5 fusion.7
  114.3 8.0 %fusion.9 = bf16[4096,1024]{1,0:T(8,128)(2,1)} fusion(bf16[4,1024,1024]{2,1,0:T(8,128)(2,1)} %param.25, f32[1024]{0:T(1024)S(1)} %get-tuple-element.27, f32[4096]{0:T(1024)S(1)} %bitcast.223), kind=kLoop, calls=%fused_computation.18 | loop fusion | flops 16777216 | bytes 16797696 | tf_op jit(solution)/shard_map/convert_element_type | solution.py:29
  123.0 1.1 pad_add_fusion.tab_hbm
  124.0 2.2 collective-permute-start.1
  126.9 33.9 %fusion.19 = f32[4096,2816]{1,0:T(8,128)} fusion(bf16[4096,1024]{1,0:T(8,128)(2,1)} %fusion.9, bf16[1024,5632]{1,0:T(8,128)(2,1)} %all-gather.8.cloned.1.call-done), kind=kOutput, calls=%fused_computation.40 | convolution fusion | flops 23622320128 | bytes 60293120 | tf_op jit(solution)/shard_map/dot_general | solution.py:33
  160.8 37.4 %multiply_convert_fusion.clone.3.clone.4 = bf16[4096,2816]{1,0:T(8,128)(2,1)} fusion(f32[4096,2816]{1,0:T(8,128)} %fusion.19, bf16[4096,1024]{1,0:T(8,128)(2,1)} %fusion.9, bf16[1024,5632]{1,0:T(8,128)(2,1)} %all-gather.8.cloned.1.call-done), kind=kOutput, calls=%fused_computation.clone.clone.clone.clone.clone.clone.clone.1 | convolution fusion | flops 23691526144 | bytes 83361792 | tf_op jit(solution)/shard_map/dot_general | solution.py:33
  198.2 3.2 slice.145
  201.5 4.7 copy.117
  206.2 30.9 %fusion.3 = (f32[4096]{0:T(1024)S(1)}, bf16[4096,1024]{1,0:T(8,128)(2,1)}) fusion(bf16[352,8,8,128]{3,2,1,0:T(8,128)(2,1)} %bitcast.179, bf16[4,1024,1024]{2,1,0:T(8,128)(2,1)S(1)} %bitcast.170, bf16[4096,2816]{1,0:T(8,128)(2,1)} %multiply_convert_fusion.clone.3.clone.4), kind=kOutput, calls=%fused_computation.9 | convolution fusion | flops 23655870464 | bytes 45629440 | tf_op jit(solution)/shard_map/dot_general | solution.py:33
  237.1 2.4 slice.149
  239.5 1.7 slice.160
  241.2 2.4 fusion.70
  243.7 2.4 copy.119
  246.1 1.6 copy.120
  249.8 1.9 copy.121
  251.8 1.8 rev.7
  253.6 1.9 copy.122
  255.5 2.1 fusion.69
  258.6 1.3 copy.123
  260.0 10.9 %convolution_convert_fusion.5 = bf16[4096,384]{1,0:T(8,128)(2,1)S(1)} fusion(bf16[4096,1024]{1,0:T(8,128)(2,1)} %get-tuple-element.40, f32[1024]{0:T(1024)S(1)} %copy-done.29, f32[4096]{0:T(1024)S(1)} %add_rsqrt_fusion.3, bf16[48,8,8,128]{3,2,1,0:T(8,128)(2,1)} %bitcast.202), kind=kOutput, calls=%fused_computation.42 | convolution fusion | flops 3239575552 | bytes 12341248 | tf_op jit(solution)/shard_map/dot_general | solution.py:33
  271.3 2.8 copy.126
  274.2 4.4 fusion.12
  280.0 4.6 convolution_convert_fusion.2.kn_ref
  284.6 4.7 convolution_convert_fusion.1.v_ref
  289.3 7.0 convolution_convert_fusion.4.qn_ref
  296.3 2.0 pad_maximum_fusion.1.kr_ref
  298.3 7.0 convolution_convert_fusion.3.qp_ref.qs_ref
  305.3 77.9 %attention_core.1 = bf16[4096,1024]{1,0:T(8,128)(2,1)} custom-call(bf16[4096,1024]{1,0:T(8,128)(2,1)} %convolution_convert_fusion.4.qn_ref, bf16[4096,1024]{1,0:T(8,128)(2,1)} %convolution_convert_fusion.3.qp_ref.qs_ref, bf16[4096,1024]{1,0:T(8,128)(2,1)} %convolution_convert_fusion.3.qp_ref.qs_ref, bf16[4096,1024]{1,0:T(8,128)(2,1)} %convolution_convert_fusion.2.kn_ref, ...), custom_call_target="tpu_custom_call" | custom-call | flops 17179869184 | bytes 41943040 | tf_op jit(solution)/shard_map/attention_core/pallas_call | solution.py:74
  383.2 15.3 %fusion = (f32[4096]{0:T(1024)S(1)}, bf16[4096,1024]{1,0:T(8,128)(2,1)S(1)}) fusion(bf16[4096,1024]{1,0:T(8,128)(2,1)} %attention_core.1, bf16[128,8,8,128]{3,2,1,0:T(8,128)(2,1)S(1)} %bitcast.190, bf16[4096,1024]{1,0:T(8,128)(2,1)} %get-tuple-element.40), kind=kOutput, calls=%fused_computation.6 | convolution fusion | flops 8623484928 | bytes 27279360 | tf_op jit(solution)/shard_map/dot_general | solution.py:33
  398.5 2.2 fusion.2.u_hbm
  400.7 1.1 copy-done.4
  401.9 7.7 fusion.24
  409.6 1.6 select_reduce_fusion
  411.2 2.7 slice.136
  413.9 1.7 collective-permute-start.5
  415.6 3.1 slice.137
  419.3 4.4 fusion.73
  426.5 13.4 %convolution_convert_fusion.refs_1_ = bf16[4096,1024]{1,0:T(8,128)(2,1)} fusion(bf16[256,1024]{1,0:T(8,128)(2,1)S(1)} %copy-done, bf16[4096,1024]{1,0:T(8,128)(2,1)} %copy-done.1, bf16[1024,256]{1,0:T(8,128)(2,1)S(1)} %copy-done.41, f32[4096,256]{1,0:T(8,128)} %fusion.73), kind=kOutput, calls=%fused_computation.29 | convolution fusion | flops 4305453056 | bytes 22020096 | tf_op jit(solution)/shard_map/dot_general | solution.py:33
  439.9 44.9 %collective-permute-done.5.refs_7_ = bf16[1,3072,256]{2,1,0:T(8,128)(2,1)} collective-permute-done((bf16[1,3072,256]{2,1,0:T(8,128)(2,1)}, bf16[1,3072,256]{2,1,0:T(8,128)(2,1)}, u32[]{:S(2)}, u32[]{:S(2)}) %collective-permute-start.5) | collective-permute-done | bytes 1572896 | tf_op jit(solution)/shard_map/ppermute | solution.py:417
  484.9 4.8 collective-permute-done.6.refs_8_
  489.6 95.2 %routed_experts.4.refs_0_ = f32[32768,128]{1,0:T(8,128)} custom-call(s32[67]{0:T(128)} %get-tuple-element.31.meta_ref, s32[192]{0:T(256)} %select_reduce_fusion.3.rank_ref, f32[32776]{0:T(1024)} %concatenate.62.gate_ref, s32[192,2,256]{2,1,0:T(2,128)} %pad_add_fusion.tab_hbm, bf16[4096,1024]{1,0:T(8,128)(2,1)} %copy-done.1, bf16[4096,1024]{1,0:T(8,128)(2,1)} %copy-done.4, ...), custom_call_target="tpu_custom_call" | custom-call | flops 19327352832 | bytes 37748736 | tf_op jit(solution)/shard_map/routed_experts/pallas_call | solution.py:358
  584.9 1.1 copy-done.16
  586.1 72.0 %routed_experts.5.refs_0_ = f32[32768,128]{1,0:T(8,128)} custom-call(s32[67]{0:T(128)} %get-tuple-element.32.meta_ref, s32[192]{0:T(256)} %select_reduce_fusion.3.rank_ref, f32[32776]{0:T(1024)} %concatenate.62.gate_ref, s32[192,2,256]{2,1,0:T(2,128)} %pad_add_fusion.tab_hbm, bf16[4096,1024]{1,0:T(8,128)(2,1)} %copy-done.1, ...), custom_call_target="tpu_custom_call" | custom-call | flops 12884901888 | bytes 25165824 | tf_op jit(solution)/shard_map/routed_experts/pallas_call | solution.py:358
  658.1 68.8 %routed_experts.6.refs_0_ = f32[32768,128]{1,0:T(8,128)} custom-call(s32[67]{0:T(128)} %get-tuple-element.33.meta_ref, s32[192]{0:T(256)} %select_reduce_fusion.3.rank_ref, f32[32776]{0:T(1024)} %concatenate.62.gate_ref, s32[192,2,256]{2,1,0:T(2,128)} %pad_add_fusion.tab_hbm, bf16[4096,1024]{1,0:T(8,128)(2,1)} %copy-done.1, ...), custom_call_target="tpu_custom_call" | custom-call | flops 12884901888 | bytes 25165824 | tf_op jit(solution)/shard_map/routed_experts/pallas_call | solution.py:358
  726.9 48.4 %routed_experts.7 = bf16[4096,1024]{1,0:T(8,128)(2,1)} custom-call(s32[67]{0:T(128)} %get-tuple-element.34.meta_ref, s32[192]{0:T(256)} %select_reduce_fusion.3.rank_ref, f32[32776]{0:T(1024)} %concatenate.62.gate_ref, s32[192,2,256]{2,1,0:T(2,128)} %pad_add_fusion.tab_hbm, bf16[4096,1024]{1,0:T(8,128)(2,1)} %copy-done.1, ...), custom_call_target="tpu_custom_call" | custom-call | flops 6442450944 | bytes 12582912 | tf_op jit(solution)/shard_map/routed_experts/pallas_call | solution.py:358
  (205 shorter events, 19.8 us)
Async XLA Ops:
  6.5 420.0 %copy-start = (bf16[256,1024]{1,0:T(8,128)(2,1)S(1)}, bf16[256,1024]{1,0:T(8,128)(2,1)}, u32[]{:S(2)}) copy-start(bf16[256,1024]{1,0:T(8,128)(2,1)} %param.46) | copy-start | bytes 1572868
  6.5 5.3 copy-start.23
  6.5 5.5 slice-start.2
  6.5 5.6 copy-start.22
  6.5 6.1 copy-start.25
  6.5 6.1 copy-start.26
  6.6 6.2 copy-start.21
  6.6 117.5 %all-gather.8.cloned.1.call-start = ((), (), s32[]{:S(2)}) async-start(), calls=%async_computation | async-start | bytes 12976128 | tf_op jit(solution)/shard_map/all_gather | solution.py:436
  9.2 189.0 %all-gather.16.cloned.1.call-start = ((), (), s32[]{:S(2)}) async-start(), calls=%async_computation.4 | async-start | bytes 13123584 | tf_op jit(solution)/shard_map/all_gather | solution.py:436
  13.3 1.1 copy-start.7
  14.4 475.2 %all-gather.10.cloned.1.call-start = ((), (), s32[]{:S(2)}) async-start(), calls=%async_computation.1 | async-start | bytes 42467328 | tf_op jit(solution)/shard_map/all_gather | solution.py:436
  14.5 4.6 copy-start.5
  14.5 7.3 copy-start.6
  17.9 20.1 %copy-start.3 = (bf16[8,32,4,8,256]{4,3,1,2,0:T(8,128)(2,1)}, bf16[8,32,4,8,256]{4,3,1,2,0:T(8,128)(2,1)S(1)}, u32[]{:S(2)}) copy-start(bf16[8,32,4,8,256]{4,3,1,2,0:T(8,128)(2,1)S(1)} %copy.181) | copy-start | bytes 12582916
  38.0 6.1 copy-start.2
  46.6 611.4 %all-gather.12.cloned.1.call-start = ((), (), s32[]{:S(2)}) async-start(), calls=%async_computation.2 | async-start | bytes 28311552 | tf_op jit(solution)/shard_map/all_gather | solution.py:436
  52.5 2.8 copy-start.17
  52.6 4.6 copy-start.31
  52.6 4.6 copy-start.32
  52.6 4.6 copy-start.33
  52.6 4.6 copy-start.34
  52.6 4.6 copy-start.35
  52.6 674.3 %all-gather.14.cloned.1.call-start = ((), (), s32[]{:S(2)}) async-start(), calls=%async_computation.3 | async-start | bytes 14155776 | tf_op jit(solution)/shard_map/all_gather | solution.py:436
  82.6 12.8 %copy-start.24 = (f32[8,464]{1,0:T(8,128)}, f32[8,464]{1,0:T(8,128)S(1)}, u32[]{:S(2)}) copy-start(f32[8,464]{1,0:T(8,128)S(1)} %reshape.504) | copy-start | bytes 44548
  86.6 18.8 %copy-start.36 = (s32[4]{0:T(128)S(1)}, s32[4]{0:T(128)}, u32[]{:S(2)}) copy-start(s32[4]{0:T(128)} %constant.153.clone) | copy-start | bytes 52
  86.6 18.8 %copy-start.37 = (s32[4]{0:T(128)S(1)}, s32[4]{0:T(128)}, u32[]{:S(2)}) copy-start(s32[4]{0:T(128)} %constant.154.clone) | copy-start | bytes 52
  86.6 18.8 %copy-start.38 = (s32[4]{0:T(128)S(1)}, s32[4]{0:T(128)}, u32[]{:S(2)}) copy-start(s32[4]{0:T(128)} %constant.159) | copy-start | bytes 52
  95.7 17.3 %slice-start.3 = ((f32[8,464]{1,0:T(8,128)}), f32[8,48]{1,0:T(8,128)S(1)}, s32[]{:S(2)}) async-start(f32[8,464]{1,0:T(8,128)} %copy-done.24), calls=%async_computation.8 | async-start | bytes 8192 | tf_op jit(solution)/shard_map/slice | solution.py:450
  124.0 460.8 %collective-permute-start = (bf16[2,3072,256]{2,1,0:T(8,128)(2,1)}, bf16[2,3072,256]{2,1,0:T(8,128)(2,1)}, u32[]{:S(2)}, u32[]{:S(2)}) collective-permute-start(bf16[2,3072,256]{2,1,0:T(8,128)(2,1)} %get-tuple-element.8.refs_1_), channel_id=1, source_target_pairs={{0,1},{1,0},{2,3},{3,2},{4,5},{5,4},{6,7},{7,6}} | collective-permute-start | bytes 9437192 | tf_op jit(solution)/shard_map/ppermute | solution.py:417
  124.0 287.2 %collective-permute-start.1 = (bf16[2,3072,256]{2,1,0:T(8,128)(2,1)}, bf16[2,3072,256]{2,1,0:T(8,128)(2,1)}, u32[]{:S(2)}, u32[]{:S(2)}) collective-permute-start(bf16[2,3072,256]{2,1,0:T(8,128)(2,1)} %get-tuple-element.8.refs_1_), channel_id=1, source_target_pairs={{0,2},{1,3},{2,0},{3,1},{4,6},{5,7},{6,4},{7,5}} | collective-permute-start | bytes 9437192 | tf_op jit(solution)/shard_map/ppermute | solution.py:417
  126.2 285.0 %collective-permute-start.2 = (bf16[2,3072,256]{2,1,0:T(8,128)(2,1)}, bf16[2,3072,256]{2,1,0:T(8,128)(2,1)}, u32[]{:S(2)}, u32[]{:S(2)}) collective-permute-start(bf16[2,3072,256]{2,1,0:T(8,128)(2,1)} %get-tuple-element.8.refs_1_), channel_id=1, source_target_pairs={{0,4},{1,5},{2,6},{3,7},{4,0},{5,1},{6,2},{7,3}} | collective-permute-start | bytes 9437192 | tf_op jit(solution)/shard_map/ppermute | solution.py:417
  198.2 8.0 %slice-start = ((s8[8388608]{0:T(1024)(128)(4,1)}), s8[4194304]{0:T(1024)(128)(4,1)S(1)}, s32[]{:S(2)}) async-start(s8[8388608]{0:T(1024)(128)(4,1)} %bitcast.169), calls=%async_computation.5 | async-start | bytes 8388608
  201.5 4.7 slice-start.1
  247.7 12.2 %copy-start.29 = (f32[1024]{0:T(1024)S(1)}, f32[1024]{0:T(1024)}, u32[]{:S(2)}) copy-start(f32[1024]{0:T(1024)} %get-tuple-element.26) | copy-start | bytes 12292
  248.0 1.0 copy-start.12
  259.9 14.2 %slice-start.4 = ((s8[8388608]{0:T(1024)(128)(4,1)}), s8[4194304]{0:T(1024)(128)(4,1)S(1)}, s32[]{:S(2)}) async-start(s8[8388608]{0:T(1024)(128)(4,1)} %bitcast.227), calls=%async_computation.9 | async-start | bytes 8388608
  259.9 11.2 %copy-start.14 = (bf16[8,256,128]{2,1,0:T(8,128)(2,1)S(1)}, bf16[8,256,128]{2,1,0:T(8,128)(2,1)}, u32[]{:S(2)}) copy-start(bf16[8,256,128]{2,1,0:T(8,128)(2,1)} %get-tuple-element.19) | copy-start | bytes 1572868
  259.9 14.2 %slice-start.5 = ((s8[8388608]{0:T(1024)(128)(4,1)}), s8[4194304]{0:T(1024)(128)(4,1)S(1)}, s32[]{:S(2)}) async-start(s8[8388608]{0:T(1024)(128)(4,1)} %bitcast.227), calls=%async_computation.10 | async-start | bytes 8388608
  270.9 3.3 copy-start.19
  274.2 5.1 copy-start.8
  274.2 5.1 copy-start.9
  278.6 1.3 copy-start.10
  278.6 1.3 copy-start.27
  284.6 4.7 copy-start.13
  284.6 4.7 copy-start.30
  289.2 7.0 copy-start.39
  289.2 9.0 %copy-start.15 = (bf16[384,512]{1,0:T(8,128)(2,1)S(1)}, bf16[384,512]{1,0:T(8,128)(2,1)}, u32[]{:S(2)}) copy-start(bf16[384,512]{1,0:T(8,128)(2,1)} %slice.151) | copy-start | bytes 1179652
  289.3 9.0 %copy-start.20 = (bf16[384,512]{1,0:T(8,128)(2,1)S(1)}, bf16[384,512]{1,0:T(8,128)(2,1)}, u32[]{:S(2)}) copy-start(bf16[384,512]{1,0:T(8,128)(2,1)} %copy.122) | copy-start | bytes 1179652
  305.3 77.9 %copy-start.11 = (bf16[8,128,8,128]{3,2,1,0:T(8,128)(2,1)S(1)}, bf16[8,128,8,128]{3,2,1,0:T(8,128)(2,1)}, u32[]{:S(2)}) copy-start(bf16[8,128,8,128]{3,2,1,0:T(8,128)(2,1)} %copy.126) | copy-start | bytes 6291460
  383.2 15.3 %copy-start.28 = (f32[1024]{0:T(1024)S(1)}, f32[1024]{0:T(1024)}, u32[]{:S(2)}) copy-start(f32[1024]{0:T(1024)} %get-tuple-element.25) | copy-start | bytes 12292
  398.4 3.4 copy-start.4
  398.5 3.4 copy-start.42
  401.9 17.4 %copy-start.1 = (bf16[4096,1024]{1,0:T(8,128)(2,1)}, bf16[4096,1024]{1,0:T(8,128)(2,1)S(1)}, u32[]{:S(2)}) copy-start(bf16[4096,1024]{1,0:T(8,128)(2,1)S(1)} %fusion.2.u_hbm) | copy-start | bytes 25165828
  401.9 7.7 copy-start.18
  409.6 9.7 %copy-start.40 = (bf16[1024,256]{1,0:T(8,128)(2,1)S(1)}, bf16[1024,256]{1,0:T(8,128)(2,1)}, u32[]{:S(2)}) copy-start(bf16[1024,256]{1,0:T(8,128)(2,1)} %param.44) | copy-start | bytes 1572868
  413.9 71.0 %collective-permute-start.5 = (bf16[1,3072,256]{2,1,0:T(8,128)(2,1)}, bf16[1,3072,256]{2,1,0:T(8,128)(2,1)}, u32[]{:S(2)}, u32[]{:S(2)}) collective-permute-start(bf16[1,3072,256]{2,1,0:T(8,128)(2,1)} %slice.136), channel_id=1, source_target_pairs={{0,4},{1,5},{2,6},{3,7},{4,0},{5,1},{6,2},{7,3}} | collective-permute-start | bytes 4718600 | tf_op jit(solution)/shard_map/ppermute | solution.py:417
  418.7 7.9 %copy-start.41 = (bf16[1024,256]{1,0:T(8,128)(2,1)S(1)}, bf16[1024,256]{1,0:T(8,128)(2,1)}, u32[]{:S(2)}) copy-start(bf16[1024,256]{1,0:T(8,128)(2,1)} %param.45) | copy-start | bytes 1572868
  418.7 70.9 %collective-permute-start.6 = (bf16[1,3072,256]{2,1,0:T(8,128)(2,1)}, bf16[1,3072,256]{2,1,0:T(8,128)(2,1)}, u32[]{:S(2)}, u32[]{:S(2)}) collective-permute-start(bf16[1,3072,256]{2,1,0:T(8,128)(2,1)} %slice.137), channel_id=1, source_target_pairs={{0,2},{1,3},{2,0},{3,1},{4,6},{5,7},{6,4},{7,5}} | collective-permute-start | bytes 4718600 | tf_op jit(solution)/shard_map/ppermute | solution.py:417
  426.0 158.9 %collective-permute-start.3 = (bf16[2,3072,256]{2,1,0:T(8,128)(2,1)}, bf16[2,3072,256]{2,1,0:T(8,128)(2,1)}, u32[]{:S(2)}, u32[]{:S(2)}) collective-permute-start(bf16[2,3072,256]{2,1,0:T(8,128)(2,1)} %collective-permute-done.1.refs_3_), channel_id=1, source_target_pairs={{0,1},{1,0},{2,3},{3,2},{4,5},{5,4},{6,7},{7,6}} | collective-permute-start | bytes 9437192 | tf_op jit(solution)/shard_map/ppermute | solution.py:417
  426.0 158.9 %collective-permute-start.4 = (bf16[2,3072,256]{2,1,0:T(8,128)(2,1)}, bf16[2,3072,256]{2,1,0:T(8,128)(2,1)}, u32[]{:S(2)}, u32[]{:S(2)}) collective-permute-start(bf16[2,3072,256]{2,1,0:T(8,128)(2,1)} %collective-permute-done.2.refs_5_), channel_id=1, source_target_pairs={{0,1},{1,0},{2,3},{3,2},{4,5},{5,4},{6,7},{7,6}} | collective-permute-start | bytes 9437192 | tf_op jit(solution)/shard_map/ppermute | solution.py:417
  484.9 100.1 %collective-permute-start.7 = (bf16[1,3072,256]{2,1,0:T(8,128)(2,1)}, bf16[1,3072,256]{2,1,0:T(8,128)(2,1)S(1)}, u32[]{:S(2)}, u32[]{:S(2)}) collective-permute-start(bf16[1,3072,256]{2,1,0:T(8,128)(2,1)} %collective-permute-done.5.refs_7_), channel_id=1, source_target_pairs={{0,1},{1,0},{2,3},{3,2},{4,5},{5,4},{6,7},{7,6}} | collective-permute-start | bytes 4718600 | tf_op jit(solution)/shard_map/ppermute | solution.py:417
  489.6 95.3 %collective-permute-start.8 = (bf16[1,3072,256]{2,1,0:T(8,128)(2,1)}, bf16[1,3072,256]{2,1,0:T(8,128)(2,1)}, u32[]{:S(2)}, u32[]{:S(2)}) collective-permute-start(bf16[1,3072,256]{2,1,0:T(8,128)(2,1)} %collective-permute-done.6.refs_8_), channel_id=1, source_target_pairs={{0,1},{1,0},{2,3},{3,2},{4,5},{5,4},{6,7},{7,6}} | collective-permute-start | bytes 4718600 | tf_op jit(solution)/shard_map/ppermute | solution.py:417
  584.9 1.1 copy-start.16
Sparse Core Ops, SparseCore 0:
  9.4 65.3 all-gather.7
  76.6 71.5 all-gather.15
  150.1 214.8 all-gather.9
  366.6 153.3 all-gather.11
  521.6 66.4 all-gather.13

commit v4 on v3

--- a/solution.py
+++ b/solution.py
@@ -16,6 +16,13 @@
 PITCH = TILE + 4
 GROUP = 4
 RING = 4
+STAGES = 6
+FF_STEP = 256
+DENSE_ROWS = 512
+PREP_ROWS = 512
+POST_ROWS = 512
+DENSE_LANES = 512
+ATTN_LANES = 256
 ORDER = (("D", 0), ("S", 5), ("D", 1), ("S", 5), ("D", 2), ("S", 5), ("D", 3), ("S", 5), ("G", 0), ("S", 6), ("U", 0), ("S", 5), ("G", 1), ("S", 5), ("U", 1), ("S", 5), ("G", 2), ("S", 6), ("U", 2), ("S", 5), ("G", 3), ("S", 6), ("U", 3), ("S", 6), ("H", 0))
 LANES = 128
 PLAN = (("S", 3), ("P", 2), ("S", 2), ("S", 1))
@@ -23,8 +30,7 @@
 VMEM_LIMIT = 60 * 1024 * 1024
 
 
-def rms_norm(vals, gain):
-    vals = vals.astype(jnp.float32)
+def rms_rows(vals, gain):
     scaled = vals * lax.rsqrt(jnp.mean(vals * vals, axis=-1, keepdims=True) + EPS)
     return (scaled * gain).astype(jnp.bfloat16)
 
@@ -33,31 +39,77 @@
     return jnp.dot(lhs, rhs, preferred_element_type=jnp.float32)
 
 
-def swiglu(rows, w_gate, w_up, w_down):
-    hidden = (jax.nn.silu(mm(rows, w_gate)) * mm(rows, w_up)).astype(jnp.bfloat16)
-    return mm(hidden, w_down).astype(jnp.bfloat16)
-
-
-def to_blocks(shard):
+def to_blocks(shard, lanes):
     rows, cols = shard.shape
-    return shard.reshape(rows, cols // LANES, LANES).transpose(1, 0, 2).reshape(-1, LANES)
-
-
-def from_blocks(gathered, start, rows, cols):
-    groups = gathered.shape[0]
-    blocks = cols // LANES
-    part = gathered[:, start : start + rows * blocks].reshape(groups, blocks, rows, LANES)
-    return part.transpose(0, 2, 1, 3).reshape(groups * rows, cols)
-
-
-def attn_kernel(scale, block, qn_ref, qp_ref, qs_ref, kn_ref, kr_ref, v_ref, cos_ref, sin_ref, o_ref):
+    return shard.reshape(rows, cols // lanes, lanes).transpose(1, 0, 2).reshape(-1, lanes)
+
+
+def load_weights(packed, starts, dsts, sems):
+    groups, _, lanes = packed.shape
+    for start, dst, sem in zip(starts, dsts, sems):
+        rows = dst.shape[0] // groups
+        for b in range(dst.shape[1] // lanes):
+            for d in range(groups):
+                src = packed.at[d, pl.ds(start + b * rows, rows), :]
+                pltpu.make_async_copy(src, dst.at[pl.ds(d * rows, rows), pl.ds(b * lanes, lanes)], sem).start()
+
+
+def await_weights(dst, sem):
+    pltpu.make_async_copy(dst, dst, sem).wait()
+
+
+def dense_kernel(starts, packed, gain_ref, x_ref, o_ref, w_in, w_out, hid, sems):
+    first = pl.program_id(0) == 0
+
+    @pl.when(first)
+    def _():
+        load_weights(packed, starts, (w_in, w_out), (sems.at[0], sems.at[1]))
+
+    rows = rms_rows(x_ref[...].astype(jnp.float32), gain_ref[...])
+
+    @pl.when(first)
+    def _():
+        await_weights(w_in, sems.at[0])
+        await_weights(w_out, sems.at[1])
+
+    inner = hid.shape[1]
+    for c in range(0, inner, FF_STEP):
+        gate = mm(rows, w_in[:, c : c + FF_STEP])
+        upper = mm(rows, w_in[:, inner + c : inner + c + FF_STEP])
+        hid[:, c : c + FF_STEP] = (jax.nn.silu(gate) * upper).astype(jnp.bfloat16)
+    for c in range(0, o_ref.shape[1], FF_STEP):
+        out = mm(hid[...], w_out[:, c : c + FF_STEP]).astype(jnp.bfloat16)
+        o_ref[:, c : c + FF_STEP] = (x_ref[:, c : c + FF_STEP].astype(jnp.float32) + out.astype(jnp.float32)).astype(jnp.bfloat16)
+
+
+def dense_layer(packed, starts, flat_x, gain, inner):
+    tokens, width = flat_x.shape
+    block = pl.BlockSpec((DENSE_ROWS, width), lambda i: (i, 0))
+    return pl.pallas_call(
+        functools.partial(dense_kernel, starts),
+        grid=(tokens // DENSE_ROWS,),
+        in_specs=[pl.BlockSpec(memory_space=pl.ANY), pl.BlockSpec((1, width), lambda i: (0, 0)), block],
+        out_specs=block,
+        out_shape=jax.ShapeDtypeStruct((tokens, width), jnp.bfloat16),
+        scratch_shapes=[
+            pltpu.VMEM((width, 2 * inner), jnp.bfloat16),
+            pltpu.VMEM((inner, width), jnp.bfloat16),
+            pltpu.VMEM((DENSE_ROWS, inner), jnp.bfloat16),
+            pltpu.SemaphoreType.DMA((2,)),
+        ],
+        compiler_params=pltpu.CompilerParams(vmem_limit_bytes=VMEM_LIMIT),
+        cost_estimate=pl.CostEstimate(flops=6 * tokens * width * inner, bytes_accessed=4 * tokens * width + 6 * width * inner, transcendentals=0),
+        name="dense_layer",
+    )(packed, gain.reshape(1, width), flat_x)
+
+
+def attn_kernel(scale, block, qn_ref, qr_ref, kn_ref, kr_ref, v_ref, o_ref):
     seq = qn_ref.shape[0]
     keys = jnp.concatenate([kn_ref[...], kr_ref[...]], axis=1)
     vals = v_ref[...]
     for start in range(0, seq, block):
         stop = start + block
-        turned = qp_ref[start:stop, :].astype(jnp.float32) * cos_ref[start:stop, :] + qs_ref[start:stop, :].astype(jnp.float32) * sin_ref[start:stop, :]
-        query = jnp.concatenate([qn_ref[start:stop, :], turned.astype(jnp.bfloat16)], axis=1)
+        query = jnp.concatenate([qn_ref[start:stop, :], qr_ref[start:stop, :]], axis=1)
         scores = lax.dot_general(query, keys[:stop], (((1,), (1,)), ((), ())), preferred_element_type=jnp.float32)
         row = lax.broadcasted_iota(jnp.int32, scores.shape, 0) + start
         col = lax.broadcasted_iota(jnp.int32, scores.shape, 1)
@@ -67,7 +119,7 @@
         o_ref[start:stop, :] = mm(probs, vals[:stop]).astype(jnp.bfloat16)
 
 
-def attention_core(q_nope, q_pe, k_nope, k_rot, values, cos_w, sin_w, seq_len, scale):
+def attention_core(q_nope, q_rot, k_nope, k_rot, values, seq_len, scale):
     tokens, width = q_nope.shape
     seqs, heads = tokens // seq_len, width // LANES
     spec = lambda fn: pl.BlockSpec((seq_len, LANES), fn)
@@ -77,67 +129,135 @@
         in_specs=[
             spec(lambda s, h: (s, h)),
             spec(lambda s, h: (s, h // 2)),
-            spec(lambda s, h: (s, heads // 2 + h // 2)),
             spec(lambda s, h: (s, h)),
             spec(lambda s, h: (s, h % 2)),
             spec(lambda s, h: (s, h)),
-            spec(lambda s, h: (0, 0)),
-            spec(lambda s, h: (0, 0)),
         ],
         out_specs=spec(lambda s, h: (s, h)),
         out_shape=jax.ShapeDtypeStruct((tokens, width), jnp.bfloat16),
         cost_estimate=pl.CostEstimate(flops=4 * tokens * seq_len * width, bytes_accessed=10 * tokens * width, transcendentals=0),
         name="attention_core",
-    )(q_nope, q_pe, q_pe, k_nope, k_rot, values, cos_w, sin_w)
-
-
-def swap_halves(cols, half):
-    rows, width = cols.shape
-    pairs = cols.reshape(rows, width // (2 * half), 2, half)
-    return pairs[:, :, ::-1, :].reshape(rows, width)
-
-
-def attention(normed, w_dq, g_q, w_uq, w_dkv, g_kv, w_uk, w_uv, w_out, seq_len, rope_dim):
-    tokens = normed.shape[0]
-    num_seqs = tokens // seq_len
-    kv_rank, heads_nope = w_uk.shape
-    half = rope_dim // 2
-    heads = (w_uq.shape[1] - heads_nope) // rope_dim
-    nope_dim = heads_nope // heads
-    positions = jnp.arange(seq_len)
-    inv_freq = 1.0 / (ROPE_BASE ** (jnp.arange(0, rope_dim, 2).astype(jnp.float32) / rope_dim))
-    angles = positions.astype(jnp.float32)[:, None] * inv_freq[None, :]
-    cos_t, sin_t = jnp.cos(angles), jnp.sin(angles)
-    cos_w = jnp.concatenate([cos_t] * 4, axis=1)
-    sin_w = jnp.concatenate([-sin_t, sin_t] * 2, axis=1)
-    q_lat = rms_norm(mm(normed, w_dq).astype(jnp.bfloat16), g_q)
-    q_nope = mm(q_lat, w_uq[:, :heads_nope]).astype(jnp.bfloat16)
-    w_pe = w_uq[:, heads_nope:]
-    q_pe = mm(q_lat, jnp.concatenate([w_pe, swap_halves(w_pe, half)], axis=1)).astype(jnp.bfloat16)
-
-    kv_all = mm(normed, w_dkv).astype(jnp.bfloat16)
-    latent = rms_norm(kv_all[:, :kv_rank], g_kv)
-    k_pe = kv_all[:, kv_rank:].reshape(num_seqs, seq_len, 2 * rope_dim).astype(jnp.float32)
-    k_rot = k_pe[..., :rope_dim] * cos_w[None, :, :rope_dim] + k_pe[..., rope_dim:] * sin_w[None, :, :rope_dim]
-    k_rot = k_rot.astype(jnp.bfloat16).reshape(tokens, rope_dim)
-    blank = jnp.zeros_like(k_rot)
-    k_rot = jnp.concatenate([k_rot, blank, blank, k_rot], axis=1)
-    k_nope = mm(latent, w_uk).astype(jnp.bfloat16)
-    values = mm(latent, w_uv).astype(jnp.bfloat16)
-    attended = attention_core(q_nope, q_pe, k_nope, k_rot, values, cos_w, sin_w, seq_len, (nope_dim + rope_dim) ** -0.5)
-    return mm(attended, w_out).astype(jnp.bfloat16)
-
-
-def moe_kernel(first, last, arrays, meta_ref, rank_ref, gate_ref, tab_hbm, u_hbm, *refs):
-    if first:
-        h_hbm, s_hbm, *refs = refs
-    else:
-        a_hbm, *refs = refs
+    )(q_nope, q_rot, k_nope, k_rot, values)
+
+
+def prep_kernel(starts, packed, ga_ref, gq_ref, gkv_ref, cos_ref, sin_ref, h_ref, qn_ref, qr_ref, kn_ref, kr_ref, v_ref, w_low, w_q, w_k, w_v, sems):
+    first = pl.program_id(0) == 0
+    weights = (w_low, w_q, w_k, w_v)
+
+    @pl.when(first)
+    def _():
+        load_weights(packed, starts, weights, [sems.at[i] for i in range(4)])
+
+    rows = rms_rows(h_ref[...].astype(jnp.float32), ga_ref[...])
+
+    @pl.when(first)
+    def _():
+        for i, dst in enumerate(weights):
+            await_weights(dst, sems.at[i])
+
+    lane = lax.broadcasted_iota(jnp.int32, (h_ref.shape[0], LANES), 1)
+
+    def turn(vals):
+        swapped = jnp.where(lane % 64 < 32, pltpu.roll(vals, LANES - 32, 1), pltpu.roll(vals, 32, 1))
+        return (vals * cos_ref[...] + swapped * sin_ref[...]).astype(jnp.bfloat16)
+
+    q_rank, kv_rank, nope = w_q.shape[0], w_k.shape[0], w_k.shape[1]
+    low = mm(rows, w_low[...]).astype(jnp.bfloat16).astype(jnp.float32)
+    q_lat = rms_rows(low[:, :q_rank], gq_ref[...])
+    latent = rms_rows(low[:, q_rank : q_rank + kv_rank], gkv_ref[...])
+    for c in range(0, nope, FF_STEP):
+        kn_ref[:, c : c + FF_STEP] = mm(latent, w_k[:, c : c + FF_STEP]).astype(jnp.bfloat16)
+        v_ref[:, c : c + FF_STEP] = mm(latent, w_v[:, c : c + FF_STEP]).astype(jnp.bfloat16)
+        qn_ref[:, c : c + FF_STEP] = mm(q_lat, w_q[:, c : c + FF_STEP]).astype(jnp.bfloat16)
+    for c in range(nope, w_q.shape[1], FF_STEP):
+        part = mm(q_lat, w_q[:, c : c + FF_STEP]).astype(jnp.bfloat16).astype(jnp.float32)
+        for j in range(0, FF_STEP, LANES):
+            qr_ref[:, c - nope + j : c - nope + j + LANES] = turn(part[:, j : j + LANES])
+    key = turn(low[:, q_rank + kv_rank :]).astype(jnp.float32)
+    kr_ref[:, 0:LANES] = jnp.where(lane < 64, key, 0.0).astype(jnp.bfloat16)
+    kr_ref[:, LANES : 2 * LANES] = jnp.where(lane < 64, 0.0, key).astype(jnp.bfloat16)
+
+
+def attention_prep(packed, starts, h_one, g_attn, g_q, g_kv, cos_w, sin_w, nope, pe):
+    tokens, width = h_one.shape
+    seq_blocks = cos_w.shape[0] // PREP_ROWS
+    q_rank, kv_rank = g_q.shape[0], g_kv.shape[0]
+    vec = lambda n: pl.BlockSpec((1, n), lambda i: (0, 0))
+    rows = lambda n: pl.BlockSpec((PREP_ROWS, n), lambda i: (i, 0))
+    table = pl.BlockSpec((PREP_ROWS, LANES), lambda i: (i % seq_blocks, 0))
+    cols = (nope, pe, nope, 2 * LANES, nope)
+    return pl.pallas_call(
+        functools.partial(prep_kernel, starts),
+        grid=(tokens // PREP_ROWS,),
+        in_specs=[pl.BlockSpec(memory_space=pl.ANY), vec(width), vec(q_rank), vec(kv_rank), table, table, rows(width)],
+        out_specs=[rows(n) for n in cols],
+        out_shape=[jax.ShapeDtypeStruct((tokens, n), jnp.bfloat16) for n in cols],
+        scratch_shapes=[
+            pltpu.VMEM((width, q_rank + kv_rank + LANES), jnp.bfloat16),
+            pltpu.VMEM((q_rank, nope + pe), jnp.bfloat16),
+            pltpu.VMEM((kv_rank, nope), jnp.bfloat16),
+            pltpu.VMEM((kv_rank, nope), jnp.bfloat16),
+            pltpu.SemaphoreType.DMA((4,)),
+        ],
+        compiler_params=pltpu.CompilerParams(vmem_limit_bytes=VMEM_LIMIT),
+        cost_estimate=pl.CostEstimate(flops=2 * tokens * (width * 768 + q_rank * (nope + pe) + 2 * kv_rank * nope), bytes_accessed=12 * tokens * width, transcendentals=0),
+        name="attention_prep",
+    )(packed, g_attn.reshape(1, -1), g_q.reshape(1, -1), g_kv.reshape(1, -1), cos_w, sin_w, h_one)
+
+
+def post_kernel(starts, packed, gain_ref, wr_ref, wsi_ref, wso_ref, att_ref, h_ref, u_ref, s_ref, o_ref, w_out, sems):
+    first = pl.program_id(0) == 0
+
+    @pl.when(first)
+    def _():
+        load_weights(packed, starts, (w_out,), (sems.at[0],))
+        await_weights(w_out, sems.at[0])
+
+    count, width = h_ref.shape
+    pieces = width // LANES
+    attn = mm(att_ref[...], w_out[...]).astype(jnp.bfloat16)
+    h_two = (h_ref[...].astype(jnp.float32) + attn.astype(jnp.float32)).astype(jnp.bfloat16).astype(jnp.float32)
+    rows = rms_rows(h_two, gain_ref[...])
+    u_ref[...] = rows
+    terms = lax.dot_general(rows, wr_ref[...], (((1,), (1,)), ((), ())), preferred_element_type=jnp.float32)
+    logits = terms[:, :LANES] + pltpu.roll(terms[:, :LANES], LANES // 2, 1) + terms[:, LANES:]
+    s_ref[...] = jax.nn.sigmoid(logits)
+    inner = wso_ref.shape[0]
+    hidden = (jax.nn.silu(mm(rows, wsi_ref[:, :inner])) * mm(rows, wsi_ref[:, inner:])).astype(jnp.bfloat16)
+    shared = mm(hidden, wso_ref[...]).astype(jnp.bfloat16)
+    total = h_two + shared.astype(jnp.float32)
+    for j in range(pieces):
+        o_ref[pl.ds(j, count, stride=pieces), :] = total[:, j * LANES : (j + 1) * LANES]
+
+
+def attention_post(packed, starts, attended, h_one, gain, wr, ws_in, ws_out):
+    tokens, width = h_one.shape
+    pieces = width // LANES
+    whole = lambda arr: pl.BlockSpec(arr.shape, lambda i: (0, 0))
+    rows = lambda n: pl.BlockSpec((POST_ROWS, n), lambda i: (i, 0))
+    return pl.pallas_call(
+        functools.partial(post_kernel, starts),
+        grid=(tokens // POST_ROWS,),
+        in_specs=[pl.BlockSpec(memory_space=pl.ANY), pl.BlockSpec((1, width), lambda i: (0, 0)), whole(wr), whole(ws_in), whole(ws_out), rows(width), rows(width)],
+        out_specs=[rows(width), rows(LANES), pl.BlockSpec((POST_ROWS * pieces, LANES), lambda i: (i, 0))],
+        out_shape=[
+            jax.ShapeDtypeStruct((tokens, width), jnp.bfloat16),
+            jax.ShapeDtypeStruct((tokens, LANES), jnp.float32),
+            jax.ShapeDtypeStruct((tokens * pieces, LANES), jnp.float32),
+        ],
+        scratch_shapes=[pltpu.VMEM((attended.shape[1], width), jnp.bfloat16), pltpu.SemaphoreType.DMA((1,))],
+        compiler_params=pltpu.CompilerParams(vmem_limit_bytes=VMEM_LIMIT),
+        cost_estimate=pl.CostEstimate(flops=2 * tokens * width * (width + 1024), bytes_accessed=10 * tokens * width, transcendentals=0),
+        name="attention_post",
+    )(packed, gain.reshape(1, width), wr, ws_in, ws_out, attended, h_one)
+
+
+def moe_kernel(last, arrays, meta_ref, rank_ref, gate_ref, tab_hbm, u_hbm, a_hbm, *refs):
     w_hbms, refs = refs[:arrays], refs[arrays:]
     o_hbm, u_vm, acc, wbuf, *refs = refs
     x_bufs, o_bufs, h_bufs = refs[0:2], refs[2:4], refs[4:6]
     t_next, t_prev, s_prev = refs[6 : 6 + RING], refs[6 + RING : 6 + 2 * RING], refs[6 + 2 * RING : 6 + 3 * RING]
-    st_a, st_b, wsem, sem_a, sem_b, asem, lsem = refs[6 + 3 * RING :]
+    stage, wsem, ssem, asem, lsem = refs[6 + 3 * RING :]
     tokens, width = u_hbm.shape
     pieces = width // LANES
     inter = w_hbms[0].shape[2]
@@ -165,46 +285,27 @@
     def _():
         w_start(0)
 
-    if not first:
-        acc_in = pltpu.make_async_copy(a_hbm, acc.at[pl.ds(0, tokens * pieces), :], asem)
-        acc_in.start()
-
-    def spread(dst, base, block):
-        for j in range(pieces):
-            dst[pl.ds(base * pieces + j, TILE, stride=pieces), :] = block[:, j * LANES : (j + 1) * LANES]
-
-    def load_rows(src, stage, sem, step):
-        return pltpu.make_async_copy(src.at[pl.ds(step * TILE, TILE), :], stage.at[lax.rem(step, 2)], sem.at[lax.rem(step, 2)])
-
-    load_rows(u_hbm, st_a, sem_a, 0).start()
+    def row_copy(step):
+        slot = lax.rem(step, STAGES)
+        return pltpu.make_async_copy(u_hbm.at[pl.ds(step * TILE, TILE), :], stage.at[slot], ssem.at[slot])
+
+    for step in range(min(STAGES - 1, blocks)):
+        row_copy(step).start()
+    acc_in = pltpu.make_async_copy(a_hbm, acc.at[pl.ds(0, tokens * pieces), :], asem)
+    acc_in.start()
 
     @pl.loop(0, blocks)
     def _(step):
-        @pl.when(step + 1 < blocks)
+        @pl.when(step + STAGES - 1 < blocks)
         def _():
-            load_rows(u_hbm, st_a, sem_a, step + 1).start()
-
-        load_rows(u_hbm, st_a, sem_a, step).wait()
-        spread(u_vm, step * TILE, st_a[lax.rem(step, 2)].astype(jnp.float32))
+            row_copy(step + STAGES - 1).start()
+
+        row_copy(step).wait()
+        block = stage[lax.rem(step, STAGES)].astype(jnp.float32)
+        for j in range(pieces):
+            u_vm[pl.ds(step * TILE * pieces + j, TILE, stride=pieces), :] = block[:, j * LANES : (j + 1) * LANES]
 
     u_vm[pl.ds(tokens * pieces, 8), :] = jnp.zeros((8, LANES), jnp.float32)
-    if first:
-        load_rows(h_hbm, st_a, sem_a, 0).start()
-        load_rows(s_hbm, st_b, sem_b, 0).start()
-
-        @pl.loop(0, blocks)
-        def _(step):
-            @pl.when(step + 1 < blocks)
-            def _():
-                load_rows(h_hbm, st_a, sem_a, step + 1).start()
-                load_rows(s_hbm, st_b, sem_b, step + 1).start()
-
-            load_rows(h_hbm, st_a, sem_a, step).wait()
-            load_rows(s_hbm, st_b, sem_b, step).wait()
-            slot = lax.rem(step, 2)
-            spread(acc, step * TILE, st_a[slot].astype(jnp.float32) + st_b[slot].astype(jnp.float32))
-    else:
-        acc_in.wait()
     acc[pl.ds(tokens * pieces, 8), :] = jnp.zeros((8, LANES), jnp.float32)
 
     idle = tab_hbm.shape[0] - 1
@@ -298,6 +399,7 @@
         x_bufs[0][pl.ds(r, pieces, stride=PITCH), :] = u_vm[row_at(t_next[RING - 1][r]), :]
 
     rounds = (count + RING + 1) // RING
+    acc_in.wait()
 
     @pl.loop(0, rounds)
     def _(i):
@@ -311,27 +413,28 @@
     if last:
 
         def store_rows(step):
-            return pltpu.make_async_copy(st_a.at[lax.rem(step, 2)], o_hbm.at[pl.ds(step * TILE, TILE), :], sem_a.at[lax.rem(step, 2)])
+            slot = lax.rem(step, STAGES)
+            return pltpu.make_async_copy(stage.at[slot], o_hbm.at[pl.ds(step * TILE, TILE), :], ssem.at[slot])
 
         @pl.loop(0, blocks)
         def _(step):
-            @pl.when(step >= 2)
+            @pl.when(step >= STAGES)
             def _():
-                store_rows(step - 2).wait()
+                store_rows(step - STAGES).wait()
 
             parts = [acc[pl.ds(step * TILE * pieces + j, TILE, stride=pieces), :].astype(jnp.bfloat16) for j in range(pieces)]
-            st_a[lax.rem(step, 2)] = jnp.concatenate(parts, axis=1)
+            stage[lax.rem(step, STAGES)] = jnp.concatenate(parts, axis=1)
             store_rows(step).start()
 
-        store_rows(blocks - 2).wait()
-        store_rows(blocks - 1).wait()
+        for step in range(blocks - min(STAGES, blocks), blocks):
+            store_rows(step).wait()
     else:
         acc_out = pltpu.make_async_copy(acc.at[pl.ds(0, tokens * pieces), :], o_hbm, asem)
         acc_out.start()
         acc_out.wait()
 
 
-def moe_call(first, last, meta, table, ranks, gates, u_norm, extra, weights):
+def moe_call(last, meta, table, ranks, gates, u_norm, total, weights):
     tokens, width = u_norm.shape
     pieces = width // LANES
     experts = sum(w.shape[0] for w in weights)
@@ -345,26 +448,24 @@
         *[pltpu.VMEM((pieces * PITCH, LANES), jnp.float32)] * 4,
         *[pltpu.VMEM((TILE, inter), jnp.bfloat16)] * 2,
         *[pltpu.SMEM((TILE,), jnp.int32)] * (3 * RING),
-        pltpu.VMEM((2, TILE, width), jnp.bfloat16),
-        pltpu.VMEM((2, TILE, width), jnp.bfloat16),
+        pltpu.VMEM((STAGES, TILE, width), jnp.bfloat16),
         pltpu.SemaphoreType.DMA((3,)),
-        pltpu.SemaphoreType.DMA((2,)),
-        pltpu.SemaphoreType.DMA((2,)),
+        pltpu.SemaphoreType.DMA((STAGES,)),
         pltpu.SemaphoreType.DMA,
         pltpu.SemaphoreType.DMA((RING, 3)),
     ]
     out_shape = jax.ShapeDtypeStruct((tokens, width), jnp.bfloat16) if last else jax.ShapeDtypeStruct((tokens * pieces, LANES), jnp.float32)
     rows = experts * tokens // 8
     return pl.pallas_call(
-        functools.partial(moe_kernel, first, last, len(weights)),
-        in_specs=[smem] * 3 + [hbm] * (2 + len(extra) + len(weights)),
+        functools.partial(moe_kernel, last, len(weights)),
+        in_specs=[smem] * 3 + [hbm] * (3 + len(weights)),
         out_specs=hbm,
         out_shape=out_shape,
         scratch_shapes=scratch,
         compiler_params=pltpu.CompilerParams(vmem_limit_bytes=VMEM_LIMIT),
         cost_estimate=pl.CostEstimate(flops=2 * rows * wrows * inter, bytes_accessed=2 * experts * wrows * inter, transcendentals=0),
         name="routed_experts",
-    )(meta, ranks, gates, table, u_norm, *extra, *weights)
+    )(meta, ranks, gates, table, u_norm, total, *weights)
 
 
 def route_plan(choice_ids, num_experts, groups, here):
@@ -445,55 +546,67 @@
 
         gains = [g_mlp, g_attn, g_q, g_kv, g_moe]
         sizes = [g.shape[0] for g in gains]
-        packed = lax.all_gather(jnp.concatenate(gains), AXIS, axis=0, tiled=False)
+        here = lax.axis_index(AXIS)
+        vectors = jnp.concatenate(gains)[None]
+        bit = 1
+        while bit < groups:
+            other = lax.ppermute(vectors, AXIS, [(i, i ^ bit) for i in range(groups)])
+            mine_first = (here & bit) == 0
+            vectors = jnp.where(mine_first, jnp.concatenate([vectors, other]), jnp.concatenate([other, vectors]))
+            bit *= 2
         offs = [sum(sizes[:i]) for i in range(len(sizes))]
-        g_mlp, g_attn, g_q, g_kv, g_moe = [packed[:, o : o + s].reshape(-1) for o, s in zip(offs, sizes)]
+        g_mlp, g_attn, g_q, g_kv, g_moe = [vectors[:, o : o + s].reshape(-1) for o, s in zip(offs, sizes)]
 
         inner = w_gate.shape[1]
-        gate_up = gather(jnp.concatenate([w_gate, w_up], axis=1))
+        dense_w = gather(jnp.concatenate([to_blocks(jnp.concatenate([w_gate, w_up], axis=1), DENSE_LANES), to_blocks(w_down, DENSE_LANES)])[None])
+        dense_at = (0, 2 * inner // DENSE_LANES * w_gate.shape[0])
         kv_rank = w_uk.shape[0] * groups
         rope_dim = w_dkv.shape[1] - kv_rank
-        heads = (w_uq.shape[1] - w_uk.shape[1]) // rope_dim
-        nope_dim = w_uk.shape[1] // heads
+        nope = w_uk.shape[1]
+        heads = (w_uq.shape[1] - nope) // rope_dim
+        nope_dim = nope // heads
         per_head = w_uq.reshape(w_uq.shape[0], heads, nope_dim + rope_dim)
-        uq_local = jnp.concatenate([per_head[:, :, :nope_dim].reshape(-1, heads * nope_dim), per_head[:, :, nope_dim:].reshape(-1, heads * rope_dim)], axis=1)
-        dkv_local = jnp.concatenate([w_dkv, swap_halves(w_dkv[:, kv_rank:], rope_dim // 2)], axis=1)
-        shards = [w_down, w_dq, dkv_local, uq_local, w_uk, w_uv, w_out]
-        blocks = [to_blocks(s) for s in shards]
+        uq_local = jnp.concatenate([per_head[:, :, :nope_dim].reshape(-1, nope), per_head[:, :, nope_dim:].reshape(-1, heads * rope_dim)], axis=1)
+        shards = [jnp.concatenate([w_dq, w_dkv, w_dkv[:, kv_rank:]], axis=1), uq_local, w_uk, w_uv, w_out]
+        blocks = [to_blocks(s, ATTN_LANES) for s in shards]
         attn_w = gather(jnp.concatenate(blocks, axis=0)[None])
-        starts = [sum(b.shape[0] for b in blocks[:i]) for i in range(len(blocks))]
-        down, w_dq, w_dkv, w_uq, w_uk, w_uv, w_out = [from_blocks(attn_w, st, s.shape[0], s.shape[1]) for st, s in zip(starts, shards)]
+        attn_at = tuple(sum(b.shape[0] for b in blocks[:i]) for i in range(len(blocks)))
 
         down_blocks = we_down.reshape(we_down.shape[0], inter, width // inter, inter).transpose(0, 2, 1, 3).reshape(we_down.shape[0], width, inter)
         pack = jnp.concatenate([we_gate, we_up, down_blocks], axis=1)
         table, ranks, metas = route_plan(choice_ids, num_experts, groups, lax.axis_index(AXIS))
 
-        normed = rms_norm(flat_x, g_mlp)
-        hidden = (jax.nn.silu(mm(normed, gate_up[:, :inner])) * mm(normed, gate_up[:, inner:])).astype(jnp.bfloat16)
-        mlp_out = mm(hidden, down).astype(jnp.bfloat16)
-        h_one = (flat_x.astype(jnp.float32) + mlp_out.astype(jnp.float32)).astype(jnp.bfloat16)
+        h_one = dense_layer(dense_w, dense_at, flat_x, g_mlp, inner)
         expert_w = []
         low = 0
         for way, size in PLAN:
             part = pack[low : low + size]
-            expert_w.append(spread_pair(part, gate_up, h_one) if way == "P" else (gather(part),))
+            expert_w.append(spread_pair(part, dense_w, h_one) if way == "P" else (gather(part),))
             low += size
 
-        attn_out = attention(rms_norm(h_one, g_attn), w_dq, g_q, w_uq, w_dkv, g_kv, w_uk, w_uv, w_out, seq_len, rope_dim)
-        h_two = (h_one.astype(jnp.float32) + attn_out.astype(jnp.float32)).astype(jnp.bfloat16)
-        u_norm = rms_norm(h_two, g_moe)
-        logits = jnp.einsum("td,ed->te", u_norm.astype(jnp.float32), w_router, precision=lax.Precision.HIGHEST)
-        scores = jax.nn.sigmoid(logits)
+        positions = jnp.arange(seq_len)
+        inv_freq = 1.0 / (ROPE_BASE ** (jnp.arange(0, rope_dim, 2).astype(jnp.float32) / rope_dim))
+        angles = positions.astype(jnp.float32)[:, None] * inv_freq[None, :]
+        cos_t, sin_t = jnp.cos(angles), jnp.sin(angles)
+        cos_w = jnp.concatenate([cos_t] * 4, axis=1)
+        sin_w = jnp.concatenate([-sin_t, sin_t] * 2, axis=1)
+        queries_keys = attention_prep(attn_w, attn_at[:4], h_one, g_attn, g_q, g_kv, cos_w, sin_w, nope, heads * rope_dim)
+        attended = attention_core(*queries_keys, seq_len, (nope_dim + rope_dim) ** -0.5)
+
+        terms, rest = [], w_router
+        for _ in range(3):
+            terms.append(lax.reduce_precision(rest, 8, 7))
+            rest = rest - terms[-1]
+        terms.append(jnp.zeros_like(rest))
+        wr = jnp.concatenate(terms).astype(jnp.bfloat16)
+        u_norm, scores, total = attention_post(attn_w, attn_at[4:], attended, h_one, g_moe, wr, jnp.concatenate([ws_gate, ws_up], axis=1), ws_down)
+        scores = scores[:, :num_experts]
         hits = choice_ids[:, :, None] == jnp.arange(num_experts)[None, None, :]
         picked = jnp.sum(jnp.where(hits, scores[:, None, :], 0.0), axis=2)
         gates = (ROUTE_SCALE * picked / jnp.sum(picked, axis=1, keepdims=True)).reshape(-1)
         gates = jnp.concatenate([gates, jnp.zeros((8,), jnp.float32)])
-        shared = swiglu(u_norm, ws_gate, ws_up, ws_down)
-
-        total = None
         for i, weights in enumerate(expert_w):
-            extra = (h_two, shared) if i == 0 else (total,)
-            total = moe_call(i == 0, i == len(expert_w) - 1, metas[i], table, ranks, gates, u_norm, extra, weights)
+            total = moe_call(i == len(expert_w) - 1, metas[i], table, ranks, gates, u_norm, total, weights)
         return total.reshape(num_seqs, seq_len, width)
 
     return jax.shard_map(local, mesh=mesh, in_specs=in_specs, out_specs=cube_spec, check_vma=False)

time: 796 us -> 669 us (0.84)
  the two profiles are of different devices: /device:TPU:0 before, /device:TPU:1 now
where the time goes in v4:
time: 669 us; the launch traced here: 661 us
  Pallas kernels  484 us (72%)
  waiting for transfers between devices  52.5 us (8%)
  other arithmetic  50.2 us (8%)
  local copies, waits for them, and re-layouts  47.6 us (7%)
  between operations  14.1 us (2%)
  starting transfers between devices  12.3 us (2%)
    pallas_call x4, Pallas kernels, moe_call(): pl.pallas_call(functools.partial(moe_kernel, last, len(weights)), in_spec...  259 us
    pallas_call x1, Pallas kernels, dense_layer(): pl.pallas_call(functools.partial(dense_kernel, starts), grid=(tokens // D...  84.8 us
    pallas_call x1, Pallas kernels, attention_core(): pl.pallas_call(functools.partial(attn_kernel, scale, 256), grid=(seqs, he...  76.8 us
    pallas_call x1, Pallas kernels, attention_post(): pl.pallas_call(functools.partial(post_kernel, starts), grid=(tokens // PO...  31.9 us
    pallas_call x1, Pallas kernels, attention_prep(): pl.pallas_call(functools.partial(prep_kernel, starts), grid=(tokens // PR...  31.4 us
    ppermute x9, waiting for transfers between devices, send(): return lax.ppermute(vals, AXIS, [(i, i ^ bit) for i in range(count)])  30.8 us
    all_gather x5, waiting for transfers between devices, gather(): return lax.all_gather(shard, AXIS, axis=0, tiled=True)  19.8 us
    concatenate x1, other arithmetic, local(): pack = jnp.concatenate([we_gate, we_up, down_blocks], axis=1)  16.2 us
  transfers between devices with their start and end apart: 17, of which 5 were waited for; matrix products, arithmetic and copies ran while one was open for 12% of the time, Pallas kernels for 67%

profile of v4, /device:TPU:1, one launch (start us, length us, event | category | flops | bytes accessed | tf_op | source)
XLA Modules:
  0.0 660.8 jit_solution(10453484423611388718)
XLA Ops:
  6.5 2.0 copy.129
  8.6 1.5 copy.115
  10.0 1.5 copy.114
  11.6 0.7 copy.116
  12.4 2.7 pad_maximum_fusion.1
  16.6 0.9 copy-done.6
  17.6 2.9 copy.128
  21.0 3.3 copy-done.3
  24.3 16.2 %pad_maximum_fusion = bf16[8,3072,256]{2,1,0:T(8,128)(2,1)S(1)} fusion(bf16[8,1024,256]{2,1,0:T(8,128)(2,1)S(1)} %bitcast.60, bf16[8,1024,256]{2,1,0:T(8,128)(2,1)S(1)} %copy-done.2, bf16[8,1024,256]{2,1,0:T(8,128)(2,1)S(1)} %copy-done.3), kind=kLoop, calls=%fused_computation | loop fusion | flops 37748736 | bytes 25165824 | tf_op jit(solution)/shard_map/concatenate | solution.py:576
  40.6 4.5 copy-done
  45.1 2.5 slice.87
  47.7 6.2 fusion.17
  54.0 3.1 pad_maximum_fusion.2
  57.4 0.9 convert_reduce_fusion
  58.4 0.6 copy.106
  59.1 0.8 select_reduce_fusion.6
  60.2 0.7 copy.123
  60.9 2.9 iota_add_fusion
  63.8 2.8 add.252
  66.6 1.0 reshape.346
  67.9 0.9 pad_add_fusion.1
  68.8 9.2 %sort.8 = s32[49152]{0:T(1024)S(1)} sort(s32[49152]{0:T(1024)S(1)} %pad_add_fusion.1), dimensions={0}, to_apply=%region_6.7 | sort | flops 786432 | bytes 393216 | tf_op jit(solution)/shard_map/jit(sort)/sort | solution.py:488
  78.3 0.8 select_reduce_fusion.4
  79.1 0.8 select_reduce_fusion.2
  80.0 1.0 pad_maximum_fusion.4.wsi_ref
  81.1 0.6 slice_bitcast_fusion
  81.7 1.0 reduce-precision_convert_fusion.1
  82.7 1.0 maximum_maximum_fusion.wr_ref
  83.7 2.1 fusion.2
  85.8 1.8 pad_maximum_fusion.5
  87.6 0.8 maximum_select_fusion.2
  88.4 4.1 collective-permute-start.1
  92.5 1.0 pad_add_fusion.tab_hbm
  93.5 0.6 collective-permute-done.1
  94.1 1.4 collective-permute-start.2
  95.5 0.6 select_reduce_fusion.3.rank_ref
  96.1 1.2 collective-permute-done.2
  97.4 0.7 reshape_reshape.17.gq_ref
  98.1 0.7 reshape_reshape.18.gkv_ref
  98.8 0.7 fusion.18
  99.4 4.6 all-gather.16.cloned.1.call-done
  104.3 1.2 collective-permute-start.4
  105.8 84.8 %dense_layer.1.h_ref = bf16[4096,1024]{1,0:T(8,128)(2,1)} custom-call(bf16[8,2112,512]{2,1,0:T(8,128)(2,1)} %bitcast.93, f32[1,1024]{1,0:T(1,128)} %bitcast.89, bf16[4096,1024]{1,0:T(8,128)(2,1)} %bitcast.94), custom_call_target="tpu_custom_call" | custom-call | flops 70866960384 | bytes 34078720 | tf_op jit(solution)/shard_map/dense_layer/pallas_call | solution.py:88
  190.6 31.4 %attention_prep.1 = (bf16[4096,1024]{1,0:T(8,128)(2,1)}, bf16[4096,512]{1,0:T(8,128)(2,1)}, bf16[4096,1024]{1,0:T(8,128)(2,1)}, bf16[4096,256]{1,0:T(8,128)(2,1)}, bf16[4096,1024]{1,0:T(8,128)(2,1)}) custom-call(bf16[8,1440,256]{2,1,0:T(8,128)(2,1)} %bitcast.95, f32[1,1024]{1,0:T(1,128)} %bitcast.88, f32[1,384]{1,0:T(1,128)} %reshape_reshape.17.gq_ref, ...), custom_call_target="tpu_custom_call" | custom-call | flops 15569256448 | bytes 50331648 | tf_op jit(solution)/shard_map/attention_prep/pallas_call | solution.py:189
  222.0 76.8 %attention_core.1.att_ref = bf16[4096,1024]{1,0:T(8,128)(2,1)} custom-call(bf16[4096,1024]{1,0:T(8,128)(2,1)} %get-tuple-element.16.qn_ref, bf16[4096,512]{1,0:T(8,128)(2,1)} %get-tuple-element.17.qr_ref, bf16[4096,1024]{1,0:T(8,128)(2,1)} %get-tuple-element.18.kn_ref, bf16[4096,256]{1,0:T(8,128)(2,1)} %get-tuple-element.19.kr_ref, ...), custom_call_target="tpu_custom_call" | custom-call | flops 17179869184 | bytes 41943040 | tf_op jit(solution)/shard_map/attention_core/pallas_call | solution.py:126
  298.8 0.8 collective-permute-start.6
  299.6 2.7 slice.76
  302.3 2.7 slice.77
  305.0 1.2 collective-permute-start.8
  306.5 31.9 %attention_post.1 = (bf16[4096,1024]{1,0:T(8,128)(2,1)}, f32[4096,128]{1,0:T(8,128)}, f32[32768,128]{1,0:T(8,128)}) custom-call(bf16[8,1440,256]{2,1,0:T(8,128)(2,1)} %bitcast.96, f32[1,1024]{1,0:T(1,128)} %bitcast.87, bf16[256,1024]{1,0:T(8,128)(2,1)} %maximum_maximum_fusion.wr_ref, bf16[1024,512]{1,0:T(8,128)(2,1)} %pad_maximum_fusion.4.wsi_ref, ...), custom_call_target="tpu_custom_call" | custom-call | flops 17179869184 | bytes 41943040 | tf_op jit(solution)/shard_map/attention_post/pallas_call | solution.py:238
  338.4 2.2 copy.118
  340.6 1.6 select_reduce_fusion
  342.2 0.6 copy.119
  342.8 1.0 div.98
  343.8 0.7 concatenate.79.gate_ref
  344.5 30.8 %collective-permute-done.8.refs_6_ = bf16[1,3072,256]{2,1,0:T(8,128)(2,1)} collective-permute-done((bf16[1,3072,256]{2,1,0:T(8,128)(2,1)}, bf16[1,3072,256]{2,1,0:T(8,128)(2,1)}, u32[]{:S(2)}, u32[]{:S(2)}) %collective-permute-start.8) | collective-permute-done | bytes 1572896 | tf_op jit(solution)/shard_map/ppermute | solution.py:518
  375.3 1.2 collective-permute-start.10
  376.5 1.4 collective-permute-start.11
  377.9 15.1 %all-gather.8.cloned.1.call-done.refs_0_ = bf16[24,3072,256]{2,1,0:T(8,128)(2,1)} async-done(((bf16[3,3072,256]{2,1,0:T(8,128)(2,1)}), bf16[24,3072,256]{2,1,0:T(8,128)(2,1)}) %all-gather.8.cloned.1.call-update) | async-done | bytes 37748752 | tf_op jit(solution)/shard_map/all_gather | solution.py:537
  393.0 84.2 %routed_experts.4.a_hbm = f32[32768,128]{1,0:T(8,128)} custom-call(s32[67]{0:T(128)} %get-tuple-element.46.meta_ref, s32[192]{0:T(256)} %select_reduce_fusion.3.rank_ref, f32[32776]{0:T(1024)} %concatenate.79.gate_ref, s32[192,2,256]{2,1,0:T(2,128)} %pad_add_fusion.tab_hbm, bf16[4096,1024]{1,0:T(8,128)(2,1)} %get-tuple-element.22.u_hbm, ...), custom_call_target="tpu_custom_call" | custom-call | flops 19327352832 | bytes 37748736 | tf_op jit(solution)/shard_map/routed_experts/pallas_call | solution.py:459
  477.3 1.1 copy-done.4
  478.9 70.3 %routed_experts.5.a_hbm = f32[32768,128]{1,0:T(8,128)} custom-call(s32[67]{0:T(128)} %get-tuple-element.47.meta_ref, s32[192]{0:T(256)} %select_reduce_fusion.3.rank_ref, f32[32776]{0:T(1024)} %concatenate.79.gate_ref, s32[192,2,256]{2,1,0:T(2,128)} %pad_add_fusion.tab_hbm, bf16[4096,1024]{1,0:T(8,128)(2,1)} %get-tuple-element.22.u_hbm, ...), custom_call_target="tpu_custom_call" | custom-call | flops 12884901888 | bytes 25165824 | tf_op jit(solution)/shard_map/routed_experts/pallas_call | solution.py:459
  549.2 63.4 %routed_experts.6.a_hbm = f32[32768,128]{1,0:T(8,128)} custom-call(s32[67]{0:T(128)} %get-tuple-element.48.meta_ref, s32[192]{0:T(256)} %select_reduce_fusion.3.rank_ref, f32[32776]{0:T(1024)} %concatenate.79.gate_ref, s32[192,2,256]{2,1,0:T(2,128)} %pad_add_fusion.tab_hbm, bf16[4096,1024]{1,0:T(8,128)(2,1)} %get-tuple-element.22.u_hbm, ...), custom_call_target="tpu_custom_call" | custom-call | flops 12884901888 | bytes 25165824 | tf_op jit(solution)/shard_map/routed_experts/pallas_call | solution.py:459
  612.6 41.4 %routed_experts.7 = bf16[4096,1024]{1,0:T(8,128)(2,1)} custom-call(s32[67]{0:T(128)} %get-tuple-element.49.meta_ref, s32[192]{0:T(256)} %select_reduce_fusion.3.rank_ref, f32[32776]{0:T(1024)} %concatenate.79.gate_ref, s32[192,2,256]{2,1,0:T(2,128)} %pad_add_fusion.tab_hbm, bf16[4096,1024]{1,0:T(8,128)(2,1)} %get-tuple-element.22.u_hbm, ...), custom_call_target="tpu_custom_call" | custom-call | flops 6442450944 | bytes 12582912 | tf_op jit(solution)/shard_map/routed_experts/pallas_call | solution.py:459
  (124 shorter events, 5.2 us)
Async XLA Ops:
  6.5 97.5 %all-gather.16.cloned.1.call-start = ((), (), s32[]{:S(2)}) async-start(), calls=%async_computation.4 | async-start | bytes 19464192 | tf_op jit(solution)/shard_map/all_gather | solution.py:537
  11.6 3.6 copy-start.11
  12.3 3.1 copy-start.13
  12.3 3.2 copy-start.12
  12.3 3.2 slice-start
  12.3 3.8 copy-start.14
  12.3 3.9 copy-start.15
  12.3 3.9 copy-start.10
  15.1 175.5 %all-gather.14.cloned.1.call-start = ((), (), s32[]{:S(2)}) async-start(), calls=%async_computation.3 | async-start | bytes 6635520 | tf_op jit(solution)/shard_map/all_gather | solution.py:537
  16.6 0.9 copy-start.6
  17.5 375.4 %all-gather.8.cloned.1.call-start = ((), (), s32[]{:S(2)}) async-start(), calls=%async_computation | async-start | bytes 42467328 | tf_op jit(solution)/shard_map/all_gather | solution.py:537
  17.6 3.5 copy-start.2
  17.6 6.7 %copy-start.3 = (bf16[8,1024,256]{2,1,0:T(8,128)(2,1)S(1)}, bf16[8,1024,256]{2,1,0:T(8,128)(2,1)}, u32[]{:S(2)}) copy-start(bf16[8,1024,256]{2,1,0:T(8,128)(2,1)} %param.41) | copy-start | bytes 12582916
  20.5 20.1 %copy-start.1 = (bf16[8,32,4,8,256]{4,3,1,2,0:T(8,128)(2,1)}, bf16[8,32,4,8,256]{4,3,1,2,0:T(8,128)(2,1)S(1)}, u32[]{:S(2)}) copy-start(bf16[8,32,4,8,256]{4,3,1,2,0:T(8,128)(2,1)S(1)} %copy.128) | copy-start | bytes 12582916
  40.6 4.5 copy-start
  47.5 6.3 copy-start.17
  47.6 6.3 copy-start.18
  47.6 6.3 copy-start.19
  47.6 6.3 copy-start.20
  47.6 6.3 copy-start.21
  47.6 501.6 %all-gather.10.cloned.1.call-start = ((), (), s32[]{:S(2)}) async-start(), calls=%async_computation.1 | async-start | bytes 28311552 | tf_op jit(solution)/shard_map/all_gather | solution.py:537
  53.8 558.8 %all-gather.12.cloned.1.call-start = ((), (), s32[]{:S(2)}) async-start(), calls=%async_computation.2 | async-start | bytes 14155776 | tf_op jit(solution)/shard_map/all_gather | solution.py:537
  54.0 3.2 copy-start.7
  54.0 33.6 %collective-permute-start = (f32[1,464]{1,0:T(1,128)S(1)}, f32[1,464]{1,0:T(1,128)}, u32[]{:S(2)}, u32[]{:S(2)}) collective-permute-start(f32[1,464]{1,0:T(1,128)S(1)} %bitcast.85), channel_id=1, source_target_pairs={{0,1},{1,0},{2,3},{3,2},{4,5},{5,4},{6,7},{7,6}} | collective-permute-start | bytes 5576 | tf_op jit(solution)/shard_map/ppermute | solution.py:553
  57.1 1.9 copy-start.22
  57.1 1.9 copy-start.23
  57.1 1.9 copy-start.24
  58.4 1.5 copy-start.16
  59.0 21.0 %copy-start.8 = (bf16[1024,256]{1,0:T(8,128)(2,1)S(1)}, bf16[1024,256]{1,0:T(8,128)(2,1)}, u32[]{:S(2)}) copy-start(bf16[1024,256]{1,0:T(8,128)(2,1)} %param.45) | copy-start | bytes 1572868
  59.0 21.0 %copy-start.9 = (bf16[1024,256]{1,0:T(8,128)(2,1)S(1)}, bf16[1024,256]{1,0:T(8,128)(2,1)}, u32[]{:S(2)}) copy-start(bf16[1024,256]{1,0:T(8,128)(2,1)} %param.44) | copy-start | bytes 1572868
  88.4 5.7 collective-permute-start.1
  94.1 3.2 collective-permute-start.2
  104.1 373.1 %collective-permute-start.3 = (bf16[2,3072,256]{2,1,0:T(8,128)(2,1)}, bf16[2,3072,256]{2,1,0:T(8,128)(2,1)}, u32[]{:S(2)}, u32[]{:S(2)}) collective-permute-start(bf16[2,3072,256]{2,1,0:T(8,128)(2,1)} %get-tuple-element.24.refs_0_), channel_id=1, source_target_pairs={{0,1},{1,0},{2,3},{3,2},{4,5},{5,4},{6,7},{7,6}} | collective-permute-start | bytes 9437192 | tf_op jit(solution)/shard_map/ppermute | solution.py:518
  104.3 194.5 %collective-permute-start.4 = (bf16[2,3072,256]{2,1,0:T(8,128)(2,1)}, bf16[2,3072,256]{2,1,0:T(8,128)(2,1)}, u32[]{:S(2)}, u32[]{:S(2)}) collective-permute-start(bf16[2,3072,256]{2,1,0:T(8,128)(2,1)} %get-tuple-element.24.refs_0_), channel_id=1, source_target_pairs={{0,2},{1,3},{2,0},{3,1},{4,6},{5,7},{6,4},{7,5}} | collective-permute-start | bytes 9437192 | tf_op jit(solution)/shard_map/ppermute | solution.py:518
  105.5 193.3 %collective-permute-start.5 = (bf16[2,3072,256]{2,1,0:T(8,128)(2,1)}, bf16[2,3072,256]{2,1,0:T(8,128)(2,1)}, u32[]{:S(2)}, u32[]{:S(2)}) collective-permute-start(bf16[2,3072,256]{2,1,0:T(8,128)(2,1)} %get-tuple-element.24.refs_0_), channel_id=1, source_target_pairs={{0,4},{1,5},{2,6},{3,7},{4,0},{5,1},{6,2},{7,3}} | collective-permute-start | bytes 9437192 | tf_op jit(solution)/shard_map/ppermute | solution.py:518
  298.8 178.4 %collective-permute-start.6 = (bf16[2,3072,256]{2,1,0:T(8,128)(2,1)}, bf16[2,3072,256]{2,1,0:T(8,128)(2,1)}, u32[]{:S(2)}, u32[]{:S(2)}) collective-permute-start(bf16[2,3072,256]{2,1,0:T(8,128)(2,1)} %collective-permute-done.4.refs_2_), channel_id=1, source_target_pairs={{0,1},{1,0},{2,3},{3,2},{4,5},{5,4},{6,7},{7,6}} | collective-permute-start | bytes 9437192 | tf_op jit(solution)/shard_map/ppermute | solution.py:518
  302.3 174.9 %collective-permute-start.7 = (bf16[2,3072,256]{2,1,0:T(8,128)(2,1)}, bf16[2,3072,256]{2,1,0:T(8,128)(2,1)}, u32[]{:S(2)}, u32[]{:S(2)}) collective-permute-start(bf16[2,3072,256]{2,1,0:T(8,128)(2,1)} %collective-permute-done.5.refs_4_), channel_id=1, source_target_pairs={{0,1},{1,0},{2,3},{3,2},{4,5},{5,4},{6,7},{7,6}} | collective-permute-start | bytes 9437192 | tf_op jit(solution)/shard_map/ppermute | solution.py:518
  305.0 70.3 %collective-permute-start.8 = (bf16[1,3072,256]{2,1,0:T(8,128)(2,1)}, bf16[1,3072,256]{2,1,0:T(8,128)(2,1)}, u32[]{:S(2)}, u32[]{:S(2)}) collective-permute-start(bf16[1,3072,256]{2,1,0:T(8,128)(2,1)} %slice.76), channel_id=1, source_target_pairs={{0,4},{1,5},{2,6},{3,7},{4,0},{5,1},{6,2},{7,3}} | collective-permute-start | bytes 4718600 | tf_op jit(solution)/shard_map/ppermute | solution.py:518
  306.2 70.3 %collective-permute-start.9 = (bf16[1,3072,256]{2,1,0:T(8,128)(2,1)}, bf16[1,3072,256]{2,1,0:T(8,128)(2,1)}, u32[]{:S(2)}, u32[]{:S(2)}) collective-permute-start(bf16[1,3072,256]{2,1,0:T(8,128)(2,1)} %slice.77), channel_id=1, source_target_pairs={{0,2},{1,3},{2,0},{3,1},{4,6},{5,7},{6,4},{7,5}} | collective-permute-start | bytes 4718600 | tf_op jit(solution)/shard_map/ppermute | solution.py:518
  375.3 101.9 %collective-permute-start.10 = (bf16[1,3072,256]{2,1,0:T(8,128)(2,1)}, bf16[1,3072,256]{2,1,0:T(8,128)(2,1)S(1)}, u32[]{:S(2)}, u32[]{:S(2)}) collective-permute-start(bf16[1,3072,256]{2,1,0:T(8,128)(2,1)} %collective-permute-done.8.refs_6_), channel_id=1, source_target_pairs={{0,1},{1,0},{2,3},{3,2},{4,5},{5,4},{6,7},{7,6}} | collective-permute-start | bytes 4718600 | tf_op jit(solution)/shard_map/ppermute | solution.py:518
  376.5 100.7 %collective-permute-start.11 = (bf16[1,3072,256]{2,1,0:T(8,128)(2,1)}, bf16[1,3072,256]{2,1,0:T(8,128)(2,1)S(1)}, u32[]{:S(2)}, u32[]{:S(2)}) collective-permute-start(bf16[1,3072,256]{2,1,0:T(8,128)(2,1)} %collective-permute-done.9.refs_7_), channel_id=1, source_target_pairs={{0,1},{1,0},{2,3},{3,2},{4,5},{5,4},{6,7},{7,6}} | collective-permute-start | bytes 4718600 | tf_op jit(solution)/shard_map/ppermute | solution.py:518
  477.2 1.1 copy-start.4
  477.3 1.6 copy-start.5
Sparse Core Ops, SparseCore 0:
  15.2 88.7 all-gather.15
  105.9 62.0 all-gather.13
  169.8 223.0 all-gather.7
  394.6 119.6 all-gather.9
  516.0 66.4 all-gather.11
